TPU v7x, 128 devices: a whole 4x4x4 slice. The times are simulated.
128 devices in a mesh: row: 8 (over y, z_lo), col: 16 (over x, z_hi, core).
Axes of the slice: x: 4, y: 4, z: 4 (z_hi: 2, z_lo: 2; z = z_hi * 2 + z_lo), core: 2. Of those that a mesh axis runs over, the one named last changes fastest.
Arguments:
- hidden_states: bfloat16 [16384, 8192], P(('row', 'col')), may hold values from -6 to 6
- w_c: bfloat16 [8192, 512], replicated, may hold values from -0.0625 to 0.0625
- w_b: bfloat16 [8192, 128], replicated, may hold values from -0.0625 to 0.0625
- teacher_q: bfloat16 [16384, 512], P(('row', 'col')), may hold values from -4 to 4
- teacher_k: bfloat16 [16384, 128], P(('row', 'col')), may hold values from -4 to 4
Outputs:
- grad_c: bfloat16 [16384, 512], P(('row', 'col'))
- grad_b: bfloat16 [16384, 128], P(('row', 'col'))
All inputs are finite; a program needn't handle non-finite values.
Results may differ from a plain program's by a relative error of at most 0.0056.
Values may be sent and summed in bfloat16 or wider, within the bound.
No kernel may reach another device: no remote copies, remote signals or barrier semaphores. Data moves between devices by JAX's collectives and lax.ppermute only.
A program may use at most 128 MiB of HBM per device.

v0:
```python
import functools
import math

import jax
import jax.numpy as jnp
from jax import lax
from jax.experimental import pallas as pl
from jax.experimental.pallas import tpu as pltpu
from jax.sharding import Mesh, PartitionSpec as P


HEADS = 4
HEAD = 128
TOK = 128
LOSS_GAIN = 16.0
LENGTH_BASE = 512.0
LOG2E = math.log2(math.e)

AXES = ("y", "zl", "x", "zh", "c")
SIZES = (4, 2, 4, 2, 2)
PLANE = ("zl", "x", "zh")
PLANE_N = 16
RING = 4
HALF = PLANE_N * TOK
BLOCK = 2 * HALF
ROWS = HEADS * TOK
TILE = 512
TILES = HALF // TILE
MASKED = -1e30
LOWEST = -1e29
TOO_LARGE = 2.0 ** 60
VMEM_LIMIT = 20 * 1024 * 1024


NT = (((1,), (1,)), ((), ()))
NN = (((1,), (0,)), ((), ()))
TN = (((0,), (0,)), ((), ()))


def mxu(a, b, dims):
    return lax.dot_general(a, b, dims, preferred_element_type=jnp.float32)


def stack_heads(dst, slot, src):
    for h in range(HEADS):
        dst[slot, h * TOK:(h + 1) * TOK, :] = src[:, h * HEAD:(h + 1) * HEAD]


def query_rows(first):
    lane = lax.broadcasted_iota(jnp.int32, (1, ROWS), 1)
    return first + (lane & (TOK - 1))


def temper(pos):
    scale = LOG2E / (math.log(LENGTH_BASE) * math.sqrt(HEAD))
    return jnp.log(pos.astype(jnp.float32) + 2.0) * scale


def visible(tile, core, query):
    row = lax.broadcasted_iota(jnp.int32, (TILE, 1), 0)
    group = tile * (TILE // TOK) + (row >> 7)
    key = (group * 2 + core) * TOK + (row & (TOK - 1))
    return key <= query


def rows_of(ref, tile, first):
    pieces = TILE // TOK
    return ref[pl.ds(tile * pieces, pieces), first:first + TOK].reshape(TILE, HEAD)


def place():
    group = (lax.axis_index("zl") * 4 + lax.axis_index("x")) * 2 + lax.axis_index("zh")
    core = lax.axis_index("c")
    return lax.axis_index("y"), group, core, (group * 2 + core) * TOK


def weights_kernel(km_ref, ko_ref, q0, q1, q2, q3, p_ref, peak_ref, out_ref, qs, sums):
    y, group, core, offset = place()
    for k, q in enumerate((q0, q1, q2, q3)):
        stack_heads(qs, k, q)
    for k in range(RING):
        out_ref[k, 0:1, :] = jnp.full((1, ROWS), LOWEST, jnp.float32)
        out_ref[k, 1:2, :] = jnp.zeros((1, ROWS), jnp.float32)
    local = query_rows(offset)

    def masks_of(tile):
        return visible(tile, core, local), visible(tile, 1 - core, local)

    def quick(k, tiles, own):
        scale = temper(query_rows((y + k) * BLOCK + offset))
        some = mxu(km_ref[0, :TOK], qs[k], NT) * scale
        if own:
            key = core * TOK + lax.broadcasted_iota(jnp.int32, (TOK, 1), 0)
            some = jnp.where(key <= local, some, MASKED)
        level = jnp.max(some, axis=0, keepdims=True)

        def inner(tile, total):
            row = pl.multiple_of(tile * TILE, TILE)
            for half, keys_ref in enumerate((km_ref, ko_ref)):
                weight = jnp.exp2(mxu(rows_of(keys_ref, tile, 0), qs[k], NT) * scale - level)
                if own:
                    weight = jnp.where(masks_of(tile)[half], weight, 0.0)
                p_ref[k, pl.ds(half * HALF + row, TILE), :] = weight.astype(jnp.bfloat16)
                total = total + jnp.sum(weight.reshape(TILE // 8, 8, ROWS), axis=0)
            return total

        total = lax.fori_loop(0, tiles, inner, jnp.zeros((8, ROWS), jnp.float32))
        total = jnp.sum(total, axis=0, keepdims=True)
        peak_ref[k] = jnp.broadcast_to(level, (2 * TILES, ROWS))
        out_ref[y + k, 0:1, :] = level
        out_ref[y + k, 1:2, :] = total
        return jnp.max(total) > TOO_LARGE

    def careful(k, tiles, own):
        scale = temper(query_rows((y + k) * BLOCK + offset))
        peak_ref[k] = jnp.full((2 * TILES, ROWS), LOWEST, jnp.float32)
        sums[...] = jnp.zeros((2 * TILES, ROWS), jnp.float32)

        def inner(tile, unused):
            row = pl.multiple_of(tile * TILE, TILE)
            for half, keys_ref in enumerate((km_ref, ko_ref)):
                logits = mxu(rows_of(keys_ref, tile, 0), qs[k], NT) * scale
                if own:
                    logits = jnp.where(masks_of(tile)[half], logits, MASKED)
                peak = jnp.maximum(jnp.max(logits, axis=0, keepdims=True), LOWEST)
                weight = jnp.exp2(logits - peak)
                p_ref[k, pl.ds(half * HALF + row, TILE), :] = weight.astype(jnp.bfloat16)
                peak_ref[k, pl.ds(half * TILES + tile, 1), :] = peak
                sums[pl.ds(half * TILES + tile, 1), :] = jnp.sum(weight, axis=0, keepdims=True)
            return unused

        lax.fori_loop(0, tiles, inner, 0)
        peak = peak_ref[k]
        best = jnp.max(peak, axis=0, keepdims=True)
        out_ref[y + k, 0:1, :] = best
        out_ref[y + k, 1:2, :] = jnp.sum(sums[...] * jnp.exp2(peak - best), axis=0, keepdims=True)

    own_tiles = group // (TILE // TOK) + 1
    pl.when(quick(0, own_tiles, True))(lambda: careful(0, own_tiles, True))

    def later(k, unused):
        pl.when(quick(k, TILES, False))(lambda: careful(k, TILES, False))
        return unused

    lax.fori_loop(1, RING - y, later, 0)


def narrow(value):
    return value.astype(jnp.bfloat16)


def student_kernel(bm_ref, bo_ref, c0, c1, c2, c3, ct, bt, acc, sums, state):
    y, group, core, offset = place()
    last = RING - y
    below = (group * TOK, (group + core) * TOK)
    row_of = lax.broadcasted_iota(jnp.int32, (TILE, 1), 0)
    lane_of = lax.broadcasted_iota(jnp.int32, (1, TILE), 1)
    for k, c in enumerate((c0, c1, c2, c3)):
        for h in range(HEADS):
            ct[k, :, h * TOK:(h + 1) * TOK] = c[:, h * HEAD:(h + 1) * HEAD].T

    def shrink(k):
        pos = query_rows((y + k) * BLOCK + offset).astype(jnp.float32)
        return 1.0 / (math.sqrt(HEAD) * (pos + 1.0))

    before = jnp.zeros((HEAD, HEAD), jnp.float32)
    whole = jnp.zeros((HEAD, HEAD), jnp.float32)
    for half, b_ref in enumerate((bm_ref, bo_ref)):
        for tile in range(TILES):
            bs = rows_of(b_ref, tile, TOK)
            turned = bs.T
            bt[half * TILES + tile] = turned
            part = jnp.where(row_of + tile * TILE < below[half], bs, jnp.zeros_like(bs))
            before += mxu(turned, part, NN)
            whole += mxu(turned, bs, NN)

    def apply(square, k):
        high = narrow(square)
        low = narrow(square - high.astype(jnp.float32))
        return (mxu(high, ct[k], NN) + mxu(low, ct[k], NN)) * shrink(k)

    state[...] = jnp.zeros((HEAD, HEAD), jnp.float32)

    def later(k, unused):
        acc[k] = apply(whole, k)
        state[...] += mxu(ct[k], narrow(ct[k].astype(jnp.float32) * shrink(k)), NT)
        return unused

    lax.fori_loop(1, last, later, 0)
    own = mxu(ct[0], narrow(ct[0].astype(jnp.float32) * shrink(0)), NT)
    both = narrow(jnp.concatenate([state[...], own], axis=1))
    for half in range(2):
        for tile in range(TILES):
            turned = bt[half * TILES + tile]
            part = jnp.where(lane_of + tile * TILE < below[half], turned, jnp.zeros_like(turned))
            value = mxu(both, jnp.concatenate([turned, part], axis=0), NN)
            for piece in range(TILE // TOK):
                sums[half, tile * (TILE // TOK) + piece] = value[:, piece * TOK:(piece + 1) * TOK]

    bs = bm_ref[group, TOK:]
    error = mxu(bs, ct[0], NN) * shrink(0)
    inside = lax.broadcasted_iota(jnp.int32, (TOK, 1), 0) <= query_rows(0)
    error = narrow(jnp.where(inside, error, 0.0))
    sums[0, group] += mxu(ct[0], error, NT)
    acc[0] = apply(before, 0) + mxu(bs, error, TN)


def sums_kernel(p_ref, peak_ref, t0, t1, t2, t3, ct, bt, acc_in, sums_in,
                o0, o1, o2, o3, gm_ref, go_ref, acc, sums):
    y, group, _, _ = place()
    factor = LOSS_GAIN / math.sqrt(HEAD)
    last = RING - y
    stats = (t0, t1, t2, t3)
    pieces = TILE // TOK
    sums[...] = jnp.zeros(sums.shape, jnp.float32)

    def chunk(k, unused):
        best = functools.reduce(jnp.maximum, [t[y + k, 0:1, :] for t in stats])
        total = sum(t[y + k, 1:2, :] * jnp.exp2(t[y + k, 0:1, :] - best) for t in stats)
        lse = best + jnp.log(total) * LOG2E
        acc[k] = acc_in[k]

        def inner(tile, unused):
            row = pl.multiple_of(tile * TILE, TILE)
            for half in range(2):
                weights = p_ref[k, pl.ds(half * HALF + row, TILE), :]
                fit = jnp.exp2(peak_ref[k, pl.ds(half * TILES + tile, 1), :] - lse)
                acc[k] -= mxu(bt[half * TILES + tile], weights, NN) * fit
                crow = narrow(ct[k].astype(jnp.float32) * fit)
                sums[half * TILES + tile] += mxu(crow, weights, NT)
            return unused

        tiles = jnp.where(k == 0, group // pieces + 1, TILES)
        lax.fori_loop(0, tiles, inner, 0)
        return unused

    lax.fori_loop(0, last, chunk, 0)

    for k, o in enumerate((o0, o1, o2, o3)):
        @pl.when(k < last)
        def _():
            for h in range(HEADS):
                piece = acc[k, :, h * TOK:(h + 1) * TOK].T * factor
                o[:, h * HEAD:(h + 1) * HEAD] = piece.astype(o.dtype)

        @pl.when(k >= last)
        def _():
            o[...] = jnp.zeros(o.shape, o.dtype)
    for half, g in enumerate((gm_ref, go_ref)):
        for i in range(PLANE_N):
            part = sums[half * TILES + i // pieces, :, (i % pieces) * TOK:(i % pieces + 1) * TOK]
            g[i] = ((sums_in[half, i] - part) * factor).astype(g.dtype)


def finish_kernel(g_ref, out_ref):
    out_ref[...] = narrow(jnp.sum(g_ref[...].astype(jnp.float32), axis=0).T)


def down(value, k):
    return lax.ppermute(value, "y", [(s, s - k) for s in range(k, RING)])


def up(value, k):
    return lax.ppermute(value, "y", [(s, s + k) for s in range(RING - k)])


def around(value, k):
    return lax.ppermute(value, "y", [(s, (s + k) % RING) for s in range(RING)])


def swap(value):
    return lax.ppermute(value, "c", [(0, 1), (1, 0)])


def exchange(value):
    return lax.all_to_all(value, PLANE, 0, 0, tiled=True)


def on_device(hidden_states, w_c, w_b, teacher_q, teacher_k):
    b_proj = narrow(jnp.dot(hidden_states, w_b, preferred_element_type=jnp.float32))
    mine = exchange(jnp.tile(jnp.concatenate([teacher_k, b_proj], axis=0)[None], (PLANE_N, 1, 1)))
    queries = [teacher_q] + [down(teacher_q, k) for k in (1, 2, 3)]
    c_proj = narrow(jnp.dot(hidden_states, w_c, preferred_element_type=jnp.float32))
    crows = [c_proj] + [down(c_proj, k) for k in (1, 2, 3)]
    other = swap(mine)

    def call(kernel, ins, outs, scratch):
        vmem = pl.BlockSpec(memory_space=pltpu.VMEM)
        return pl.pallas_call(
            kernel,
            out_shape=outs,
            in_specs=[vmem] * len(ins),
            out_specs=jax.tree.map(lambda unused: vmem, outs),
            scratch_shapes=[pltpu.VMEM(*s) for s in scratch],
            compiler_params=pltpu.CompilerParams(vmem_limit_bytes=VMEM_LIMIT),
        )(*ins)

    full, half = jnp.float32, jnp.bfloat16
    shaped = jax.ShapeDtypeStruct
    weights, peaks, stats = call(
        weights_kernel, (mine, other, *queries),
        (shaped((RING, BLOCK, ROWS), half), shaped((RING, 2 * TILES, ROWS), full), shaped((RING, 2, ROWS), full)),
        [((RING, ROWS, HEAD), half), ((2 * TILES, ROWS), full)],
    )
    all_stats = [stats] + [around(stats, k) for k in (1, 2, 3)]
    turned = call(
        student_kernel, (mine, other, *crows),
        (shaped((RING, HEAD, ROWS), half), shaped((2 * TILES, HEAD, TILE), half),
         shaped((RING, HEAD, ROWS), full), shaped((2, PLANE_N, HEAD, TOK), full)),
        [((HEAD, HEAD), full)],
    )
    part = shaped((TOK, ROWS), half)
    o0, o1, o2, o3, g_mine, g_other = call(
        sums_kernel, (weights, peaks, *all_stats, *turned),
        (shaped((TOK, ROWS), full), part, part, part,
         shaped((PLANE_N, HEAD, TOK), full), shaped((PLANE_N, HEAD, TOK), half)),
        [((RING, HEAD, ROWS), full), ((2 * TILES, HEAD, TILE), full)],
    )
    g_parts = exchange(narrow(g_mine + swap(g_other).astype(full)))
    rows = o0
    for k, o in ((1, o1), (2, o2), (3, o3)):
        rows = rows + up(o, k).astype(full)
    grad_b = call(finish_kernel, (g_parts,), shaped((TOK, HEAD), half), [])
    return narrow(rows), grad_b


def solution(mesh):
    inner = Mesh(mesh.devices.reshape(SIZES), AXES)
    tokens = P(AXES, None)

    return jax.shard_map(
        on_device,
        mesh=inner,
        in_specs=(tokens, P(), P(), tokens, tokens),
        out_specs=(tokens, tokens),
        check_vma=False,
    )
```

profile of v0, /device:TPU:0, one launch (start us, length us, event | category | flops | bytes accessed | tf_op | source)
XLA Modules:
  0.0 94.6 jit_solution(1156275734932821531)
XLA Ops:
  0.6 0.0 copy-start
  0.6 0.0 copy-start.2
  0.7 1.6 %copy-done = bf16[128,8192]{1,0:T(8,128)(2,1)S(1)} copy-done((bf16[128,8192]{1,0:T(8,128)(2,1)S(1)}, bf16[128,8192]{1,0:T(8,128)(2,1)}, u32[]{:S(2)}) %copy-start) | copy-done | bytes 2097176
  2.2 2.3 %convolution_convert_fusion.1 = bf16[128,128]{1,0:T(8,128)(2,1)S(1)} fusion(bf16[128,8192]{1,0:T(8,128)(2,1)S(1)} %copy-done, bf16[8192,128]{1,0:T(8,128)(2,1)} %param.7), kind=kOutput, calls=%fused_computation.1 | convolution fusion | flops 268451840 | bytes 4227072 | tf_op jit(solution)/shard_map/dot_general | solution.py:280
  4.5 0.0 copy-done.2
  4.5 0.0 copy-start.1
  4.6 0.2 tile.2
  4.8 24.8 %all_to_all.10.km_ref.bm_ref = bf16[16,256,128]{2,1,0:T(8,128)(2,1)S(1)} all-to-all(bf16[16,256,128]{2,1,0:T(8,128)(2,1)S(1)} %tile.2), channel_id=1, replica_groups=mesh['y'=4,'zl'=2,'x'=4,'zh'=2,'c'=2] {'zl','x','zh'}, dimensions={0} | all-to-all | bytes 2097152 | tf_op jit(solution)/shard_map/all_to_all | solution.py:276
  29.6 0.0 collective-permute-start
  29.6 0.0 copy-done.1
  29.6 1.3 %collective-permute-start.2 = (bf16[128,512]{1,0:T(8,128)(2,1)S(1)}, bf16[128,512]{1,0:T(8,128)(2,1)S(1)}, u32[]{:S(2)}, u32[]{:S(2)}) collective-permute-start(bf16[128,512]{1,0:T(8,128)(2,1)S(1)} %copy-done.1), channel_id=1, source_target_pairs={{64,0},{96,32},{65,1},{97,33},{66,2},{98,34},{67,3},{99,35},{68,4}... | collective-permute-start | bytes 393224 | tf_op jit(solution)/shard_map/ppermute | solution.py:260
  30.9 1.3 %collective-permute-start.1 = (bf16[128,512]{1,0:T(8,128)(2,1)S(1)}, bf16[128,512]{1,0:T(8,128)(2,1)S(1)}, u32[]{:S(2)}, u32[]{:S(2)}) collective-permute-start(bf16[128,512]{1,0:T(8,128)(2,1)S(1)} %copy-done.1), channel_id=1, source_target_pairs={{32,0},{64,32},{96,64},{33,1},{65,33},{97,65},{34,2},{66,34},{98,6... | collective-permute-start | bytes 393224 | tf_op jit(solution)/shard_map/ppermute | solution.py:260
  32.2 1.3 %collective-permute-start.3 = (bf16[128,512]{1,0:T(8,128)(2,1)S(1)}, bf16[128,512]{1,0:T(8,128)(2,1)S(1)}, u32[]{:S(2)}, u32[]{:S(2)}) collective-permute-start(bf16[128,512]{1,0:T(8,128)(2,1)S(1)} %copy-done.1), channel_id=1, source_target_pairs={{96,0},{97,1},{98,2},{99,3},{100,4},{101,5},{102,6},{103,7},{104,8... | collective-permute-start | bytes 393224 | tf_op jit(solution)/shard_map/ppermute | solution.py:260
  33.5 4.6 %convolution_convert_fusion.c0 = bf16[128,512]{1,0:T(8,128)(2,1)S(1)} fusion(bf16[128,8192]{1,0:T(8,128)(2,1)S(1)} %copy-done, bf16[8192,512]{1,0:T(8,128)(2,1)} %param.6), kind=kOutput, calls=%fused_computation | convolution fusion | flops 1073807360 | bytes 10616832 | tf_op jit(solution)/shard_map/dot_general | solution.py:283
  38.1 1.3 %collective-permute-start.9 = (bf16[128,512]{1,0:T(8,128)(2,1)S(1)}, bf16[128,512]{1,0:T(8,128)(2,1)S(1)}, u32[]{:S(2)}, u32[]{:S(2)}) collective-permute-start(bf16[128,512]{1,0:T(8,128)(2,1)S(1)} %convolution_convert_fusion.c0), channel_id=1, source_target_pairs={{96,0},{97,1},{98,2},{99,3},{100,4},{101,5},{102,6},{103,7},{104,8... | collective-permute-start | bytes 393224 | tf_op jit(solution)/shard_map/ppermute | solution.py:260
  39.4 0.0 collective-permute-done.2.q2
  39.4 1.3 %collective-permute-start.8 = (bf16[128,512]{1,0:T(8,128)(2,1)S(1)}, bf16[128,512]{1,0:T(8,128)(2,1)S(1)}, u32[]{:S(2)}, u32[]{:S(2)}) collective-permute-start(bf16[128,512]{1,0:T(8,128)(2,1)S(1)} %convolution_convert_fusion.c0), channel_id=1, source_target_pairs={{64,0},{96,32},{65,1},{97,33},{66,2},{98,34},{67,3},{99,35},{68,4}... | collective-permute-start | bytes 393224 | tf_op jit(solution)/shard_map/ppermute | solution.py:260
  40.7 0.0 collective-permute-done.1.q1
  40.8 1.3 %collective-permute-start.7 = (bf16[128,512]{1,0:T(8,128)(2,1)S(1)}, bf16[128,512]{1,0:T(8,128)(2,1)S(1)}, u32[]{:S(2)}, u32[]{:S(2)}) collective-permute-start(bf16[128,512]{1,0:T(8,128)(2,1)S(1)} %convolution_convert_fusion.c0), channel_id=1, source_target_pairs={{32,0},{64,32},{96,64},{33,1},{65,33},{97,65},{34,2},{66,34},{98,6... | collective-permute-start | bytes 393224 | tf_op jit(solution)/shard_map/ppermute | solution.py:260
  42.1 0.3 collective-permute-done.3.q3
  42.4 0.0 collective-permute-done.ko_ref.bo_ref
  42.4 7.9 %shard_map.68 = (bf16[4,4096,512]{2,1,0:T(8,128)(2,1)S(1)}, f32[4,8,512]{2,1,0:T(8,128)S(1)}, f32[4,2,512]{2,1,0:T(2,128)S(1)}) custom-call(bf16[16,256,128]{2,1,0:T(8,128)(2,1)S(1)} %all_to_all.10.km_ref.bm_ref, bf16[16,256,128]{2,1,0:T(8,128)(2,1)S(1)} %collective-permute-done.ko_ref.bo_ref, bf16[128,512]{1,0:T(8,128)(2,1)S(1)} %copy-done.1, ...), custom_call_target="tpu_custom_call" | custom-call | tf_op jit(solution)/shard_map/pallas_call | solution.py:289
  50.3 0.1 collective-permute-start.6
  50.4 2.6 %collective-permute-start.5 = (f32[4,2,512]{2,1,0:T(2,128)S(1)}, f32[4,2,512]{2,1,0:T(2,128)S(1)}, u32[]{:S(2)}, u32[]{:S(2)}) collective-permute-start(f32[4,2,512]{2,1,0:T(2,128)S(1)} %get-tuple-element.17.t0), channel_id=1, source_target_pairs={{0,64},{32,96},{64,0},{96,32},{1,65},{33,97},{65,1},{97,33},{2,66}... | collective-permute-start | bytes 49160 | tf_op jit(solution)/shard_map/ppermute | solution.py:268
  53.0 0.0 collective-permute-done.9.c3
  53.0 0.0 collective-permute-start.4
  53.0 0.0 collective-permute-done.8.c2
  53.0 0.0 collective-permute-done.7.c1
  53.0 2.6 %shard_map.69 = (bf16[4,128,512]{2,1,0:T(8,128)(2,1)S(1)}, bf16[8,128,512]{2,1,0:T(8,128)(2,1)S(1)}, f32[4,128,512]{2,1,0:T(8,128)S(1)}, f32[2,16,128,128]{3,2,1,0:T(8,128)S(1)}) custom-call(bf16[16,256,128]{2,1,0:T(8,128)(2,1)S(1)} %all_to_all.10.km_ref.bm_ref, bf16[16,256,128]{2,1,0:T(8,128)(2,1)S(1)} %collective-permute-done.ko_ref.bo_ref, ...), custom_call_target="tpu_custom_call" | custom-call | tf_op jit(solution)/shard_map/pallas_call | solution.py:289
  55.6 0.0 collective-permute-done.6.t3
  55.6 0.1 collective-permute-done.5.t2
  55.7 2.2 %collective-permute-done.4.t1 = f32[4,2,512]{2,1,0:T(2,128)S(1)} collective-permute-done((f32[4,2,512]{2,1,0:T(2,128)S(1)}, f32[4,2,512]{2,1,0:T(2,128)S(1)}, u32[]{:S(2)}, u32[]{:S(2)}) %collective-permute-start.4) | collective-permute-done | bytes 16416 | tf_op jit(solution)/shard_map/ppermute | solution.py:268
  57.9 9.7 %shard_map.70 = (f32[128,512]{1,0:T(8,128)S(1)}, bf16[128,512]{1,0:T(8,128)(2,1)S(1)}, bf16[128,512]{1,0:T(8,128)(2,1)S(1)}, bf16[128,512]{1,0:T(8,128)(2,1)S(1)...) custom-call(bf16[4,4096,512]{2,1,0:T(8,128)(2,1)S(1)} %get-tuple-element.15.p_ref, ...), custom_call_target="tpu_custom_call" | custom-call | tf_op jit(solution)/shard_map/pallas_call | solution.py:289
  67.6 0.1 collective-permute-start.13
  67.7 1.9 %collective-permute-done.13 = bf16[16,128,128]{2,1,0:T(8,128)(2,1)S(1)} collective-permute-done((bf16[16,128,128]{2,1,0:T(8,128)(2,1)S(1)}, bf16[16,128,128]{2,1,0:T(8,128)(2,1)S(1)}, u32[]{:S(2)}, u32[]{:S(2)}) %collective-permute-start.13) | collective-permute-done | bytes 524320 | tf_op jit(solution)/shard_map/ppermute | solution.py:272
  69.6 0.9 add_convert_fusion
  70.5 11.3 %all-to-all-start.1 = ((bf16[16,128,128]{2,1,0:T(8,128)(2,1)}), bf16[16,128,128]{2,1,0:T(8,128)(2,1)S(1)}, u32[]{:S(2)}, u32[]{:S(2)}) async-start(bf16[16,128,128]{2,1,0:T(8,128)(2,1)} %add_convert_fusion), calls=%async_computation.1 | async-start | bytes 1048576 | tf_op jit(solution)/shard_map/all_to_all | solution.py:276
  81.8 1.3 %collective-permute-start.10 = (bf16[128,512]{1,0:T(8,128)(2,1)S(1)}, bf16[128,512]{1,0:T(8,128)(2,1)S(1)}, u32[]{:S(2)}, u32[]{:S(2)}) collective-permute-start(bf16[128,512]{1,0:T(8,128)(2,1)S(1)} %get-tuple-element.23), channel_id=1, source_target_pairs={{0,32},{32,64},{64,96},{1,33},{33,65},{65,97},{2,34},{34,66},{66,9... | collective-permute-start | bytes 393224 | tf_op jit(solution)/shard_map/ppermute | solution.py:264
  83.1 1.3 %collective-permute-start.11 = (bf16[128,512]{1,0:T(8,128)(2,1)S(1)}, bf16[128,512]{1,0:T(8,128)(2,1)S(1)}, u32[]{:S(2)}, u32[]{:S(2)}) collective-permute-start(bf16[128,512]{1,0:T(8,128)(2,1)S(1)} %get-tuple-element.24), channel_id=1, source_target_pairs={{0,64},{32,96},{1,65},{33,97},{2,66},{34,98},{3,67},{35,99},{4,68}... | collective-permute-start | bytes 393224 | tf_op jit(solution)/shard_map/ppermute | solution.py:264
  84.4 1.3 %collective-permute-start.12 = (bf16[128,512]{1,0:T(8,128)(2,1)S(1)}, bf16[128,512]{1,0:T(8,128)(2,1)S(1)}, u32[]{:S(2)}, u32[]{:S(2)}) collective-permute-start(bf16[128,512]{1,0:T(8,128)(2,1)S(1)} %get-tuple-element.25), channel_id=1, source_target_pairs={{0,96},{1,97},{2,98},{3,99},{4,100},{5,101},{6,102},{7,103},{8,104... | collective-permute-start | bytes 393224 | tf_op jit(solution)/shard_map/ppermute | solution.py:264
  85.7 1.3 %collective-permute-done.10 = bf16[128,512]{1,0:T(8,128)(2,1)S(1)} collective-permute-done((bf16[128,512]{1,0:T(8,128)(2,1)S(1)}, bf16[128,512]{1,0:T(8,128)(2,1)S(1)}, u32[]{:S(2)}, u32[]{:S(2)}) %collective-permute-start.10) | collective-permute-done | bytes 131104 | tf_op jit(solution)/shard_map/ppermute | solution.py:264
  87.0 2.2 %collective-permute-done.11 = bf16[128,512]{1,0:T(8,128)(2,1)S(1)} collective-permute-done((bf16[128,512]{1,0:T(8,128)(2,1)S(1)}, bf16[128,512]{1,0:T(8,128)(2,1)S(1)}, u32[]{:S(2)}, u32[]{:S(2)}) %collective-permute-start.11) | collective-permute-done | bytes 131104 | tf_op jit(solution)/shard_map/ppermute | solution.py:264
  89.2 0.0 collective-permute-done.12
  89.2 0.7 add_convert_fusion.1
  89.9 4.0 %all-to-all-done.1.g_ref = bf16[16,128,128]{2,1,0:T(8,128)(2,1)S(1)} async-done(((bf16[16,128,128]{2,1,0:T(8,128)(2,1)}), bf16[16,128,128]{2,1,0:T(8,128)(2,1)S(1)}, u32[]{:S(2)}, u32[]{:S(2)}) %all-to-all-start.1) | async-done | bytes 524320 | tf_op jit(solution)/shard_map/all_to_all | solution.py:276
  93.9 0.8 shard_map.71
  (1 shorter events, 0.0 us)
Async XLA Ops:
  0.6 1.6 %copy-start = (bf16[128,8192]{1,0:T(8,128)(2,1)S(1)}, bf16[128,8192]{1,0:T(8,128)(2,1)}, u32[]{:S(2)}) copy-start(bf16[128,8192]{1,0:T(8,128)(2,1)} %param.5) | copy-start | bytes 6291460
  0.6 3.9 %copy-start.2 = (bf16[128,128]{1,0:T(8,128)(2,1)S(1)}, bf16[128,128]{1,0:T(8,128)(2,1)}, u32[]{:S(2)}) copy-start(bf16[128,128]{1,0:T(8,128)(2,1)} %param.9) | copy-start | bytes 98308
  4.5 25.1 %copy-start.1 = (bf16[128,512]{1,0:T(8,128)(2,1)S(1)}, bf16[128,512]{1,0:T(8,128)(2,1)}, u32[]{:S(2)}) copy-start(bf16[128,512]{1,0:T(8,128)(2,1)} %q0.1) | copy-start | bytes 393220
  29.6 12.8 %collective-permute-start = (bf16[16,256,128]{2,1,0:T(8,128)(2,1)S(1)}, bf16[16,256,128]{2,1,0:T(8,128)(2,1)S(1)}, u32[]{:S(2)}, u32[]{:S(2)}) collective-permute-start(bf16[16,256,128]{2,1,0:T(8,128)(2,1)S(1)} %all_to_all.10.km_ref.bm_ref), channel_id=1, source_target_pairs={{0,1},{1,0},{2,3},{3,2},{4,5},{5,4},{6,7},{7,6},{8,9},{9,8},{10,11... | collective-permute-start | bytes 3145736 | tf_op jit(solution)/shard_map/ppermute | solution.py:272
  29.6 9.8 %collective-permute-start.2 = (bf16[128,512]{1,0:T(8,128)(2,1)S(1)}, bf16[128,512]{1,0:T(8,128)(2,1)S(1)}, u32[]{:S(2)}, u32[]{:S(2)}) collective-permute-start(bf16[128,512]{1,0:T(8,128)(2,1)S(1)} %copy-done.1), channel_id=1, source_target_pairs={{64,0},{96,32},{65,1},{97,33},{66,2},{98,34},{67,3},{99,35},{68,4}... | collective-permute-start | bytes 393224 | tf_op jit(solution)/shard_map/ppermute | solution.py:260
  30.9 9.9 %collective-permute-start.1 = (bf16[128,512]{1,0:T(8,128)(2,1)S(1)}, bf16[128,512]{1,0:T(8,128)(2,1)S(1)}, u32[]{:S(2)}, u32[]{:S(2)}) collective-permute-start(bf16[128,512]{1,0:T(8,128)(2,1)S(1)} %copy-done.1), channel_id=1, source_target_pairs={{32,0},{64,32},{96,64},{33,1},{65,33},{97,65},{34,2},{66,34},{98,6... | collective-permute-start | bytes 393224 | tf_op jit(solution)/shard_map/ppermute | solution.py:260
  32.2 10.2 %collective-permute-start.3 = (bf16[128,512]{1,0:T(8,128)(2,1)S(1)}, bf16[128,512]{1,0:T(8,128)(2,1)S(1)}, u32[]{:S(2)}, u32[]{:S(2)}) collective-permute-start(bf16[128,512]{1,0:T(8,128)(2,1)S(1)} %copy-done.1), channel_id=1, source_target_pairs={{96,0},{97,1},{98,2},{99,3},{100,4},{101,5},{102,6},{103,7},{104,8... | collective-permute-start | bytes 393224 | tf_op jit(solution)/shard_map/ppermute | solution.py:260
  38.1 14.8 %collective-permute-start.9 = (bf16[128,512]{1,0:T(8,128)(2,1)S(1)}, bf16[128,512]{1,0:T(8,128)(2,1)S(1)}, u32[]{:S(2)}, u32[]{:S(2)}) collective-permute-start(bf16[128,512]{1,0:T(8,128)(2,1)S(1)} %convolution_convert_fusion.c0), channel_id=1, source_target_pairs={{96,0},{97,1},{98,2},{99,3},{100,4},{101,5},{102,6},{103,7},{104,8... | collective-permute-start | bytes 393224 | tf_op jit(solution)/shard_map/ppermute | solution.py:260
  39.4 13.5 %collective-permute-start.8 = (bf16[128,512]{1,0:T(8,128)(2,1)S(1)}, bf16[128,512]{1,0:T(8,128)(2,1)S(1)}, u32[]{:S(2)}, u32[]{:S(2)}) collective-permute-start(bf16[128,512]{1,0:T(8,128)(2,1)S(1)} %convolution_convert_fusion.c0), channel_id=1, source_target_pairs={{64,0},{96,32},{65,1},{97,33},{66,2},{98,34},{67,3},{99,35},{68,4}... | collective-permute-start | bytes 393224 | tf_op jit(solution)/shard_map/ppermute | solution.py:260
  40.8 12.2 %collective-permute-start.7 = (bf16[128,512]{1,0:T(8,128)(2,1)S(1)}, bf16[128,512]{1,0:T(8,128)(2,1)S(1)}, u32[]{:S(2)}, u32[]{:S(2)}) collective-permute-start(bf16[128,512]{1,0:T(8,128)(2,1)S(1)} %convolution_convert_fusion.c0), channel_id=1, source_target_pairs={{32,0},{64,32},{96,64},{33,1},{65,33},{97,65},{34,2},{66,34},{98,6... | collective-permute-start | bytes 393224 | tf_op jit(solution)/shard_map/ppermute | solution.py:260
  50.3 5.3 %collective-permute-start.6 = (f32[4,2,512]{2,1,0:T(2,128)S(1)}, f32[4,2,512]{2,1,0:T(2,128)S(1)}, u32[]{:S(2)}, u32[]{:S(2)}) collective-permute-start(f32[4,2,512]{2,1,0:T(2,128)S(1)} %get-tuple-element.17.t0), channel_id=1, source_target_pairs={{0,96},{32,0},{64,32},{96,64},{1,97},{33,1},{65,33},{97,65},{2,98}... | collective-permute-start | bytes 49160 | tf_op jit(solution)/shard_map/ppermute | solution.py:268
  50.4 5.3 %collective-permute-start.5 = (f32[4,2,512]{2,1,0:T(2,128)S(1)}, f32[4,2,512]{2,1,0:T(2,128)S(1)}, u32[]{:S(2)}, u32[]{:S(2)}) collective-permute-start(f32[4,2,512]{2,1,0:T(2,128)S(1)} %get-tuple-element.17.t0), channel_id=1, source_target_pairs={{0,64},{32,96},{64,0},{96,32},{1,65},{33,97},{65,1},{97,33},{2,66}... | collective-permute-start | bytes 49160 | tf_op jit(solution)/shard_map/ppermute | solution.py:268
  53.0 5.0 %collective-permute-start.4 = (f32[4,2,512]{2,1,0:T(2,128)S(1)}, f32[4,2,512]{2,1,0:T(2,128)S(1)}, u32[]{:S(2)}, u32[]{:S(2)}) collective-permute-start(f32[4,2,512]{2,1,0:T(2,128)S(1)} %get-tuple-element.17.t0), channel_id=1, source_target_pairs={{0,32},{32,64},{64,96},{96,0},{1,33},{33,65},{65,97},{97,1},{2,34}... | collective-permute-start | bytes 49160 | tf_op jit(solution)/shard_map/ppermute | solution.py:268
  67.6 2.0 %collective-permute-start.13 = (bf16[16,128,128]{2,1,0:T(8,128)(2,1)S(1)}, bf16[16,128,128]{2,1,0:T(8,128)(2,1)S(1)}, u32[]{:S(2)}, u32[]{:S(2)}) collective-permute-start(bf16[16,128,128]{2,1,0:T(8,128)(2,1)S(1)} %get-tuple-element.27), channel_id=1, source_target_pairs={{0,1},{1,0},{2,3},{3,2},{4,5},{5,4},{6,7},{7,6},{8,9},{9,8},{10,11... | collective-permute-start | bytes 1572872 | tf_op jit(solution)/shard_map/ppermute | solution.py:272
  70.5 23.3 %all-to-all-start.1 = ((bf16[16,128,128]{2,1,0:T(8,128)(2,1)}), bf16[16,128,128]{2,1,0:T(8,128)(2,1)S(1)}, u32[]{:S(2)}, u32[]{:S(2)}) async-start(bf16[16,128,128]{2,1,0:T(8,128)(2,1)} %add_convert_fusion), calls=%async_computation.1 | async-start | bytes 1048576 | tf_op jit(solution)/shard_map/all_to_all | solution.py:276
  81.8 5.2 %collective-permute-start.10 = (bf16[128,512]{1,0:T(8,128)(2,1)S(1)}, bf16[128,512]{1,0:T(8,128)(2,1)S(1)}, u32[]{:S(2)}, u32[]{:S(2)}) collective-permute-start(bf16[128,512]{1,0:T(8,128)(2,1)S(1)} %get-tuple-element.23), channel_id=1, source_target_pairs={{0,32},{32,64},{64,96},{1,33},{33,65},{65,97},{2,34},{34,66},{66,9... | collective-permute-start | bytes 393224 | tf_op jit(solution)/shard_map/ppermute | solution.py:264
  83.1 6.1 %collective-permute-start.11 = (bf16[128,512]{1,0:T(8,128)(2,1)S(1)}, bf16[128,512]{1,0:T(8,128)(2,1)S(1)}, u32[]{:S(2)}, u32[]{:S(2)}) collective-permute-start(bf16[128,512]{1,0:T(8,128)(2,1)S(1)} %get-tuple-element.24), channel_id=1, source_target_pairs={{0,64},{32,96},{1,65},{33,97},{2,66},{34,98},{3,67},{35,99},{4,68}... | collective-permute-start | bytes 393224 | tf_op jit(solution)/shard_map/ppermute | solution.py:264
  84.4 4.8 %collective-permute-start.12 = (bf16[128,512]{1,0:T(8,128)(2,1)S(1)}, bf16[128,512]{1,0:T(8,128)(2,1)S(1)}, u32[]{:S(2)}, u32[]{:S(2)}) collective-permute-start(bf16[128,512]{1,0:T(8,128)(2,1)S(1)} %get-tuple-element.25), channel_id=1, source_target_pairs={{0,96},{1,97},{2,98},{3,99},{4,100},{5,101},{6,102},{7,103},{8,104... | collective-permute-start | bytes 393224 | tf_op jit(solution)/shard_map/ppermute | solution.py:264
where the time goes:
time: 95.1 us; the launch traced here: 94.6 us
  starting transfers between devices  25.7 us (27%)
  blocking collectives  24.8 us (26%)
  Pallas kernels  20.9 us (22%)
  waiting for transfers between devices  12 us (13%)
  matrix products  6.92 us (7%)
  local copies, waits for them, and re-layouts  1.79 us (2%)
  other arithmetic  1.67 us (2%)
    all_to_all x1, blocking collectives, exchange(): return lax.all_to_all(value, PLANE, 0, 0, tiled=True)  24.8 us
    pallas_call x4, Pallas kernels, call(): pl.pallas_call(kernel, out_shape=outs, in_specs=[vmem] * len(ins), out_sp...  20.9 us
    all_to_all x1, starting transfers between devices, exchange(): return lax.all_to_all(value, PLANE, 0, 0, tiled=True)  11.3 us
    ppermute x6, starting transfers between devices, down(): return lax.ppermute(value, 'y', [(s, s - k) for s in range(k, RING)])  7.74 us
    dot_general x1, matrix products, on_device(): jnp.dot(hidden_states, w_c, preferred_element_type=jnp.float32)  4.64 us
    all_to_all x1, waiting for transfers between devices, exchange(): return lax.all_to_all(value, PLANE, 0, 0, tiled=True)  3.96 us
    ppermute x3, starting transfers between devices, up(): return lax.ppermute(value, 'y', [(s, s + k) for s in range(RING - k)])  3.89 us
    ppermute x3, waiting for transfers between devices, up(): return lax.ppermute(value, 'y', [(s, s + k) for s in range(RING - k)])  3.47 us
  transfers between devices with their start and end apart: 15, of which 7 were waited for; matrix products, arithmetic and copies ran while one was open for 6% of the time, Pallas kernels for 11%

commit v1 on v0

v1 whole, which is shorter than its diff:
```python
import functools
import math

import jax
import jax.numpy as jnp
from jax import lax
from jax.experimental import pallas as pl
from jax.experimental.pallas import tpu as pltpu
from jax.sharding import Mesh, PartitionSpec as P


HEADS = 4
HEAD = 128
TOK = 128
LOSS_GAIN = 16.0
LENGTH_BASE = 512.0
LOG2E = math.log2(math.e)

AXES = ("y", "zl", "x", "zh", "c")
SIZES = (4, 2, 4, 2, 2)
PLANE = ("zl", "x", "zh")
PLANE_N = 16
RING = 4
HALF = PLANE_N * TOK
BLOCK = 2 * HALF
ROWS = HEADS * TOK
TILE = 512
TILES = HALF // TILE
PIECES = TILE // TOK
DEPTH = 8
MASKED = -1e30
LOWEST = -1e29
TOO_LARGE = 2.0 ** 60
VMEM_LIMIT = 20 * 1024 * 1024


NT = (((1,), (1,)), ((), ()))
NN = (((1,), (0,)), ((), ()))
TN = (((0,), (0,)), ((), ()))


def mxu(a, b, dims):
    return lax.dot_general(a, b, dims, preferred_element_type=jnp.float32)


def stack_heads(dst, slot, src):
    for h in range(HEADS):
        dst[slot, h * TOK:(h + 1) * TOK, :] = src[:, h * HEAD:(h + 1) * HEAD]


def query_rows(first):
    lane = lax.broadcasted_iota(jnp.int32, (1, ROWS), 1)
    return first + (lane & (TOK - 1))


def temper(pos):
    scale = LOG2E / (math.log(LENGTH_BASE) * math.sqrt(HEAD))
    return jnp.log(pos.astype(jnp.float32) + 2.0) * scale


def visible(tile, core, query):
    row = lax.broadcasted_iota(jnp.int32, (TILE, 1), 0)
    group = tile * PIECES + (row >> 7)
    key = (group * 2 + core) * TOK + (row & (TOK - 1))
    return key <= query


def place():
    group = (lax.axis_index("zl") * 4 + lax.axis_index("x")) * 2 + lax.axis_index("zh")
    core = lax.axis_index("c")
    return lax.axis_index("y"), group, core, (group * 2 + core) * TOK


def fetch(pairs, sems):
    copies = []
    for j, (source, target, split) in enumerate(pairs):
        size = source.shape[split] // DEPTH
        for i in range(DEPTH):
            cut = (slice(None),) * split + (pl.ds(i * size, size),)
            copies.append(pltpu.make_async_copy(source.at[cut], target.at[cut], sems.at[j * DEPTH + i]))
    for i in range(DEPTH):
        for copy in copies[i::DEPTH]:
            copy.start()
    return copies


def project(hidden, weights, copies):
    size = hidden.shape[1] // DEPTH
    total = None
    for i in range(DEPTH):
        for copy in copies[i::DEPTH]:
            copy.wait()
        part = mxu(hidden[:, i * size:(i + 1) * size], weights[i * size:(i + 1) * size, :], NN)
        total = part if total is None else total + part
    return narrow(total)


def project_b_kernel(h_ref, w_ref, k_ref, out_ref, hidden, weights, pair, sems, out_sems):
    copies = fetch(((h_ref, hidden, 1), (w_ref, weights, 0)), sems)
    pair[:TOK] = k_ref[...]
    pair[TOK:] = project(hidden, weights, copies)
    copies = [pltpu.make_async_copy(pair, out_ref.at[i], out_sems.at[i]) for i in range(PLANE_N)]
    for copy in copies:
        copy.start()
    for copy in copies:
        copy.wait()


def project_c_kernel(h_ref, w_ref, out_ref, hidden, weights, sems):
    copies = fetch(((h_ref, hidden, 1), (w_ref, weights, 0)), sems)
    out_ref[...] = project(hidden, weights, copies)


def rows_of(ref, tile, first, tiles=1):
    rows = ref[pl.ds(tile * PIECES, tiles * PIECES), first:first + TOK]
    return rows.reshape(tiles * TILE, HEAD)


def narrow(value):
    return value.astype(jnp.bfloat16)


def weights_kernel(swapped, *refs):
    keys_ref, *q_refs = refs[:1 + RING]
    given = refs[1 + RING:-5] if swapped else ()
    p_ref, level_ref, out_ref, qs, best_ref = refs[-5:]
    y, group, core, offset = place()
    for k, q in enumerate(q_refs):
        stack_heads(qs, k, q)
    for k in range(RING):
        out_ref[k, 0:1, :] = jnp.full((1, ROWS), LOWEST, jnp.float32)
        out_ref[k, 1:2, :] = jnp.zeros((1, ROWS), jnp.float32)
    local = query_rows(offset)
    side = 1 - core if swapped else core
    edge = group // PIECES

    def scale_of(k):
        return temper(query_rows((y + k) * BLOCK + offset))

    def fill(k, own, level):
        scale = scale_of(k)

        def inner(tile, total, masked=False):
            row = pl.multiple_of(tile * TILE, TILE)
            weight = jnp.exp2(mxu(rows_of(keys_ref, tile, 0), qs[k], NT) * scale - level)
            if masked:
                weight = jnp.where(visible(tile, side, local), weight, 0.0)
            p_ref[k, pl.ds(row, TILE), :] = narrow(weight)
            return total + jnp.sum(weight.reshape(TILE // 8, 8, ROWS), axis=0)

        total = jnp.zeros((8, ROWS), jnp.float32)
        if own:
            total = inner(edge, lax.fori_loop(0, edge, inner, total), True)
        else:
            for tile in range(TILES):
                total = inner(tile, total)
        return jnp.sum(total, axis=0, keepdims=True)

    def keep(k, level, total):
        level_ref[k] = level
        if not swapped:
            out_ref[y + k, 0:1, :] = level
            out_ref[y + k, 1:2, :] = total
            return
        first = given[0][y + k, 0:1, :]
        top = jnp.maximum(first, level)
        out_ref[y + k, 0:1, :] = top
        out_ref[y + k, 1:2, :] = given[0][y + k, 1:2, :] * jnp.exp2(first - top) + total * jnp.exp2(level - top)

    def quick(k, own):
        some = mxu(keys_ref[0, :TOK], qs[k], NT) * scale_of(k)
        if own:
            key = side * TOK + lax.broadcasted_iota(jnp.int32, (TOK, 1), 0)
            some = jnp.where(key <= local, some, MASKED)
        level = jnp.maximum(jnp.max(some, axis=0, keepdims=True), LOWEST)
        total = fill(k, own, level)
        keep(k, level, total)
        return jnp.max(total) > TOO_LARGE

    def careful(k, tiles, own):
        scale = scale_of(k)
        best_ref[...] = jnp.full((1, ROWS), LOWEST, jnp.float32)

        def inner(tile, unused):
            logits = mxu(rows_of(keys_ref, tile, 0), qs[k], NT) * scale
            if own:
                logits = jnp.where(visible(tile, side, local), logits, MASKED)
            best_ref[...] = jnp.maximum(best_ref[...], jnp.max(logits, axis=0, keepdims=True))
            return unused

        lax.fori_loop(0, tiles, inner, 0)
        level = best_ref[...]
        keep(k, level, fill(k, own, level))

    pl.when(quick(0, True))(lambda: careful(0, edge + 1, True))

    def later(k, unused):
        pl.when(quick(k, False))(lambda: careful(k, TILES, False))
        return unused

    lax.fori_loop(1, RING - y, later, 0)


def student_kernel(bm_ref, bo_ref, c0, c1, c2, c3, ct, bt, acc, sums, state):
    y, group, core, offset = place()
    last = RING - y
    below = (group * TOK, (group + core) * TOK)
    row_of = lax.broadcasted_iota(jnp.int32, (TILE, 1), 0)
    for k, c in enumerate((c0, c1, c2, c3)):
        for h in range(HEADS):
            ct[k, :, h * TOK:(h + 1) * TOK] = c[:, h * HEAD:(h + 1) * HEAD].T

    def shrink(k):
        pos = query_rows((y + k) * BLOCK + offset).astype(jnp.float32)
        return 1.0 / (math.sqrt(HEAD) * (pos + 1.0))

    def early(half, tile, bs):
        return jnp.where(row_of + tile * TILE < below[half], bs, jnp.zeros_like(bs))

    before = jnp.zeros((HEAD, HEAD), jnp.float32)
    whole = jnp.zeros((HEAD, HEAD), jnp.float32)
    for half, b_ref in enumerate((bm_ref, bo_ref)):
        for tile in range(TILES):
            bs = rows_of(b_ref, tile, TOK)
            turned = bs.T
            bt[half, :, tile * TILE:(tile + 1) * TILE] = turned
            before += mxu(turned, early(half, tile, bs), NN)
            whole += mxu(turned, bs, NN)

    def apply(square, k):
        high = narrow(square)
        low = narrow(square - high.astype(jnp.float32))
        return (mxu(high, ct[k], NN) + mxu(low, ct[k], NN)) * shrink(k)

    state[...] = jnp.zeros((HEAD, HEAD), jnp.float32)

    def later(k, unused):
        acc[k] = apply(whole, k)
        state[...] += mxu(narrow(ct[k].astype(jnp.float32) * shrink(k)), ct[k], NT)
        return unused

    lax.fori_loop(1, last, later, 0)
    own = mxu(narrow(ct[0].astype(jnp.float32) * shrink(0)), ct[0], NT)
    both = narrow(jnp.concatenate([state[...], own], axis=0))
    for half, b_ref in enumerate((bm_ref, bo_ref)):
        for tile in range(TILES):
            bs = rows_of(b_ref, tile, TOK)
            pair = jnp.concatenate([bs, early(half, tile, bs)], axis=1)
            sums[half, tile * TILE:(tile + 1) * TILE, :] = mxu(pair, both, NN)

    bs = bm_ref[group, TOK:]
    error = mxu(bs, ct[0], NN) * shrink(0)
    inside = lax.broadcasted_iota(jnp.int32, (TOK, 1), 0) <= query_rows(0)
    error = narrow(jnp.where(inside, error, 0.0))
    sums[0, pl.ds(pl.multiple_of(group * TOK, TOK), TOK), :] += mxu(error, ct[0], NT)
    acc[0] = apply(before, 0) + mxu(bs, error, TN)


def lse_of(stats, chunk):
    best = functools.reduce(jnp.maximum, [t[chunk, 0:1, :] for t in stats])
    total = sum(t[chunk, 1:2, :] * jnp.exp2(t[chunk, 0:1, :] - best) for t in stats)
    return best + jnp.log(total) * LOG2E


def key_sums_kernel(half, p_ref, level_ref, t0, t1, t2, t3, ct, sums_in, *refs):
    *received, g_ref, sums = refs
    y, group, _, _ = place()
    factor = LOSS_GAIN / math.sqrt(HEAD)
    sums[...] = sums_in[half]

    def weighted(k):
        fit = jnp.exp2(level_ref[k] - lse_of((t0, t1, t2, t3), y + k))
        return narrow(ct[k].astype(jnp.float32) * fit)

    own = weighted(0)

    def inner(tile, unused):
        rows = pl.ds(pl.multiple_of(tile * TILE, TILE), TILE)
        sums[rows, :] -= mxu(p_ref[0, rows, :], own, NT)
        return unused

    lax.fori_loop(0, group // PIECES + 1, inner, 0)

    def later(k, unused):
        sums[...] -= mxu(p_ref[k], weighted(k), NT)
        return unused

    lax.fori_loop(1, RING - y, later, 0)
    value = sums[...] * factor
    if received:
        value = value + received[0][...].astype(jnp.float32)
    g_ref[...] = narrow(value)


def row_sums_kernel(pm_ref, po_ref, lm_ref, lo_ref, t0, t1, t2, t3, bt, acc_in, o0, o1, o2, o3, acc):
    y, group, _, _ = place()
    factor = LOSS_GAIN / math.sqrt(HEAD)
    last = RING - y

    def fits(k):
        lse = lse_of((t0, t1, t2, t3), y + k)
        return jnp.exp2(lm_ref[k] - lse), jnp.exp2(lo_ref[k] - lse)

    fit = fits(0)
    acc[0] = acc_in[0]

    def inner(tile, unused):
        rows = pl.ds(pl.multiple_of(tile * TILE, TILE), TILE)
        acc[0] -= mxu(bt[0, :, rows], pm_ref[0, rows, :], NN) * fit[0]
        acc[0] -= mxu(bt[1, :, rows], po_ref[0, rows, :], NN) * fit[1]
        return unused

    lax.fori_loop(0, group // PIECES + 1, inner, 0)

    def later(k, unused):
        fit = fits(k)
        mine = mxu(bt[0], pm_ref[k], NN) * fit[0]
        other = mxu(bt[1], po_ref[k], NN) * fit[1]
        acc[k] = acc_in[k] - mine - other
        return unused

    lax.fori_loop(1, last, later, 0)

    for k, o in enumerate((o0, o1, o2, o3)):
        @pl.when(k < last)
        def _():
            for h in range(HEADS):
                piece = acc[k, :, h * TOK:(h + 1) * TOK].T * factor
                o[:, h * HEAD:(h + 1) * HEAD] = piece.astype(o.dtype)

        @pl.when(k >= last)
        def _():
            o[...] = jnp.zeros(o.shape, o.dtype)


def down(value, k):
    return lax.ppermute(value, "y", [(s, s - k) for s in range(k, RING)])


def up(value, k):
    return lax.ppermute(value, "y", [(s, s + k) for s in range(RING - k)])


def around(value, k):
    return lax.ppermute(value, "y", [(s, (s + k) % RING) for s in range(RING)])


def swap(value):
    return lax.ppermute(value, "c", [(0, 1), (1, 0)])


def exchange(value):
    return lax.all_to_all(value, PLANE, 0, 0, tiled=True)


def on_device(hidden_states, w_c, w_b, teacher_q, teacher_k):
    shaped = jax.ShapeDtypeStruct
    bf16 = jnp.bfloat16
    hbm, vmem = pl.BlockSpec(memory_space=pltpu.HBM), pl.BlockSpec(memory_space=pltpu.VMEM)
    limit = pltpu.CompilerParams(vmem_limit_bytes=VMEM_LIMIT)
    pairs = pl.pallas_call(
        project_b_kernel,
        out_shape=shaped((PLANE_N, 2 * TOK, HEAD), bf16),
        in_specs=[hbm, hbm, vmem],
        out_specs=hbm,
        scratch_shapes=[pltpu.VMEM(hidden_states.shape, bf16), pltpu.VMEM(w_b.shape, bf16), pltpu.VMEM((2 * TOK, HEAD), bf16),
                        pltpu.SemaphoreType.DMA((2 * DEPTH,)), pltpu.SemaphoreType.DMA((PLANE_N,))],
        compiler_params=pltpu.CompilerParams(vmem_limit_bytes=127 * 512 * 1024),
        name="project_b",
    )(hidden_states, w_b, teacher_k)
    mine = exchange(pairs)
    queries = [teacher_q] + [down(teacher_q, k) for k in (1, 2, 3)]
    c_proj = pl.pallas_call(
        project_c_kernel,
        out_shape=shaped((TOK, ROWS), bf16),
        in_specs=[hbm, hbm],
        out_specs=vmem,
        scratch_shapes=[pltpu.VMEM(hidden_states.shape, bf16), pltpu.VMEM(w_c.shape, bf16),
                        pltpu.SemaphoreType.DMA((2 * DEPTH,))],
        compiler_params=pltpu.CompilerParams(vmem_limit_bytes=58 * 1024 * 1024),
        name="project_c",
    )(hidden_states, w_c)
    crows = [c_proj] + [down(c_proj, k) for k in (1, 2, 3)]
    other = swap(mine)

    def call(kernel, ins, outs, scratch):
        return pl.pallas_call(
            kernel,
            out_shape=outs,
            in_specs=[vmem] * len(ins),
            out_specs=jax.tree.map(lambda unused: vmem, outs),
            scratch_shapes=[pltpu.VMEM(*s) for s in scratch],
            compiler_params=limit,
        )(*ins)

    full, half = jnp.float32, jnp.bfloat16
    kept = (shaped((RING, HALF, ROWS), half), shaped((RING, 1, ROWS), full), shaped((RING, 2, ROWS), full))
    room = [((RING, ROWS, HEAD), half), ((1, ROWS), full)]
    p_mine, l_mine, first = call(
        functools.partial(weights_kernel, False), (mine, *queries), kept, room)
    p_other, l_other, stats = call(
        functools.partial(weights_kernel, True), (other, *queries, first), kept, room)
    all_stats = [stats] + [around(stats, k) for k in (1, 2, 3)]
    ct, bt, acc, sums = call(
        student_kernel, (mine, other, *crows),
        (shaped((RING, HEAD, ROWS), half), shaped((2, HEAD, HALF), half),
         shaped((RING, HEAD, ROWS), full), shaped((2, HALF, HEAD), full)),
        [((HEAD, HEAD), full)],
    )
    held = [((HALF, HEAD), full)]
    g_other = call(functools.partial(key_sums_kernel, 1),
                   (p_other, l_other, *all_stats, ct, sums), shaped((HALF, HEAD), half), held)
    g_swapped = swap(g_other)
    part = shaped((TOK, ROWS), half)
    o0, o1, o2, o3 = call(
        row_sums_kernel, (p_mine, p_other, l_mine, l_other, *all_stats, bt, acc),
        (shaped((TOK, ROWS), full), part, part, part),
        [((RING, HEAD, ROWS), full)],
    )
    g_sum = call(functools.partial(key_sums_kernel, 0),
                 (p_mine, l_mine, *all_stats, ct, sums, g_swapped), shaped((HALF, HEAD), half), held)
    g_parts = exchange(g_sum.reshape(PLANE_N, TOK, HEAD))
    given = [up(o, k) for k, o in ((1, o1), (2, o2), (3, o3))]
    rows = o0 + sum(o.astype(full) for o in given)
    grad_b = jnp.sum(g_parts.astype(full), axis=0)
    return narrow(rows), narrow(grad_b)


def solution(mesh):
    inner = Mesh(mesh.devices.reshape(SIZES), AXES)
    tokens = P(AXES, None)

    return jax.shard_map(
        on_device,
        mesh=inner,
        in_specs=(tokens, P(), P(), tokens, tokens),
        out_specs=(tokens, tokens),
        check_vma=False,
    )
```

time: 95.1 us -> 103 us (1.083); the launches traced: 94.6 us -> 101 us
  local copies, waits for them, and re-layouts: 1.79 us -> 10.9 us
  Pallas kernels: 20.9 us -> 29.7 us
  matrix products: 6.92 us -> 0 us
  waiting for transfers between devices: 12 us -> 8.11 us
    pallas_call x0 -> x2, Pallas kernels: none -> 10 us  [the longest x1 5.13 us: on_device(): pl.pallas_call(project_c_kernel, out_shape=shaped((TOK, ROWS), bf16), in_...]
    unnamed x6 -> x12, local copies, waits for them, and re-layouts: 1.59 us -> 10.9 us
    dot_general x2 -> x0, matrix products: 6.92 us -> none  [the longest x1 4.64 us: on_device(): jnp.dot(hidden_states, w_c, preferred_element_type=jnp.float32)]
    all_to_all x1, waiting for transfers between devices: 3.96 us -> 0.01 us  [exchange(): return lax.all_to_all(value, PLANE, 0, 0, tiled=True)]
    ppermute x6, waiting for transfers between devices: 0.36 us -> 1.71 us  [down(): return lax.ppermute(value, 'y', [(s, s - k) for s in range(k, RING)])]
    ppermute x3, waiting for transfers between devices: 2.3 us -> 1.01 us  [around(): return lax.ppermute(value, 'y', [(s, (s + k) % RING) for s in range(RING)])]
    pallas_call x4 -> x6, Pallas kernels: 20.9 us -> 19.7 us  [call(): pl.pallas_call(kernel, out_shape=outs, in_specs=[vmem] * len(ins), out_sp...]
  transfers between devices with their start and end apart: 15 -> 15, of which waited for: 7 -> 5; matrix products, arithmetic and copies ran while one was open for 6% -> 1% of each run, Pallas kernels for 11% -> 18%
where the time goes in v1:
time: 103 us; the launch traced here: 101 us
  Pallas kernels  29.7 us (29%)
  blocking collectives  25.1 us (24%)
  starting transfers between devices  25.1 us (24%)
  local copies, waits for them, and re-layouts  10.9 us (11%)
  waiting for transfers between devices  8.11 us (8%)
  other arithmetic  1.41 us (1%)
    all_to_all x1, blocking collectives, exchange(): return lax.all_to_all(value, PLANE, 0, 0, tiled=True)  25.1 us
    pallas_call x6, Pallas kernels, call(): pl.pallas_call(kernel, out_shape=outs, in_specs=[vmem] * len(ins), out_sp...  19.7 us
    unnamed x12, local copies, waits for them, and re-layouts  10.9 us
    all_to_all x1, starting transfers between devices, exchange(): return lax.all_to_all(value, PLANE, 0, 0, tiled=True)  10.6 us
    ppermute x6, starting transfers between devices, down(): return lax.ppermute(value, 'y', [(s, s - k) for s in range(k, RING)])  7.73 us
    pallas_call x1, Pallas kernels, on_device(): pl.pallas_call(project_c_kernel, out_shape=shaped((TOK, ROWS), bf16), in_...  5.13 us
    pallas_call x1, Pallas kernels, on_device(): pl.pallas_call(project_b_kernel, out_shape=shaped((PLANE_N, 2 * TOK, HEAD...  4.87 us
    ppermute x3, starting transfers between devices, up(): return lax.ppermute(value, 'y', [(s, s + k) for s in range(RING - k)])  3.89 us
  transfers between devices with their start and end apart: 15, of which 5 were waited for; matrix products, arithmetic and copies ran while one was open for 1% of the time, Pallas kernels for 18%

profile of v1, /device:TPU:0, one launch (start us, length us, event | category | flops | bytes accessed | tf_op | source)
XLA Modules:
  0.0 101.1 jit_solution(11841106871601177990)
XLA Ops:
  0.6 0.0 copy-start.4
  0.6 4.9 %project_b.1 = bf16[16,256,128]{2,1,0:T(8,128)(2,1)} custom-call(bf16[128,8192]{1,0:T(8,128)(2,1)} %h_ref.3, bf16[8192,128]{1,0:T(8,128)(2,1)} %w_ref.2, bf16[128,128]{1,0:T(8,128)(2,1)} %k_ref.1), custom_call_target="tpu_custom_call" | custom-call | tf_op jit(solution)/shard_map/project_b/pallas_call | solution.py:361
  5.5 25.1 %all_to_all.10.refs_0_.bm_ref = bf16[16,256,128]{2,1,0:T(8,128)(2,1)S(1)} all-to-all(bf16[16,256,128]{2,1,0:T(8,128)(2,1)} %project_b.1), channel_id=1, replica_groups=mesh['y'=4,'zl'=2,'x'=4,'zh'=2,'c'=2] {'zl','x','zh'}, dimensions={0} | all-to-all | bytes 2097152 | tf_op jit(solution)/shard_map/all_to_all | solution.py:353
  30.6 0.0 collective-permute-start.3
  30.6 1.3 %collective-permute-start.2 = (bf16[128,512]{1,0:T(8,128)(2,1)}, bf16[128,512]{1,0:T(8,128)(2,1)S(1)}, u32[]{:S(2)}, u32[]{:S(2)}) collective-permute-start(bf16[128,512]{1,0:T(8,128)(2,1)} %refs_1_.3), channel_id=1, source_target_pairs={{96,0},{97,1},{98,2},{99,3},{100,4},{101,5},{102,6},{103,7},{104,8... | collective-permute-start | bytes 393224 | tf_op jit(solution)/shard_map/ppermute | solution.py:337
  31.9 1.3 %collective-permute-start.1 = (bf16[128,512]{1,0:T(8,128)(2,1)}, bf16[128,512]{1,0:T(8,128)(2,1)S(1)}, u32[]{:S(2)}, u32[]{:S(2)}) collective-permute-start(bf16[128,512]{1,0:T(8,128)(2,1)} %refs_1_.3), channel_id=1, source_target_pairs={{64,0},{96,32},{65,1},{97,33},{66,2},{98,34},{67,3},{99,35},{68,4}... | collective-permute-start | bytes 393224 | tf_op jit(solution)/shard_map/ppermute | solution.py:337
  33.2 1.3 %collective-permute-start = (bf16[128,512]{1,0:T(8,128)(2,1)}, bf16[128,512]{1,0:T(8,128)(2,1)S(1)}, u32[]{:S(2)}, u32[]{:S(2)}) collective-permute-start(bf16[128,512]{1,0:T(8,128)(2,1)} %refs_1_.3), channel_id=1, source_target_pairs={{32,0},{64,32},{96,64},{33,1},{65,33},{97,65},{34,2},{66,34},{98,6... | collective-permute-start | bytes 393224 | tf_op jit(solution)/shard_map/ppermute | solution.py:337
  34.5 5.1 %project_c.1.c0 = bf16[128,512]{1,0:T(8,128)(2,1)} custom-call(bf16[128,8192]{1,0:T(8,128)(2,1)} %h_ref.3, bf16[8192,512]{1,0:T(8,128)(2,1)} %w_ref.3), custom_call_target="tpu_custom_call" | custom-call | tf_op jit(solution)/shard_map/project_c/pallas_call | solution.py:373
  39.6 1.3 %collective-permute-start.9 = (bf16[128,512]{1,0:T(8,128)(2,1)}, bf16[128,512]{1,0:T(8,128)(2,1)S(1)}, u32[]{:S(2)}, u32[]{:S(2)}) collective-permute-start(bf16[128,512]{1,0:T(8,128)(2,1)} %project_c.1.c0), channel_id=1, source_target_pairs={{96,0},{97,1},{98,2},{99,3},{100,4},{101,5},{102,6},{103,7},{104,8... | collective-permute-start | bytes 393224 | tf_op jit(solution)/shard_map/ppermute | solution.py:337
  40.9 1.7 %collective-permute-done.2.refs_4_ = bf16[128,512]{1,0:T(8,128)(2,1)S(1)} collective-permute-done((bf16[128,512]{1,0:T(8,128)(2,1)}, bf16[128,512]{1,0:T(8,128)(2,1)S(1)}, u32[]{:S(2)}, u32[]{:S(2)}) %collective-permute-start.2) | collective-permute-done | bytes 131104 | tf_op jit(solution)/shard_map/ppermute | solution.py:337
  42.6 1.3 %collective-permute-start.8 = (bf16[128,512]{1,0:T(8,128)(2,1)}, bf16[128,512]{1,0:T(8,128)(2,1)S(1)}, u32[]{:S(2)}, u32[]{:S(2)}) collective-permute-start(bf16[128,512]{1,0:T(8,128)(2,1)} %project_c.1.c0), channel_id=1, source_target_pairs={{64,0},{96,32},{65,1},{97,33},{66,2},{98,34},{67,3},{99,35},{68,4}... | collective-permute-start | bytes 393224 | tf_op jit(solution)/shard_map/ppermute | solution.py:337
  43.9 0.0 collective-permute-done.1.refs_3_
  43.9 1.3 %collective-permute-start.7 = (bf16[128,512]{1,0:T(8,128)(2,1)}, bf16[128,512]{1,0:T(8,128)(2,1)S(1)}, u32[]{:S(2)}, u32[]{:S(2)}) collective-permute-start(bf16[128,512]{1,0:T(8,128)(2,1)} %project_c.1.c0), channel_id=1, source_target_pairs={{32,0},{64,32},{96,64},{33,1},{65,33},{97,65},{34,2},{66,34},{98,6... | collective-permute-start | bytes 393224 | tf_op jit(solution)/shard_map/ppermute | solution.py:337
  45.2 0.0 collective-permute-done.refs_2_
  45.2 0.0 copy-done.4
  45.2 3.7 %shard_map.68 = (bf16[4,2048,512]{2,1,0:T(8,128)(2,1)S(1)}, f32[4,1,512]{2,1,0:T(1,128)S(1)}, f32[4,2,512]{2,1,0:T(2,128)S(1)}) custom-call(bf16[16,256,128]{2,1,0:T(8,128)(2,1)S(1)} %all_to_all.10.refs_0_.bm_ref, bf16[128,512]{1,0:T(8,128)(2,1)S(1)} %copy-done.4, bf16[128,512]{1,0:T(8,128)(2,1)S(1)} %collective-permute-done.refs_2_, ...), custom_call_target="tpu_custom_call" | custom-call | tf_op jit(solution)/shard_map/pallas_call | solution.py:387
  48.9 0.0 copy-start.2
  48.9 0.0 collective-permute-done.3.refs_0_.bo_ref
  49.0 3.7 %shard_map.69 = (bf16[4,2048,512]{2,1,0:T(8,128)(2,1)S(1)}, f32[4,1,512]{2,1,0:T(1,128)S(1)}, f32[4,2,512]{2,1,0:T(2,128)S(1)}) custom-call(bf16[16,256,128]{2,1,0:T(8,128)(2,1)S(1)} %collective-permute-done.3.refs_0_.bo_ref, bf16[128,512]{1,0:T(8,128)(2,1)S(1)} %copy-done.4, bf16[128,512]{1,0:T(8,128)(2,1)S(1)} %collective-permute-done.refs_2_, ...), custom_call_target="tpu_custom_call" | custom-call | tf_op jit(solution)/shard_map/pallas_call | solution.py:387
  52.7 0.1 collective-permute-start.6
  52.7 2.8 %collective-permute-start.5 = (f32[4,2,512]{2,1,0:T(2,128)S(1)}, f32[4,2,512]{2,1,0:T(2,128)S(1)}, u32[]{:S(2)}, u32[]{:S(2)}) collective-permute-start(f32[4,2,512]{2,1,0:T(2,128)S(1)} %get-tuple-element.21.t0), channel_id=1, source_target_pairs={{0,64},{32,96},{64,0},{96,32},{1,65},{33,97},{65,1},{97,33},{2,66}... | collective-permute-start | bytes 49160 | tf_op jit(solution)/shard_map/ppermute | solution.py:345
  55.5 0.0 collective-permute-done.9.c3
  55.5 0.0 collective-permute-start.4
  55.5 0.0 collective-permute-done.8.c2
  55.5 0.0 collective-permute-done.7.c1
  55.6 0.0 copy-start.5
  55.6 0.9 copy-done.5
  56.5 3.0 %shard_map.70 = (bf16[4,128,512]{2,1,0:T(8,128)(2,1)S(1)}, bf16[2,128,2048]{2,1,0:T(8,128)(2,1)S(1)}, f32[4,128,512]{2,1,0:T(8,128)S(1)}, f32[2,2048,128]{2,1,0:T(8,128)S(1)}) custom-call(bf16[16,256,128]{2,1,0:T(8,128)(2,1)S(1)} %all_to_all.10.refs_0_.bm_ref, bf16[16,256,128]{2,1,0:T(8,128)(2,1)S(1)} %collective-permute-done.3.refs_0_.bo_ref, ...), custom_call_target="tpu_custom_call" | custom-call | tf_op jit(solution)/shard_map/pallas_call | solution.py:387
  59.5 0.0 collective-permute-done.6.t3
  59.5 0.0 collective-permute-done.5.t2
  59.5 1.0 collective-permute-done.4.t1
  60.5 2.7 %shard_map.72 = bf16[2048,128]{1,0:T(8,128)(2,1)S(1)} custom-call(bf16[4,2048,512]{2,1,0:T(8,128)(2,1)S(1)} %get-tuple-element.18.po_ref.p_ref, f32[4,1,512]{2,1,0:T(1,128)S(1)} %get-tuple-element.20.lo_ref.level_ref, f32[4,2,512]{2,1,0:T(2,128)S(1)} %get-tuple-element.21.t0, f32[4,2,512]{2,1,0:T(2,128)S(1)} %collective-permute-done.4.t1, ...), custom_call_target="tpu_custom_call" | custom-call | tf_op jit(solution)/shard_map/pallas_call | solution.py:387
  63.2 0.0 copy-start
  63.2 3.2 %copy-done = bf16[4,2048,512]{2,1,0:T(8,128)(2,1)} copy-done((bf16[4,2048,512]{2,1,0:T(8,128)(2,1)}, bf16[4,2048,512]{2,1,0:T(8,128)(2,1)S(1)}, u32[]{:S(2)}) %copy-start) | copy-done | bytes 8388632
  66.4 0.0 collective-permute-start.13
  66.4 1.9 %collective-permute-done.13.refs_0_ = bf16[2048,128]{1,0:T(8,128)(2,1)S(1)} collective-permute-done((bf16[2048,128]{1,0:T(8,128)(2,1)S(1)}, bf16[2048,128]{1,0:T(8,128)(2,1)S(1)}, u32[]{:S(2)}, u32[]{:S(2)}) %collective-permute-start.13) | collective-permute-done | bytes 524320 | tf_op jit(solution)/shard_map/ppermute | solution.py:349
  68.3 3.6 %shard_map.73 = bf16[2048,128]{1,0:T(8,128)(2,1)} custom-call(bf16[4,2048,512]{2,1,0:T(8,128)(2,1)S(1)} %get-tuple-element.16.pm_ref.p_ref, f32[4,1,512]{2,1,0:T(1,128)S(1)} %get-tuple-element.19.lm_ref.level_ref, f32[4,2,512]{2,1,0:T(2,128)S(1)} %get-tuple-element.21.t0, f32[4,2,512]{2,1,0:T(2,128)S(1)} %collective-permute-done.4.t1, ...), custom_call_target="tpu_custom_call" | custom-call | tf_op jit(solution)/shard_map/pallas_call | solution.py:387
  71.9 0.0 copy-done.2
  71.9 10.6 %all-to-all-start.1 = ((bf16[16,128,128]{2,1,0:T(8,128)(2,1)}), bf16[16,128,128]{2,1,0:T(8,128)(2,1)S(1)}, u32[]{:S(2)}, u32[]{:S(2)}) async-start(bf16[16,128,128]{2,1,0:T(8,128)(2,1)} %bitcast), calls=%async_computation.1 | async-start | bytes 1048576 | tf_op jit(solution)/shard_map/all_to_all | solution.py:353
  82.5 0.0 copy-start.1
  82.5 3.4 %copy-done.1 = bf16[4,2048,512]{2,1,0:T(8,128)(2,1)S(1)} copy-done((bf16[4,2048,512]{2,1,0:T(8,128)(2,1)S(1)}, bf16[4,2048,512]{2,1,0:T(8,128)(2,1)}, u32[]{:S(2)}) %copy-start.1) | copy-done | bytes 8388632
  85.9 0.0 copy-start.3
  85.9 3.4 %copy-done.3 = bf16[4,2048,512]{2,1,0:T(8,128)(2,1)S(1)} copy-done((bf16[4,2048,512]{2,1,0:T(8,128)(2,1)S(1)}, bf16[4,2048,512]{2,1,0:T(8,128)(2,1)}, u32[]{:S(2)}) %copy-start.3) | copy-done | bytes 8388632
  89.2 3.1 %shard_map.71 = (f32[128,512]{1,0:T(8,128)S(1)}, bf16[128,512]{1,0:T(8,128)(2,1)S(1)}, bf16[128,512]{1,0:T(8,128)(2,1)S(1)}, bf16[128,512]{1,0:T(8,128)(2,1)S(1)}) custom-call(bf16[4,2048,512]{2,1,0:T(8,128)(2,1)S(1)} %copy-done.3, bf16[4,2048,512]{2,1,0:T(8,128)(2,1)S(1)} %copy-done.1, f32[4,1,512]{2,1,0:T(1,128)S(1)} %get-tuple-element.19.lm_ref.level_ref, ...), custom_call_target="tpu_custom_call" | custom-call | tf_op jit(solution)/shard_map/pallas_call | solution.py:387
  92.3 1.3 %collective-permute-start.10 = (bf16[128,512]{1,0:T(8,128)(2,1)S(1)}, bf16[128,512]{1,0:T(8,128)(2,1)S(1)}, u32[]{:S(2)}, u32[]{:S(2)}) collective-permute-start(bf16[128,512]{1,0:T(8,128)(2,1)S(1)} %get-tuple-element.25), channel_id=1, source_target_pairs={{0,32},{32,64},{64,96},{1,33},{33,65},{65,97},{2,34},{34,66},{66,9... | collective-permute-start | bytes 393224 | tf_op jit(solution)/shard_map/ppermute | solution.py:341
  93.6 1.3 %collective-permute-start.11 = (bf16[128,512]{1,0:T(8,128)(2,1)S(1)}, bf16[128,512]{1,0:T(8,128)(2,1)S(1)}, u32[]{:S(2)}, u32[]{:S(2)}) collective-permute-start(bf16[128,512]{1,0:T(8,128)(2,1)S(1)} %get-tuple-element.26), channel_id=1, source_target_pairs={{0,64},{32,96},{1,65},{33,97},{2,66},{34,98},{3,67},{35,99},{4,68}... | collective-permute-start | bytes 393224 | tf_op jit(solution)/shard_map/ppermute | solution.py:341
  94.9 1.3 %collective-permute-start.12 = (bf16[128,512]{1,0:T(8,128)(2,1)S(1)}, bf16[128,512]{1,0:T(8,128)(2,1)S(1)}, u32[]{:S(2)}, u32[]{:S(2)}) collective-permute-start(bf16[128,512]{1,0:T(8,128)(2,1)S(1)} %get-tuple-element.27), channel_id=1, source_target_pairs={{0,96},{1,97},{2,98},{3,99},{4,100},{5,101},{6,102},{7,103},{8,104... | collective-permute-start | bytes 393224 | tf_op jit(solution)/shard_map/ppermute | solution.py:341
  96.2 1.3 %collective-permute-done.10 = bf16[128,512]{1,0:T(8,128)(2,1)S(1)} collective-permute-done((bf16[128,512]{1,0:T(8,128)(2,1)S(1)}, bf16[128,512]{1,0:T(8,128)(2,1)S(1)}, u32[]{:S(2)}, u32[]{:S(2)}) %collective-permute-start.10) | collective-permute-done | bytes 131104 | tf_op jit(solution)/shard_map/ppermute | solution.py:341
  97.5 2.2 %collective-permute-done.11 = bf16[128,512]{1,0:T(8,128)(2,1)S(1)} collective-permute-done((bf16[128,512]{1,0:T(8,128)(2,1)S(1)}, bf16[128,512]{1,0:T(8,128)(2,1)S(1)}, u32[]{:S(2)}, u32[]{:S(2)}) %collective-permute-start.11) | collective-permute-done | bytes 131104 | tf_op jit(solution)/shard_map/ppermute | solution.py:341
  99.7 0.0 collective-permute-done.12
  99.7 0.7 add_convert_fusion
  100.4 0.0 all-to-all-done.1
  100.4 0.7 reduce_sum.12
Async XLA Ops:
  0.6 44.6 %copy-start.4 = (bf16[128,512]{1,0:T(8,128)(2,1)S(1)}, bf16[128,512]{1,0:T(8,128)(2,1)}, u32[]{:S(2)}) copy-start(bf16[128,512]{1,0:T(8,128)(2,1)} %refs_1_.3) | copy-start | bytes 393220
  30.6 18.4 %collective-permute-start.3 = (bf16[16,256,128]{2,1,0:T(8,128)(2,1)S(1)}, bf16[16,256,128]{2,1,0:T(8,128)(2,1)S(1)}, u32[]{:S(2)}, u32[]{:S(2)}) collective-permute-start(bf16[16,256,128]{2,1,0:T(8,128)(2,1)S(1)} %all_to_all.10.refs_0_.bm_ref), channel_id=1, source_target_pairs={{0,1},{1,0},{2,3},{3,2},{4,5},{5,4},{6,7},{7,6},{8,9},{9,8},{10,11... | collective-permute-start | bytes 3145736 | tf_op jit(solution)/shard_map/ppermute | solution.py:349
  30.6 12.0 %collective-permute-start.2 = (bf16[128,512]{1,0:T(8,128)(2,1)}, bf16[128,512]{1,0:T(8,128)(2,1)S(1)}, u32[]{:S(2)}, u32[]{:S(2)}) collective-permute-start(bf16[128,512]{1,0:T(8,128)(2,1)} %refs_1_.3), channel_id=1, source_target_pairs={{96,0},{97,1},{98,2},{99,3},{100,4},{101,5},{102,6},{103,7},{104,8... | collective-permute-start | bytes 393224 | tf_op jit(solution)/shard_map/ppermute | solution.py:337
  31.9 12.0 %collective-permute-start.1 = (bf16[128,512]{1,0:T(8,128)(2,1)}, bf16[128,512]{1,0:T(8,128)(2,1)S(1)}, u32[]{:S(2)}, u32[]{:S(2)}) collective-permute-start(bf16[128,512]{1,0:T(8,128)(2,1)} %refs_1_.3), channel_id=1, source_target_pairs={{64,0},{96,32},{65,1},{97,33},{66,2},{98,34},{67,3},{99,35},{68,4}... | collective-permute-start | bytes 393224 | tf_op jit(solution)/shard_map/ppermute | solution.py:337
  33.2 12.0 %collective-permute-start = (bf16[128,512]{1,0:T(8,128)(2,1)}, bf16[128,512]{1,0:T(8,128)(2,1)S(1)}, u32[]{:S(2)}, u32[]{:S(2)}) collective-permute-start(bf16[128,512]{1,0:T(8,128)(2,1)} %refs_1_.3), channel_id=1, source_target_pairs={{32,0},{64,32},{96,64},{33,1},{65,33},{97,65},{34,2},{66,34},{98,6... | collective-permute-start | bytes 393224 | tf_op jit(solution)/shard_map/ppermute | solution.py:337
  39.6 15.9 %collective-permute-start.9 = (bf16[128,512]{1,0:T(8,128)(2,1)}, bf16[128,512]{1,0:T(8,128)(2,1)S(1)}, u32[]{:S(2)}, u32[]{:S(2)}) collective-permute-start(bf16[128,512]{1,0:T(8,128)(2,1)} %project_c.1.c0), channel_id=1, source_target_pairs={{96,0},{97,1},{98,2},{99,3},{100,4},{101,5},{102,6},{103,7},{104,8... | collective-permute-start | bytes 393224 | tf_op jit(solution)/shard_map/ppermute | solution.py:337
  42.6 12.9 %collective-permute-start.8 = (bf16[128,512]{1,0:T(8,128)(2,1)}, bf16[128,512]{1,0:T(8,128)(2,1)S(1)}, u32[]{:S(2)}, u32[]{:S(2)}) collective-permute-start(bf16[128,512]{1,0:T(8,128)(2,1)} %project_c.1.c0), channel_id=1, source_target_pairs={{64,0},{96,32},{65,1},{97,33},{66,2},{98,34},{67,3},{99,35},{68,4}... | collective-permute-start | bytes 393224 | tf_op jit(solution)/shard_map/ppermute | solution.py:337
  43.9 11.6 %collective-permute-start.7 = (bf16[128,512]{1,0:T(8,128)(2,1)}, bf16[128,512]{1,0:T(8,128)(2,1)S(1)}, u32[]{:S(2)}, u32[]{:S(2)}) collective-permute-start(bf16[128,512]{1,0:T(8,128)(2,1)} %project_c.1.c0), channel_id=1, source_target_pairs={{32,0},{64,32},{96,64},{33,1},{65,33},{97,65},{34,2},{66,34},{98,6... | collective-permute-start | bytes 393224 | tf_op jit(solution)/shard_map/ppermute | solution.py:337
  48.9 23.0 %copy-start.2 = (bf16[4,2048,512]{2,1,0:T(8,128)(2,1)}, bf16[4,2048,512]{2,1,0:T(8,128)(2,1)S(1)}, u32[]{:S(2)}) copy-start(bf16[4,2048,512]{2,1,0:T(8,128)(2,1)S(1)} %get-tuple-element.16.pm_ref.p_ref) | copy-start | bytes 25165828
  52.7 6.8 %collective-permute-start.6 = (f32[4,2,512]{2,1,0:T(2,128)S(1)}, f32[4,2,512]{2,1,0:T(2,128)S(1)}, u32[]{:S(2)}, u32[]{:S(2)}) collective-permute-start(f32[4,2,512]{2,1,0:T(2,128)S(1)} %get-tuple-element.21.t0), channel_id=1, source_target_pairs={{0,96},{32,0},{64,32},{96,64},{1,97},{33,1},{65,33},{97,65},{2,98}... | collective-permute-start | bytes 49160 | tf_op jit(solution)/shard_map/ppermute | solution.py:345
  52.7 6.7 %collective-permute-start.5 = (f32[4,2,512]{2,1,0:T(2,128)S(1)}, f32[4,2,512]{2,1,0:T(2,128)S(1)}, u32[]{:S(2)}, u32[]{:S(2)}) collective-permute-start(f32[4,2,512]{2,1,0:T(2,128)S(1)} %get-tuple-element.21.t0), channel_id=1, source_target_pairs={{0,64},{32,96},{64,0},{96,32},{1,65},{33,97},{65,1},{97,33},{2,66}... | collective-permute-start | bytes 49160 | tf_op jit(solution)/shard_map/ppermute | solution.py:345
  55.5 5.0 %collective-permute-start.4 = (f32[4,2,512]{2,1,0:T(2,128)S(1)}, f32[4,2,512]{2,1,0:T(2,128)S(1)}, u32[]{:S(2)}, u32[]{:S(2)}) collective-permute-start(f32[4,2,512]{2,1,0:T(2,128)S(1)} %get-tuple-element.21.t0), channel_id=1, source_target_pairs={{0,32},{32,64},{64,96},{96,0},{1,33},{33,65},{65,97},{97,1},{2,34}... | collective-permute-start | bytes 49160 | tf_op jit(solution)/shard_map/ppermute | solution.py:345
  55.6 0.9 copy-start.5
  63.2 3.2 %copy-start = (bf16[4,2048,512]{2,1,0:T(8,128)(2,1)}, bf16[4,2048,512]{2,1,0:T(8,128)(2,1)S(1)}, u32[]{:S(2)}) copy-start(bf16[4,2048,512]{2,1,0:T(8,128)(2,1)S(1)} %get-tuple-element.18.po_ref.p_ref) | copy-start | bytes 25165828
  66.4 1.9 %collective-permute-start.13 = (bf16[2048,128]{1,0:T(8,128)(2,1)S(1)}, bf16[2048,128]{1,0:T(8,128)(2,1)S(1)}, u32[]{:S(2)}, u32[]{:S(2)}) collective-permute-start(bf16[2048,128]{1,0:T(8,128)(2,1)S(1)} %shard_map.72), channel_id=1, source_target_pairs={{0,1},{1,0},{2,3},{3,2},{4,5},{5,4},{6,7},{7,6},{8,9},{9,8},{10,11... | collective-permute-start | bytes 1572872 | tf_op jit(solution)/shard_map/ppermute | solution.py:349
  71.9 28.5 %all-to-all-start.1 = ((bf16[16,128,128]{2,1,0:T(8,128)(2,1)}), bf16[16,128,128]{2,1,0:T(8,128)(2,1)S(1)}, u32[]{:S(2)}, u32[]{:S(2)}) async-start(bf16[16,128,128]{2,1,0:T(8,128)(2,1)} %bitcast), calls=%async_computation.1 | async-start | bytes 1048576 | tf_op jit(solution)/shard_map/all_to_all | solution.py:353
  82.5 3.4 %copy-start.1 = (bf16[4,2048,512]{2,1,0:T(8,128)(2,1)S(1)}, bf16[4,2048,512]{2,1,0:T(8,128)(2,1)}, u32[]{:S(2)}) copy-start(bf16[4,2048,512]{2,1,0:T(8,128)(2,1)} %copy-done) | copy-start | bytes 25165828
  85.9 3.4 %copy-start.3 = (bf16[4,2048,512]{2,1,0:T(8,128)(2,1)S(1)}, bf16[4,2048,512]{2,1,0:T(8,128)(2,1)}, u32[]{:S(2)}) copy-start(bf16[4,2048,512]{2,1,0:T(8,128)(2,1)} %copy-done.2) | copy-start | bytes 25165828
  92.3 5.2 %collective-permute-start.10 = (bf16[128,512]{1,0:T(8,128)(2,1)S(1)}, bf16[128,512]{1,0:T(8,128)(2,1)S(1)}, u32[]{:S(2)}, u32[]{:S(2)}) collective-permute-start(bf16[128,512]{1,0:T(8,128)(2,1)S(1)} %get-tuple-element.25), channel_id=1, source_target_pairs={{0,32},{32,64},{64,96},{1,33},{33,65},{65,97},{2,34},{34,66},{66,9... | collective-permute-start | bytes 393224 | tf_op jit(solution)/shard_map/ppermute | solution.py:341
  93.6 6.1 %collective-permute-start.11 = (bf16[128,512]{1,0:T(8,128)(2,1)S(1)}, bf16[128,512]{1,0:T(8,128)(2,1)S(1)}, u32[]{:S(2)}, u32[]{:S(2)}) collective-permute-start(bf16[128,512]{1,0:T(8,128)(2,1)S(1)} %get-tuple-element.26), channel_id=1, source_target_pairs={{0,64},{32,96},{1,65},{33,97},{2,66},{34,98},{3,67},{35,99},{4,68}... | collective-permute-start | bytes 393224 | tf_op jit(solution)/shard_map/ppermute | solution.py:341
  94.9 4.8 %collective-permute-start.12 = (bf16[128,512]{1,0:T(8,128)(2,1)S(1)}, bf16[128,512]{1,0:T(8,128)(2,1)S(1)}, u32[]{:S(2)}, u32[]{:S(2)}) collective-permute-start(bf16[128,512]{1,0:T(8,128)(2,1)S(1)} %get-tuple-element.27), channel_id=1, source_target_pairs={{0,96},{1,97},{2,98},{3,99},{4,100},{5,101},{6,102},{7,103},{8,104... | collective-permute-start | bytes 393224 | tf_op jit(solution)/shard_map/ppermute | solution.py:341

commit v2 on v1

--- a/solution.py
+++ b/solution.py
@@ -24,10 +24,10 @@
 HALF = PLANE_N * TOK
 BLOCK = 2 * HALF
 ROWS = HEADS * TOK
-TILE = 512
+TILE = 1024
 TILES = HALF // TILE
 PIECES = TILE // TOK
-DEPTH = 8
+DEPTH = 4
 MASKED = -1e30
 LOWEST = -1e29
 TOO_LARGE = 2.0 ** 60
@@ -263,7 +263,9 @@
 
 
 def key_sums_kernel(half, p_ref, level_ref, t0, t1, t2, t3, ct, sums_in, *refs):
-    *received, g_ref, sums = refs
+    spread = half == 0
+    received = refs[0] if spread else None
+    *spread_refs, sums = refs[1:] if spread else refs
     y, group, _, _ = place()
     factor = LOSS_GAIN / math.sqrt(HEAD)
     sums[...] = sums_in[half]
@@ -286,10 +288,26 @@
         return unused
 
     lax.fori_loop(1, RING - y, later, 0)
-    value = sums[...] * factor
-    if received:
-        value = value + received[0][...].astype(jnp.float32)
-    g_ref[...] = narrow(value)
+    if not spread:
+        spread_refs[0][...] = narrow(sums[...] * factor)
+        return
+    x = lax.axis_index("x")
+    for k, ref in enumerate(spread_refs):
+        for z in range(RING):
+            spot = (z // 2) * 2 * RING + ((x + k) & (RING - 1)) * 2 + z % 2
+            rows = pl.ds(pl.multiple_of(spot * TOK, TOK), TOK)
+            ref[z] = (sums[rows, :] * factor + received[rows, :].astype(jnp.float32)).astype(ref.dtype)
+
+
+def join_x_kernel(own, r1, r2, r3, s0, s1, s2, s3, sums):
+    total = own[...]
+    for ref in (r1, r2, r3):
+        total = total + ref[...].astype(jnp.float32)
+    sums[...] = total
+    z = lax.axis_index("zh") * 2 + lax.axis_index("zl")
+    for k, ref in enumerate((s0, s1, s2, s3)):
+        target = (z + k) & (RING - 1)
+        ref[...] = sums[(target & 1) * 2 + (target >> 1)].astype(ref.dtype)
 
 
 def row_sums_kernel(pm_ref, po_ref, lm_ref, lo_ref, t0, t1, t2, t3, bt, acc_in, o0, o1, o2, o3, acc):
@@ -343,6 +361,15 @@
 
 def around(value, k):
     return lax.ppermute(value, "y", [(s, (s + k) % RING) for s in range(RING)])
+
+
+def along_x(value, k):
+    return lax.ppermute(value, "x", [(s, (s + k) % RING) for s in range(RING)])
+
+
+def along_z(value, k):
+    index = [(z % 2) * 2 + z // 2 for z in range(RING)]
+    return lax.ppermute(value, ("zl", "zh"), [(index[z], index[(z + k) % RING]) for z in range(RING)])
 
 
 def swap(value):
@@ -411,18 +438,25 @@
     g_other = call(functools.partial(key_sums_kernel, 1),
                    (p_other, l_other, *all_stats, ct, sums), shaped((HALF, HEAD), half), held)
     g_swapped = swap(g_other)
+    sent = shaped((RING, TOK, HEAD), half)
+    g0, *g_sent = call(
+        functools.partial(key_sums_kernel, 0),
+        (p_mine, l_mine, *all_stats, ct, sums, g_swapped),
+        (shaped((RING, TOK, HEAD), full), sent, sent, sent), held)
+    g_near = [along_x(g, k) for k, g in enumerate(g_sent, 1)]
     part = shaped((TOK, ROWS), half)
-    o0, o1, o2, o3 = call(
+    o0, *o_sent = call(
         row_sums_kernel, (p_mine, p_other, l_mine, l_other, *all_stats, bt, acc),
         (shaped((TOK, ROWS), full), part, part, part),
         [((RING, HEAD, ROWS), full)],
     )
-    g_sum = call(functools.partial(key_sums_kernel, 0),
-                 (p_mine, l_mine, *all_stats, ct, sums, g_swapped), shaped((HALF, HEAD), half), held)
-    g_parts = exchange(g_sum.reshape(PLANE_N, TOK, HEAD))
-    given = [up(o, k) for k, o in ((1, o1), (2, o2), (3, o3))]
+    given = [up(o, k) for k, o in enumerate(o_sent, 1)]
+    sent = shaped((TOK, HEAD), half)
+    h0, *h_sent = call(join_x_kernel, (g0, *g_near), (shaped((TOK, HEAD), full), sent, sent, sent),
+                       [((RING, TOK, HEAD), full)])
+    g_far = [along_z(h, k) for k, h in enumerate(h_sent, 1)]
     rows = o0 + sum(o.astype(full) for o in given)
-    grad_b = jnp.sum(g_parts.astype(full), axis=0)
+    grad_b = h0 + sum(h.astype(full) for h in g_far)
     return narrow(rows), narrow(grad_b)
 
 

time: 103 us -> 93.3 us (0.906); the launches traced: 101 us -> 92.9 us
  local copies, waits for them, and re-layouts: 10.9 us -> 0.91 us
  starting transfers between devices: 25.1 us -> 27 us
    ppermute x0 -> x6, starting transfers between devices: none -> 12.4 us  [the longest x3 7.89 us: along_z(): lax.ppermute(value, ('zl', 'zh'), [(index[z], index[(z + k) % RING]) for...]
    all_to_all x1 -> x0, starting transfers between devices: 10.6 us -> none  [exchange(): return lax.all_to_all(value, PLANE, 0, 0, tiled=True)]
    unnamed x12 -> x4, local copies, waits for them, and re-layouts: 10.9 us -> 0.91 us
    ppermute x3, waiting for transfers between devices: 3.47 us -> 0.01 us  [up(): return lax.ppermute(value, 'y', [(s, s + k) for s in range(RING - k)])]
    ppermute x0 -> x6, waiting for transfers between devices: none -> 3.18 us  [the longest x3 3.18 us: along_z(): lax.ppermute(value, ('zl', 'zh'), [(index[z], index[(z + k) % RING]) for...]
    pallas_call x6 -> x7, Pallas kernels: 19.7 us -> 20.1 us  [call(): pl.pallas_call(kernel, out_shape=outs, in_specs=[vmem] * len(ins), out_sp...]
  transfers between devices with their start and end apart: 15 -> 20, of which waited for: 5 -> 5; matrix products, arithmetic and copies ran while one was open for 1% -> 1% of each run, Pallas kernels for 18% -> 21%
where the time goes in v2:
time: 93.3 us; the launch traced here: 92.9 us
  Pallas kernels  29.9 us (32%)
  starting transfers between devices  27 us (29%)
  blocking collectives  25.1 us (27%)
  waiting for transfers between devices  7.75 us (8%)
  other arithmetic  1.35 us (1%)
    all_to_all x1, blocking collectives, exchange(): return lax.all_to_all(value, PLANE, 0, 0, tiled=True)  25.1 us
    pallas_call x7, Pallas kernels, call(): pl.pallas_call(kernel, out_shape=outs, in_specs=[vmem] * len(ins), out_sp...  20.1 us
    ppermute x3, starting transfers between devices, along_z(): lax.ppermute(value, ('zl', 'zh'), [(index[z], index[(z + k) % RING]) for...  7.89 us
    ppermute x6, starting transfers between devices, down(): return lax.ppermute(value, 'y', [(s, s - k) for s in range(k, RING)])  7.73 us
    pallas_call x1, Pallas kernels, on_device(): pl.pallas_call(project_c_kernel, out_shape=shaped((TOK, ROWS), bf16), in_...  5.27 us
    ppermute x3, starting transfers between devices, along_x(): return lax.ppermute(value, 'x', [(s, (s + k) % RING) for s in range(RING)])  4.56 us
    pallas_call x1, Pallas kernels, on_device(): pl.pallas_call(project_b_kernel, out_shape=shaped((PLANE_N, 2 * TOK, HEAD...  4.54 us
    ppermute x3, starting transfers between devices, up(): return lax.ppermute(value, 'y', [(s, s + k) for s in range(RING - k)])  3.89 us
  transfers between devices with their start and end apart: 20, of which 5 were waited for; matrix products, arithmetic and copies ran while one was open for 1% of the time, Pallas kernels for 21%

profile of v2, /device:TPU:0, one launch (start us, length us, event | category | flops | bytes accessed | tf_op | source)
XLA Modules:
  0.0 92.9 jit_solution(10923786655068258037)
XLA Ops:
  0.6 0.0 copy-start
  0.6 4.5 %project_b.1 = bf16[16,256,128]{2,1,0:T(8,128)(2,1)} custom-call(bf16[128,8192]{1,0:T(8,128)(2,1)} %h_ref.3, bf16[8192,128]{1,0:T(8,128)(2,1)} %w_ref.2, bf16[128,128]{1,0:T(8,128)(2,1)} %k_ref.1), custom_call_target="tpu_custom_call" | custom-call | tf_op jit(solution)/shard_map/project_b/pallas_call | solution.py:388
  5.2 25.1 %all_to_all.5.refs_0_.bm_ref = bf16[16,256,128]{2,1,0:T(8,128)(2,1)S(1)} all-to-all(bf16[16,256,128]{2,1,0:T(8,128)(2,1)} %project_b.1), channel_id=1, replica_groups=mesh['y'=4,'zl'=2,'x'=4,'zh'=2,'c'=2] {'zl','x','zh'}, dimensions={0} | all-to-all | bytes 2097152 | tf_op jit(solution)/shard_map/all_to_all | solution.py:380
  30.2 0.0 collective-permute-start.3
  30.2 1.3 %collective-permute-start.2 = (bf16[128,512]{1,0:T(8,128)(2,1)}, bf16[128,512]{1,0:T(8,128)(2,1)S(1)}, u32[]{:S(2)}, u32[]{:S(2)}) collective-permute-start(bf16[128,512]{1,0:T(8,128)(2,1)} %refs_1_.3), channel_id=1, source_target_pairs={{96,0},{97,1},{98,2},{99,3},{100,4},{101,5},{102,6},{103,7},{104,8... | collective-permute-start | bytes 393224 | tf_op jit(solution)/shard_map/ppermute | solution.py:355
  31.5 1.3 %collective-permute-start.1 = (bf16[128,512]{1,0:T(8,128)(2,1)}, bf16[128,512]{1,0:T(8,128)(2,1)S(1)}, u32[]{:S(2)}, u32[]{:S(2)}) collective-permute-start(bf16[128,512]{1,0:T(8,128)(2,1)} %refs_1_.3), channel_id=1, source_target_pairs={{64,0},{96,32},{65,1},{97,33},{66,2},{98,34},{67,3},{99,35},{68,4}... | collective-permute-start | bytes 393224 | tf_op jit(solution)/shard_map/ppermute | solution.py:355
  32.8 1.3 %collective-permute-start = (bf16[128,512]{1,0:T(8,128)(2,1)}, bf16[128,512]{1,0:T(8,128)(2,1)S(1)}, u32[]{:S(2)}, u32[]{:S(2)}) collective-permute-start(bf16[128,512]{1,0:T(8,128)(2,1)} %refs_1_.3), channel_id=1, source_target_pairs={{32,0},{64,32},{96,64},{33,1},{65,33},{97,65},{34,2},{66,34},{98,6... | collective-permute-start | bytes 393224 | tf_op jit(solution)/shard_map/ppermute | solution.py:355
  34.1 5.3 %project_c.1.c0 = bf16[128,512]{1,0:T(8,128)(2,1)} custom-call(bf16[128,8192]{1,0:T(8,128)(2,1)} %h_ref.3, bf16[8192,512]{1,0:T(8,128)(2,1)} %w_ref.3), custom_call_target="tpu_custom_call" | custom-call | tf_op jit(solution)/shard_map/project_c/pallas_call | solution.py:400
  39.4 1.3 %collective-permute-start.9 = (bf16[128,512]{1,0:T(8,128)(2,1)}, bf16[128,512]{1,0:T(8,128)(2,1)S(1)}, u32[]{:S(2)}, u32[]{:S(2)}) collective-permute-start(bf16[128,512]{1,0:T(8,128)(2,1)} %project_c.1.c0), channel_id=1, source_target_pairs={{96,0},{97,1},{98,2},{99,3},{100,4},{101,5},{102,6},{103,7},{104,8... | collective-permute-start | bytes 393224 | tf_op jit(solution)/shard_map/ppermute | solution.py:355
  40.7 1.6 %collective-permute-done.2.refs_4_ = bf16[128,512]{1,0:T(8,128)(2,1)S(1)} collective-permute-done((bf16[128,512]{1,0:T(8,128)(2,1)}, bf16[128,512]{1,0:T(8,128)(2,1)S(1)}, u32[]{:S(2)}, u32[]{:S(2)}) %collective-permute-start.2) | collective-permute-done | bytes 131104 | tf_op jit(solution)/shard_map/ppermute | solution.py:355
  42.3 1.3 %collective-permute-start.8 = (bf16[128,512]{1,0:T(8,128)(2,1)}, bf16[128,512]{1,0:T(8,128)(2,1)S(1)}, u32[]{:S(2)}, u32[]{:S(2)}) collective-permute-start(bf16[128,512]{1,0:T(8,128)(2,1)} %project_c.1.c0), channel_id=1, source_target_pairs={{64,0},{96,32},{65,1},{97,33},{66,2},{98,34},{67,3},{99,35},{68,4}... | collective-permute-start | bytes 393224 | tf_op jit(solution)/shard_map/ppermute | solution.py:355
  43.6 0.0 collective-permute-done.1.refs_3_
  43.6 1.3 %collective-permute-start.7 = (bf16[128,512]{1,0:T(8,128)(2,1)}, bf16[128,512]{1,0:T(8,128)(2,1)S(1)}, u32[]{:S(2)}, u32[]{:S(2)}) collective-permute-start(bf16[128,512]{1,0:T(8,128)(2,1)} %project_c.1.c0), channel_id=1, source_target_pairs={{32,0},{64,32},{96,64},{33,1},{65,33},{97,65},{34,2},{66,34},{98,6... | collective-permute-start | bytes 393224 | tf_op jit(solution)/shard_map/ppermute | solution.py:355
  44.9 0.0 collective-permute-done.refs_2_
  44.9 0.0 copy-done
  44.9 4.0 %shard_map.68 = (bf16[4,2048,512]{2,1,0:T(8,128)(2,1)S(1)}, f32[4,1,512]{2,1,0:T(1,128)S(1)}, f32[4,2,512]{2,1,0:T(2,128)S(1)}) custom-call(bf16[16,256,128]{2,1,0:T(8,128)(2,1)S(1)} %all_to_all.5.refs_0_.bm_ref, bf16[128,512]{1,0:T(8,128)(2,1)S(1)} %copy-done, bf16[128,512]{1,0:T(8,128)(2,1)S(1)} %collective-permute-done.refs_2_, ...), custom_call_target="tpu_custom_call" | custom-call | tf_op jit(solution)/shard_map/pallas_call | solution.py:414
  48.9 0.0 collective-permute-done.3.refs_0_.bo_ref
  48.9 4.2 %shard_map.69 = (bf16[4,2048,512]{2,1,0:T(8,128)(2,1)S(1)}, f32[4,1,512]{2,1,0:T(1,128)S(1)}, f32[4,2,512]{2,1,0:T(2,128)S(1)}) custom-call(bf16[16,256,128]{2,1,0:T(8,128)(2,1)S(1)} %collective-permute-done.3.refs_0_.bo_ref, bf16[128,512]{1,0:T(8,128)(2,1)S(1)} %copy-done, bf16[128,512]{1,0:T(8,128)(2,1)S(1)} %collective-permute-done.refs_2_, ...), custom_call_target="tpu_custom_call" | custom-call | tf_op jit(solution)/shard_map/pallas_call | solution.py:414
  53.1 0.1 collective-permute-start.6
  53.2 2.8 %collective-permute-start.5 = (f32[4,2,512]{2,1,0:T(2,128)S(1)}, f32[4,2,512]{2,1,0:T(2,128)S(1)}, u32[]{:S(2)}, u32[]{:S(2)}) collective-permute-start(f32[4,2,512]{2,1,0:T(2,128)S(1)} %get-tuple-element.29.t0), channel_id=1, source_target_pairs={{0,64},{32,96},{64,0},{96,32},{1,65},{33,97},{65,1},{97,33},{2,66}... | collective-permute-start | bytes 49160 | tf_op jit(solution)/shard_map/ppermute | solution.py:363
  56.0 0.0 collective-permute-done.9.c3
  56.0 0.0 collective-permute-start.4
  56.0 0.0 collective-permute-done.8.c2
  56.0 0.0 collective-permute-done.7.c1
  56.0 0.0 copy-start.1
  56.0 0.9 copy-done.1
  56.9 2.9 %shard_map.70 = (bf16[4,128,512]{2,1,0:T(8,128)(2,1)S(1)}, bf16[2,128,2048]{2,1,0:T(8,128)(2,1)S(1)}, f32[4,128,512]{2,1,0:T(8,128)S(1)}, f32[2,2048,128]{2,1,0:T(8,128)S(1)}) custom-call(bf16[16,256,128]{2,1,0:T(8,128)(2,1)S(1)} %all_to_all.5.refs_0_.bm_ref, bf16[16,256,128]{2,1,0:T(8,128)(2,1)S(1)} %collective-permute-done.3.refs_0_.bo_ref, ...), custom_call_target="tpu_custom_call" | custom-call | tf_op jit(solution)/shard_map/pallas_call | solution.py:414
  59.8 0.0 collective-permute-done.6.t3
  59.8 0.0 collective-permute-done.5.t2
  59.8 1.1 %collective-permute-done.4.t1 = f32[4,2,512]{2,1,0:T(2,128)S(1)} collective-permute-done((f32[4,2,512]{2,1,0:T(2,128)S(1)}, f32[4,2,512]{2,1,0:T(2,128)S(1)}, u32[]{:S(2)}, u32[]{:S(2)}) %collective-permute-start.4) | collective-permute-done | bytes 16416 | tf_op jit(solution)/shard_map/ppermute | solution.py:363
  60.9 2.9 %shard_map.72 = bf16[2048,128]{1,0:T(8,128)(2,1)S(1)} custom-call(bf16[4,2048,512]{2,1,0:T(8,128)(2,1)S(1)} %get-tuple-element.26.po_ref.p_ref, f32[4,1,512]{2,1,0:T(1,128)S(1)} %get-tuple-element.28.lo_ref.level_ref, f32[4,2,512]{2,1,0:T(2,128)S(1)} %get-tuple-element.29.t0, f32[4,2,512]{2,1,0:T(2,128)S(1)} %collective-permute-done.4.t1, ...), custom_call_target="tpu_custom_call" | custom-call | tf_op jit(solution)/shard_map/pallas_call | solution.py:414
  63.8 0.1 collective-permute-start.13
  63.9 1.9 %collective-permute-done.13.refs_0_ = bf16[2048,128]{1,0:T(8,128)(2,1)S(1)} collective-permute-done((bf16[2048,128]{1,0:T(8,128)(2,1)S(1)}, bf16[2048,128]{1,0:T(8,128)(2,1)S(1)}, u32[]{:S(2)}, u32[]{:S(2)}) %collective-permute-start.13) | collective-permute-done | bytes 524320 | tf_op jit(solution)/shard_map/ppermute | solution.py:376
  65.8 2.9 %shard_map.73 = (f32[4,128,128]{2,1,0:T(8,128)S(1)}, bf16[4,128,128]{2,1,0:T(8,128)(2,1)S(1)}, bf16[4,128,128]{2,1,0:T(8,128)(2,1)S(1)}, bf16[4,128,128]{2,1,0:T(8,128)(2,1)S(1)}) custom-call(bf16[4,2048,512]{2,1,0:T(8,128)(2,1)S(1)} %get-tuple-element.24.pm_ref.p_ref, f32[4,1,512]{2,1,0:T(1,128)S(1)} %get-tuple-element.27.lm_ref.level_ref, ...), custom_call_target="tpu_custom_call" | custom-call | tf_op jit(solution)/shard_map/pallas_call | solution.py:414
  68.7 0.6 collective-permute-start.14
  69.3 2.3 %collective-permute-start.15 = (bf16[4,128,128]{2,1,0:T(8,128)(2,1)S(1)}, bf16[4,128,128]{2,1,0:T(8,128)(2,1)S(1)}, u32[]{:S(2)}, u32[]{:S(2)}) collective-permute-start(bf16[4,128,128]{2,1,0:T(8,128)(2,1)S(1)} %get-tuple-element.40), channel_id=1, source_target_pairs={{0,8},{4,12},{8,0},{12,4},{1,9},{5,13},{9,1},{13,5},{2,10},{6,14},... | collective-permute-start | bytes 393224 | tf_op jit(solution)/shard_map/ppermute | solution.py:367
  71.6 1.6 %collective-permute-start.16 = (bf16[4,128,128]{2,1,0:T(8,128)(2,1)S(1)}, bf16[4,128,128]{2,1,0:T(8,128)(2,1)S(1)}, u32[]{:S(2)}, u32[]{:S(2)}) collective-permute-start(bf16[4,128,128]{2,1,0:T(8,128)(2,1)S(1)} %get-tuple-element.41), channel_id=1, source_target_pairs={{0,12},{4,0},{8,4},{12,8},{1,13},{5,1},{9,5},{13,9},{2,14},{6,2},{... | collective-permute-start | bytes 393224 | tf_op jit(solution)/shard_map/ppermute | solution.py:367
  73.2 3.2 %shard_map.71 = (f32[128,512]{1,0:T(8,128)S(1)}, bf16[128,512]{1,0:T(8,128)(2,1)S(1)}, bf16[128,512]{1,0:T(8,128)(2,1)S(1)}, bf16[128,512]{1,0:T(8,128)(2,1)S(1)}) custom-call(bf16[4,2048,512]{2,1,0:T(8,128)(2,1)S(1)} %get-tuple-element.24.pm_ref.p_ref, bf16[4,2048,512]{2,1,0:T(8,128)(2,1)S(1)} %get-tuple-element.26.po_ref.p_ref, ...), custom_call_target="tpu_custom_call" | custom-call | tf_op jit(solution)/shard_map/pallas_call | solution.py:414
  76.4 1.3 %collective-permute-start.10 = (bf16[128,512]{1,0:T(8,128)(2,1)S(1)}, bf16[128,512]{1,0:T(8,128)(2,1)S(1)}, u32[]{:S(2)}, u32[]{:S(2)}) collective-permute-start(bf16[128,512]{1,0:T(8,128)(2,1)S(1)} %get-tuple-element.33), channel_id=1, source_target_pairs={{0,32},{32,64},{64,96},{1,33},{33,65},{65,97},{2,34},{34,66},{66,9... | collective-permute-start | bytes 393224 | tf_op jit(solution)/shard_map/ppermute | solution.py:359
  77.7 1.3 %collective-permute-start.11 = (bf16[128,512]{1,0:T(8,128)(2,1)S(1)}, bf16[128,512]{1,0:T(8,128)(2,1)S(1)}, u32[]{:S(2)}, u32[]{:S(2)}) collective-permute-start(bf16[128,512]{1,0:T(8,128)(2,1)S(1)} %get-tuple-element.34), channel_id=1, source_target_pairs={{0,64},{32,96},{1,65},{33,97},{2,66},{34,98},{3,67},{35,99},{4,68}... | collective-permute-start | bytes 393224 | tf_op jit(solution)/shard_map/ppermute | solution.py:359
  79.0 0.0 collective-permute-done.14.r1
  79.1 1.3 %collective-permute-start.12 = (bf16[128,512]{1,0:T(8,128)(2,1)S(1)}, bf16[128,512]{1,0:T(8,128)(2,1)S(1)}, u32[]{:S(2)}, u32[]{:S(2)}) collective-permute-start(bf16[128,512]{1,0:T(8,128)(2,1)S(1)} %get-tuple-element.35), channel_id=1, source_target_pairs={{0,96},{1,97},{2,98},{3,99},{4,100},{5,101},{6,102},{7,103},{8,104... | collective-permute-start | bytes 393224 | tf_op jit(solution)/shard_map/ppermute | solution.py:359
  80.4 0.0 collective-permute-done.15.r2
  80.4 0.0 collective-permute-done.16.r3
  80.4 0.1 shard_map.74
  80.5 2.8 %collective-permute-start.17 = (bf16[128,128]{1,0:T(8,128)(2,1)S(1)}, bf16[128,128]{1,0:T(8,128)(2,1)S(1)}, u32[]{:S(2)}, u32[]{:S(2)}) collective-permute-start(bf16[128,128]{1,0:T(8,128)(2,1)S(1)} %get-tuple-element.43), channel_id=1, source_target_pairs={{0,16},{16,2},{2,18},{18,0},{1,17},{17,3},{3,19},{19,1},{4,20},{20... | collective-permute-start | bytes 98312 | tf_op jit(solution)/shard_map/ppermute | solution.py:372
  83.3 5.0 %collective-permute-start.18 = (bf16[128,128]{1,0:T(8,128)(2,1)S(1)}, bf16[128,128]{1,0:T(8,128)(2,1)S(1)}, u32[]{:S(2)}, u32[]{:S(2)}) collective-permute-start(bf16[128,128]{1,0:T(8,128)(2,1)S(1)} %get-tuple-element.44), channel_id=1, source_target_pairs={{0,2},{16,18},{2,0},{18,16},{1,3},{17,19},{3,1},{19,17},{4,6},{20,... | collective-permute-start | bytes 98312 | tf_op jit(solution)/shard_map/ppermute | solution.py:372
  88.4 0.0 collective-permute-done.10
  88.4 0.0 collective-permute-start.19
  88.4 0.0 collective-permute-done.11
  88.4 0.0 collective-permute-done.12
  88.4 0.7 add_convert_fusion
  89.1 0.0 collective-permute-done.17
  89.1 1.5 %collective-permute-done.18 = bf16[128,128]{1,0:T(8,128)(2,1)S(1)} collective-permute-done((bf16[128,128]{1,0:T(8,128)(2,1)S(1)}, bf16[128,128]{1,0:T(8,128)(2,1)S(1)}, u32[]{:S(2)}, u32[]{:S(2)}) %collective-permute-start.18) | collective-permute-done | bytes 32800 | tf_op jit(solution)/shard_map/ppermute | solution.py:372
  90.6 1.7 %collective-permute-done.19 = bf16[128,128]{1,0:T(8,128)(2,1)S(1)} collective-permute-done((bf16[128,128]{1,0:T(8,128)(2,1)S(1)}, bf16[128,128]{1,0:T(8,128)(2,1)S(1)}, u32[]{:S(2)}, u32[]{:S(2)}) %collective-permute-start.19) | collective-permute-done | bytes 32800 | tf_op jit(solution)/shard_map/ppermute | solution.py:372
  92.3 0.6 add_convert_fusion.1
Async XLA Ops:
  0.6 44.2 %copy-start = (bf16[128,512]{1,0:T(8,128)(2,1)S(1)}, bf16[128,512]{1,0:T(8,128)(2,1)}, u32[]{:S(2)}) copy-start(bf16[128,512]{1,0:T(8,128)(2,1)} %refs_1_.3) | copy-start | bytes 393220
  30.2 18.7 %collective-permute-start.3 = (bf16[16,256,128]{2,1,0:T(8,128)(2,1)S(1)}, bf16[16,256,128]{2,1,0:T(8,128)(2,1)S(1)}, u32[]{:S(2)}, u32[]{:S(2)}) collective-permute-start(bf16[16,256,128]{2,1,0:T(8,128)(2,1)S(1)} %all_to_all.5.refs_0_.bm_ref), channel_id=1, source_target_pairs={{0,1},{1,0},{2,3},{3,2},{4,5},{5,4},{6,7},{7,6},{8,9},{9,8},{10,11... | collective-permute-start | bytes 3145736 | tf_op jit(solution)/shard_map/ppermute | solution.py:376
  30.2 12.0 %collective-permute-start.2 = (bf16[128,512]{1,0:T(8,128)(2,1)}, bf16[128,512]{1,0:T(8,128)(2,1)S(1)}, u32[]{:S(2)}, u32[]{:S(2)}) collective-permute-start(bf16[128,512]{1,0:T(8,128)(2,1)} %refs_1_.3), channel_id=1, source_target_pairs={{96,0},{97,1},{98,2},{99,3},{100,4},{101,5},{102,6},{103,7},{104,8... | collective-permute-start | bytes 393224 | tf_op jit(solution)/shard_map/ppermute | solution.py:355
  31.5 12.0 %collective-permute-start.1 = (bf16[128,512]{1,0:T(8,128)(2,1)}, bf16[128,512]{1,0:T(8,128)(2,1)S(1)}, u32[]{:S(2)}, u32[]{:S(2)}) collective-permute-start(bf16[128,512]{1,0:T(8,128)(2,1)} %refs_1_.3), channel_id=1, source_target_pairs={{64,0},{96,32},{65,1},{97,33},{66,2},{98,34},{67,3},{99,35},{68,4}... | collective-permute-start | bytes 393224 | tf_op jit(solution)/shard_map/ppermute | solution.py:355
  32.8 12.0 %collective-permute-start = (bf16[128,512]{1,0:T(8,128)(2,1)}, bf16[128,512]{1,0:T(8,128)(2,1)S(1)}, u32[]{:S(2)}, u32[]{:S(2)}) collective-permute-start(bf16[128,512]{1,0:T(8,128)(2,1)} %refs_1_.3), channel_id=1, source_target_pairs={{32,0},{64,32},{96,64},{33,1},{65,33},{97,65},{34,2},{66,34},{98,6... | collective-permute-start | bytes 393224 | tf_op jit(solution)/shard_map/ppermute | solution.py:355
  39.4 16.6 %collective-permute-start.9 = (bf16[128,512]{1,0:T(8,128)(2,1)}, bf16[128,512]{1,0:T(8,128)(2,1)S(1)}, u32[]{:S(2)}, u32[]{:S(2)}) collective-permute-start(bf16[128,512]{1,0:T(8,128)(2,1)} %project_c.1.c0), channel_id=1, source_target_pairs={{96,0},{97,1},{98,2},{99,3},{100,4},{101,5},{102,6},{103,7},{104,8... | collective-permute-start | bytes 393224 | tf_op jit(solution)/shard_map/ppermute | solution.py:355
  42.3 13.7 %collective-permute-start.8 = (bf16[128,512]{1,0:T(8,128)(2,1)}, bf16[128,512]{1,0:T(8,128)(2,1)S(1)}, u32[]{:S(2)}, u32[]{:S(2)}) collective-permute-start(bf16[128,512]{1,0:T(8,128)(2,1)} %project_c.1.c0), channel_id=1, source_target_pairs={{64,0},{96,32},{65,1},{97,33},{66,2},{98,34},{67,3},{99,35},{68,4}... | collective-permute-start | bytes 393224 | tf_op jit(solution)/shard_map/ppermute | solution.py:355
  43.6 12.4 %collective-permute-start.7 = (bf16[128,512]{1,0:T(8,128)(2,1)}, bf16[128,512]{1,0:T(8,128)(2,1)S(1)}, u32[]{:S(2)}, u32[]{:S(2)}) collective-permute-start(bf16[128,512]{1,0:T(8,128)(2,1)} %project_c.1.c0), channel_id=1, source_target_pairs={{32,0},{64,32},{96,64},{33,1},{65,33},{97,65},{34,2},{66,34},{98,6... | collective-permute-start | bytes 393224 | tf_op jit(solution)/shard_map/ppermute | solution.py:355
  53.1 6.7 %collective-permute-start.6 = (f32[4,2,512]{2,1,0:T(2,128)S(1)}, f32[4,2,512]{2,1,0:T(2,128)S(1)}, u32[]{:S(2)}, u32[]{:S(2)}) collective-permute-start(f32[4,2,512]{2,1,0:T(2,128)S(1)} %get-tuple-element.29.t0), channel_id=1, source_target_pairs={{0,96},{32,0},{64,32},{96,64},{1,97},{33,1},{65,33},{97,65},{2,98}... | collective-permute-start | bytes 49160 | tf_op jit(solution)/shard_map/ppermute | solution.py:363
  53.2 6.7 %collective-permute-start.5 = (f32[4,2,512]{2,1,0:T(2,128)S(1)}, f32[4,2,512]{2,1,0:T(2,128)S(1)}, u32[]{:S(2)}, u32[]{:S(2)}) collective-permute-start(f32[4,2,512]{2,1,0:T(2,128)S(1)} %get-tuple-element.29.t0), channel_id=1, source_target_pairs={{0,64},{32,96},{64,0},{96,32},{1,65},{33,97},{65,1},{97,33},{2,66}... | collective-permute-start | bytes 49160 | tf_op jit(solution)/shard_map/ppermute | solution.py:363
  56.0 5.0 %collective-permute-start.4 = (f32[4,2,512]{2,1,0:T(2,128)S(1)}, f32[4,2,512]{2,1,0:T(2,128)S(1)}, u32[]{:S(2)}, u32[]{:S(2)}) collective-permute-start(f32[4,2,512]{2,1,0:T(2,128)S(1)} %get-tuple-element.29.t0), channel_id=1, source_target_pairs={{0,32},{32,64},{64,96},{96,0},{1,33},{33,65},{65,97},{97,1},{2,34}... | collective-permute-start | bytes 49160 | tf_op jit(solution)/shard_map/ppermute | solution.py:363
  56.0 0.9 copy-start.1
  63.8 2.0 %collective-permute-start.13 = (bf16[2048,128]{1,0:T(8,128)(2,1)S(1)}, bf16[2048,128]{1,0:T(8,128)(2,1)S(1)}, u32[]{:S(2)}, u32[]{:S(2)}) collective-permute-start(bf16[2048,128]{1,0:T(8,128)(2,1)S(1)} %shard_map.72), channel_id=1, source_target_pairs={{0,1},{1,0},{2,3},{3,2},{4,5},{5,4},{6,7},{7,6},{8,9},{9,8},{10,11... | collective-permute-start | bytes 1572872 | tf_op jit(solution)/shard_map/ppermute | solution.py:376
  68.7 10.4 %collective-permute-start.14 = (bf16[4,128,128]{2,1,0:T(8,128)(2,1)S(1)}, bf16[4,128,128]{2,1,0:T(8,128)(2,1)S(1)}, u32[]{:S(2)}, u32[]{:S(2)}) collective-permute-start(bf16[4,128,128]{2,1,0:T(8,128)(2,1)S(1)} %get-tuple-element.39), channel_id=1, source_target_pairs={{0,4},{4,8},{8,12},{12,0},{1,5},{5,9},{9,13},{13,1},{2,6},{6,10},{... | collective-permute-start | bytes 393224 | tf_op jit(solution)/shard_map/ppermute | solution.py:367
  69.3 11.1 %collective-permute-start.15 = (bf16[4,128,128]{2,1,0:T(8,128)(2,1)S(1)}, bf16[4,128,128]{2,1,0:T(8,128)(2,1)S(1)}, u32[]{:S(2)}, u32[]{:S(2)}) collective-permute-start(bf16[4,128,128]{2,1,0:T(8,128)(2,1)S(1)} %get-tuple-element.40), channel_id=1, source_target_pairs={{0,8},{4,12},{8,0},{12,4},{1,9},{5,13},{9,1},{13,5},{2,10},{6,14},... | collective-permute-start | bytes 393224 | tf_op jit(solution)/shard_map/ppermute | solution.py:367
  71.6 8.8 %collective-permute-start.16 = (bf16[4,128,128]{2,1,0:T(8,128)(2,1)S(1)}, bf16[4,128,128]{2,1,0:T(8,128)(2,1)S(1)}, u32[]{:S(2)}, u32[]{:S(2)}) collective-permute-start(bf16[4,128,128]{2,1,0:T(8,128)(2,1)S(1)} %get-tuple-element.41), channel_id=1, source_target_pairs={{0,12},{4,0},{8,4},{12,8},{1,13},{5,1},{9,5},{13,9},{2,14},{6,2},{... | collective-permute-start | bytes 393224 | tf_op jit(solution)/shard_map/ppermute | solution.py:367
  76.4 11.9 %collective-permute-start.10 = (bf16[128,512]{1,0:T(8,128)(2,1)S(1)}, bf16[128,512]{1,0:T(8,128)(2,1)S(1)}, u32[]{:S(2)}, u32[]{:S(2)}) collective-permute-start(bf16[128,512]{1,0:T(8,128)(2,1)S(1)} %get-tuple-element.33), channel_id=1, source_target_pairs={{0,32},{32,64},{64,96},{1,33},{33,65},{65,97},{2,34},{34,66},{66,9... | collective-permute-start | bytes 393224 | tf_op jit(solution)/shard_map/ppermute | solution.py:359
  77.7 10.6 %collective-permute-start.11 = (bf16[128,512]{1,0:T(8,128)(2,1)S(1)}, bf16[128,512]{1,0:T(8,128)(2,1)S(1)}, u32[]{:S(2)}, u32[]{:S(2)}) collective-permute-start(bf16[128,512]{1,0:T(8,128)(2,1)S(1)} %get-tuple-element.34), channel_id=1, source_target_pairs={{0,64},{32,96},{1,65},{33,97},{2,66},{34,98},{3,67},{35,99},{4,68}... | collective-permute-start | bytes 393224 | tf_op jit(solution)/shard_map/ppermute | solution.py:359
  79.1 9.3 %collective-permute-start.12 = (bf16[128,512]{1,0:T(8,128)(2,1)S(1)}, bf16[128,512]{1,0:T(8,128)(2,1)S(1)}, u32[]{:S(2)}, u32[]{:S(2)}) collective-permute-start(bf16[128,512]{1,0:T(8,128)(2,1)S(1)} %get-tuple-element.35), channel_id=1, source_target_pairs={{0,96},{1,97},{2,98},{3,99},{4,100},{5,101},{6,102},{7,103},{8,104... | collective-permute-start | bytes 393224 | tf_op jit(solution)/shard_map/ppermute | solution.py:359
  80.5 8.6 %collective-permute-start.17 = (bf16[128,128]{1,0:T(8,128)(2,1)S(1)}, bf16[128,128]{1,0:T(8,128)(2,1)S(1)}, u32[]{:S(2)}, u32[]{:S(2)}) collective-permute-start(bf16[128,128]{1,0:T(8,128)(2,1)S(1)} %get-tuple-element.43), channel_id=1, source_target_pairs={{0,16},{16,2},{2,18},{18,0},{1,17},{17,3},{3,19},{19,1},{4,20},{20... | collective-permute-start | bytes 98312 | tf_op jit(solution)/shard_map/ppermute | solution.py:372
  83.3 7.3 %collective-permute-start.18 = (bf16[128,128]{1,0:T(8,128)(2,1)S(1)}, bf16[128,128]{1,0:T(8,128)(2,1)S(1)}, u32[]{:S(2)}, u32[]{:S(2)}) collective-permute-start(bf16[128,128]{1,0:T(8,128)(2,1)S(1)} %get-tuple-element.44), channel_id=1, source_target_pairs={{0,2},{16,18},{2,0},{18,16},{1,3},{17,19},{3,1},{19,17},{4,6},{20,... | collective-permute-start | bytes 98312 | tf_op jit(solution)/shard_map/ppermute | solution.py:372
  88.4 3.9 %collective-permute-start.19 = (bf16[128,128]{1,0:T(8,128)(2,1)S(1)}, bf16[128,128]{1,0:T(8,128)(2,1)S(1)}, u32[]{:S(2)}, u32[]{:S(2)}) collective-permute-start(bf16[128,128]{1,0:T(8,128)(2,1)S(1)} %get-tuple-element.45), channel_id=1, source_target_pairs={{0,18},{16,0},{2,16},{18,2},{1,19},{17,1},{3,17},{19,3},{4,22},{20... | collective-permute-start | bytes 98312 | tf_op jit(solution)/shard_map/ppermute | solution.py:372

commit v3 on v2

--- a/solution.py
+++ b/solution.py
@@ -310,7 +310,8 @@
         ref[...] = sums[(target & 1) * 2 + (target >> 1)].astype(ref.dtype)
 
 
-def row_sums_kernel(pm_ref, po_ref, lm_ref, lo_ref, t0, t1, t2, t3, bt, acc_in, o0, o1, o2, o3, acc):
+def row_sums_kernel(early, pm_ref, po_ref, lm_ref, lo_ref, t0, t1, t2, t3, bt, acc_in, *refs):
+    *outs, acc = refs
     y, group, _, _ = place()
     factor = LOSS_GAIN / math.sqrt(HEAD)
     last = RING - y
@@ -319,36 +320,41 @@
         lse = lse_of((t0, t1, t2, t3), y + k)
         return jnp.exp2(lm_ref[k] - lse), jnp.exp2(lo_ref[k] - lse)
 
-    fit = fits(0)
-    acc[0] = acc_in[0]
-
-    def inner(tile, unused):
-        rows = pl.ds(pl.multiple_of(tile * TILE, TILE), TILE)
-        acc[0] -= mxu(bt[0, :, rows], pm_ref[0, rows, :], NN) * fit[0]
-        acc[0] -= mxu(bt[1, :, rows], po_ref[0, rows, :], NN) * fit[1]
-        return unused
-
-    lax.fori_loop(0, group // PIECES + 1, inner, 0)
-
-    def later(k, unused):
+    def whole(k):
         fit = fits(k)
         mine = mxu(bt[0], pm_ref[k], NN) * fit[0]
         other = mxu(bt[1], po_ref[k], NN) * fit[1]
-        acc[k] = acc_in[k] - mine - other
-        return unused
-
-    lax.fori_loop(1, last, later, 0)
-
-    for k, o in enumerate((o0, o1, o2, o3)):
+        return acc_in[k] - mine - other
+
+    def give(o, value):
+        for h in range(HEADS):
+            o[:, h * HEAD:(h + 1) * HEAD] = (value[:, h * TOK:(h + 1) * TOK].T * factor).astype(o.dtype)
+
+    def later(k, o):
         @pl.when(k < last)
         def _():
-            for h in range(HEADS):
-                piece = acc[k, :, h * TOK:(h + 1) * TOK].T * factor
-                o[:, h * HEAD:(h + 1) * HEAD] = piece.astype(o.dtype)
+            give(o, whole(k))
 
         @pl.when(k >= last)
         def _():
             o[...] = jnp.zeros(o.shape, o.dtype)
+
+    if early:
+        later(3, outs[0])
+        later(2, outs[1])
+        return
+    later(1, outs[1])
+    fit = fits(0)
+    acc[...] = acc_in[0]
+
+    def inner(tile, unused):
+        rows = pl.ds(pl.multiple_of(tile * TILE, TILE), TILE)
+        acc[...] -= mxu(bt[0, :, rows], pm_ref[0, rows, :], NN) * fit[0]
+        acc[...] -= mxu(bt[1, :, rows], po_ref[0, rows, :], NN) * fit[1]
+        return unused
+
+    lax.fori_loop(0, group // PIECES + 1, inner, 0)
+    give(outs[0], acc[...])
 
 
 def down(value, k):
@@ -445,12 +451,12 @@
         (shaped((RING, TOK, HEAD), full), sent, sent, sent), held)
     g_near = [along_x(g, k) for k, g in enumerate(g_sent, 1)]
     part = shaped((TOK, ROWS), half)
-    o0, *o_sent = call(
-        row_sums_kernel, (p_mine, p_other, l_mine, l_other, *all_stats, bt, acc),
-        (shaped((TOK, ROWS), full), part, part, part),
-        [((RING, HEAD, ROWS), full)],
-    )
-    given = [up(o, k) for k, o in enumerate(o_sent, 1)]
+    row_ins = (p_mine, p_other, l_mine, l_other, *all_stats, bt, acc)
+    row_room = [((HEAD, ROWS), full)]
+    o3, o2 = call(functools.partial(row_sums_kernel, True), row_ins, (part, part), row_room)
+    o0, o1 = call(functools.partial(row_sums_kernel, False), row_ins,
+                  (shaped((TOK, ROWS), full), part), row_room)
+    given = [up(o, k) for k, o in enumerate((o1, o2, o3), 1)]
     sent = shaped((TOK, HEAD), half)
     h0, *h_sent = call(join_x_kernel, (g0, *g_near), (shaped((TOK, HEAD), full), sent, sent, sent),
                        [((RING, TOK, HEAD), full)])

time: 93.3 us -> 93.2 us (level)
    pallas_call x7 -> x8, Pallas kernels: 20.1 us -> 20.1 us  [call(): pl.pallas_call(kernel, out_shape=outs, in_specs=[vmem] * len(ins), out_sp...]
where the time goes in v3:
time: 93.2 us; the launch traced here: 92.9 us
  Pallas kernels  29.9 us (32%)
  starting transfers between devices  27 us (29%)
  blocking collectives  25.1 us (27%)
  waiting for transfers between devices  7.75 us (8%)
  other arithmetic  1.35 us (1%)
    all_to_all x1, blocking collectives, exchange(): return lax.all_to_all(value, PLANE, 0, 0, tiled=True)  25.1 us
    pallas_call x8, Pallas kernels, call(): pl.pallas_call(kernel, out_shape=outs, in_specs=[vmem] * len(ins), out_sp...  20.1 us
    ppermute x3, starting transfers between devices, along_z(): lax.ppermute(value, ('zl', 'zh'), [(index[z], index[(z + k) % RING]) for...  7.89 us
    ppermute x6, starting transfers between devices, down(): return lax.ppermute(value, 'y', [(s, s - k) for s in range(k, RING)])  7.73 us
    pallas_call x1, Pallas kernels, on_device(): pl.pallas_call(project_c_kernel, out_shape=shaped((TOK, ROWS), bf16), in_...  5.27 us
    ppermute x3, starting transfers between devices, along_x(): return lax.ppermute(value, 'x', [(s, (s + k) % RING) for s in range(RING)])  4.56 us
    pallas_call x1, Pallas kernels, on_device(): pl.pallas_call(project_b_kernel, out_shape=shaped((PLANE_N, 2 * TOK, HEAD...  4.54 us
    ppermute x3, starting transfers between devices, up(): return lax.ppermute(value, 'y', [(s, s + k) for s in range(RING - k)])  3.89 us
  transfers between devices with their start and end apart: 20, of which 5 were waited for; matrix products, arithmetic and copies ran while one was open for 1% of the time, Pallas kernels for 21%

profile of v3, /device:TPU:0, one launch (start us, length us, event | category | flops | bytes accessed | tf_op | source)
XLA Modules:
  0.0 92.9 jit_solution(7178456406277464663)
XLA Ops:
  0.6 0.0 copy-start
  0.6 4.5 %project_b.1 = bf16[16,256,128]{2,1,0:T(8,128)(2,1)} custom-call(bf16[128,8192]{1,0:T(8,128)(2,1)} %h_ref.3, bf16[8192,128]{1,0:T(8,128)(2,1)} %w_ref.2, bf16[128,128]{1,0:T(8,128)(2,1)} %k_ref.1), custom_call_target="tpu_custom_call" | custom-call | tf_op jit(solution)/shard_map/project_b/pallas_call | solution.py:394
  5.2 25.1 %all_to_all.5.refs_0_.bm_ref = bf16[16,256,128]{2,1,0:T(8,128)(2,1)S(1)} all-to-all(bf16[16,256,128]{2,1,0:T(8,128)(2,1)} %project_b.1), channel_id=1, replica_groups=mesh['y'=4,'zl'=2,'x'=4,'zh'=2,'c'=2] {'zl','x','zh'}, dimensions={0} | all-to-all | bytes 2097152 | tf_op jit(solution)/shard_map/all_to_all | solution.py:386
  30.2 0.0 collective-permute-start.3
  30.2 1.3 %collective-permute-start.2 = (bf16[128,512]{1,0:T(8,128)(2,1)}, bf16[128,512]{1,0:T(8,128)(2,1)S(1)}, u32[]{:S(2)}, u32[]{:S(2)}) collective-permute-start(bf16[128,512]{1,0:T(8,128)(2,1)} %refs_1_.3), channel_id=1, source_target_pairs={{96,0},{97,1},{98,2},{99,3},{100,4},{101,5},{102,6},{103,7},{104,8... | collective-permute-start | bytes 393224 | tf_op jit(solution)/shard_map/ppermute | solution.py:361
  31.5 1.3 %collective-permute-start.1 = (bf16[128,512]{1,0:T(8,128)(2,1)}, bf16[128,512]{1,0:T(8,128)(2,1)S(1)}, u32[]{:S(2)}, u32[]{:S(2)}) collective-permute-start(bf16[128,512]{1,0:T(8,128)(2,1)} %refs_1_.3), channel_id=1, source_target_pairs={{64,0},{96,32},{65,1},{97,33},{66,2},{98,34},{67,3},{99,35},{68,4}... | collective-permute-start | bytes 393224 | tf_op jit(solution)/shard_map/ppermute | solution.py:361
  32.8 1.3 %collective-permute-start = (bf16[128,512]{1,0:T(8,128)(2,1)}, bf16[128,512]{1,0:T(8,128)(2,1)S(1)}, u32[]{:S(2)}, u32[]{:S(2)}) collective-permute-start(bf16[128,512]{1,0:T(8,128)(2,1)} %refs_1_.3), channel_id=1, source_target_pairs={{32,0},{64,32},{96,64},{33,1},{65,33},{97,65},{34,2},{66,34},{98,6... | collective-permute-start | bytes 393224 | tf_op jit(solution)/shard_map/ppermute | solution.py:361
  34.1 5.3 %project_c.1.c0 = bf16[128,512]{1,0:T(8,128)(2,1)} custom-call(bf16[128,8192]{1,0:T(8,128)(2,1)} %h_ref.3, bf16[8192,512]{1,0:T(8,128)(2,1)} %w_ref.3), custom_call_target="tpu_custom_call" | custom-call | tf_op jit(solution)/shard_map/project_c/pallas_call | solution.py:406
  39.4 1.3 %collective-permute-start.9 = (bf16[128,512]{1,0:T(8,128)(2,1)}, bf16[128,512]{1,0:T(8,128)(2,1)S(1)}, u32[]{:S(2)}, u32[]{:S(2)}) collective-permute-start(bf16[128,512]{1,0:T(8,128)(2,1)} %project_c.1.c0), channel_id=1, source_target_pairs={{96,0},{97,1},{98,2},{99,3},{100,4},{101,5},{102,6},{103,7},{104,8... | collective-permute-start | bytes 393224 | tf_op jit(solution)/shard_map/ppermute | solution.py:361
  40.7 1.6 %collective-permute-done.2.refs_4_ = bf16[128,512]{1,0:T(8,128)(2,1)S(1)} collective-permute-done((bf16[128,512]{1,0:T(8,128)(2,1)}, bf16[128,512]{1,0:T(8,128)(2,1)S(1)}, u32[]{:S(2)}, u32[]{:S(2)}) %collective-permute-start.2) | collective-permute-done | bytes 131104 | tf_op jit(solution)/shard_map/ppermute | solution.py:361
  42.3 1.3 %collective-permute-start.8 = (bf16[128,512]{1,0:T(8,128)(2,1)}, bf16[128,512]{1,0:T(8,128)(2,1)S(1)}, u32[]{:S(2)}, u32[]{:S(2)}) collective-permute-start(bf16[128,512]{1,0:T(8,128)(2,1)} %project_c.1.c0), channel_id=1, source_target_pairs={{64,0},{96,32},{65,1},{97,33},{66,2},{98,34},{67,3},{99,35},{68,4}... | collective-permute-start | bytes 393224 | tf_op jit(solution)/shard_map/ppermute | solution.py:361
  43.6 0.0 collective-permute-done.1.refs_3_
  43.6 1.3 %collective-permute-start.7 = (bf16[128,512]{1,0:T(8,128)(2,1)}, bf16[128,512]{1,0:T(8,128)(2,1)S(1)}, u32[]{:S(2)}, u32[]{:S(2)}) collective-permute-start(bf16[128,512]{1,0:T(8,128)(2,1)} %project_c.1.c0), channel_id=1, source_target_pairs={{32,0},{64,32},{96,64},{33,1},{65,33},{97,65},{34,2},{66,34},{98,6... | collective-permute-start | bytes 393224 | tf_op jit(solution)/shard_map/ppermute | solution.py:361
  44.9 0.0 collective-permute-done.refs_2_
  44.9 0.0 copy-done
  44.9 4.0 %shard_map.68 = (bf16[4,2048,512]{2,1,0:T(8,128)(2,1)S(1)}, f32[4,1,512]{2,1,0:T(1,128)S(1)}, f32[4,2,512]{2,1,0:T(2,128)S(1)}) custom-call(bf16[16,256,128]{2,1,0:T(8,128)(2,1)S(1)} %all_to_all.5.refs_0_.bm_ref, bf16[128,512]{1,0:T(8,128)(2,1)S(1)} %copy-done, bf16[128,512]{1,0:T(8,128)(2,1)S(1)} %collective-permute-done.refs_2_, ...), custom_call_target="tpu_custom_call" | custom-call | tf_op jit(solution)/shard_map/pallas_call | solution.py:420
  48.9 0.0 collective-permute-done.3.refs_0_.bo_ref
  48.9 4.2 %shard_map.69 = (bf16[4,2048,512]{2,1,0:T(8,128)(2,1)S(1)}, f32[4,1,512]{2,1,0:T(1,128)S(1)}, f32[4,2,512]{2,1,0:T(2,128)S(1)}) custom-call(bf16[16,256,128]{2,1,0:T(8,128)(2,1)S(1)} %collective-permute-done.3.refs_0_.bo_ref, bf16[128,512]{1,0:T(8,128)(2,1)S(1)} %copy-done, bf16[128,512]{1,0:T(8,128)(2,1)S(1)} %collective-permute-done.refs_2_, ...), custom_call_target="tpu_custom_call" | custom-call | tf_op jit(solution)/shard_map/pallas_call | solution.py:420
  53.1 0.1 collective-permute-start.6
  53.2 2.8 %collective-permute-start.5 = (f32[4,2,512]{2,1,0:T(2,128)S(1)}, f32[4,2,512]{2,1,0:T(2,128)S(1)}, u32[]{:S(2)}, u32[]{:S(2)}) collective-permute-start(f32[4,2,512]{2,1,0:T(2,128)S(1)} %get-tuple-element.29.t0), channel_id=1, source_target_pairs={{0,64},{32,96},{64,0},{96,32},{1,65},{33,97},{65,1},{97,33},{2,66}... | collective-permute-start | bytes 49160 | tf_op jit(solution)/shard_map/ppermute | solution.py:369
  56.0 0.0 collective-permute-done.9.c3
  56.0 0.0 collective-permute-start.4
  56.0 0.0 collective-permute-done.8.c2
  56.0 0.0 collective-permute-done.7.c1
  56.0 0.0 copy-start.1
  56.0 0.9 copy-done.1
  56.9 2.9 %shard_map.70 = (bf16[4,128,512]{2,1,0:T(8,128)(2,1)S(1)}, bf16[2,128,2048]{2,1,0:T(8,128)(2,1)S(1)}, f32[4,128,512]{2,1,0:T(8,128)S(1)}, f32[2,2048,128]{2,1,0:T(8,128)S(1)}) custom-call(bf16[16,256,128]{2,1,0:T(8,128)(2,1)S(1)} %all_to_all.5.refs_0_.bm_ref, bf16[16,256,128]{2,1,0:T(8,128)(2,1)S(1)} %collective-permute-done.3.refs_0_.bo_ref, ...), custom_call_target="tpu_custom_call" | custom-call | tf_op jit(solution)/shard_map/pallas_call | solution.py:420
  59.8 0.0 collective-permute-done.6.t3
  59.8 0.0 collective-permute-done.5.t2
  59.8 1.1 %collective-permute-done.4.t1 = f32[4,2,512]{2,1,0:T(2,128)S(1)} collective-permute-done((f32[4,2,512]{2,1,0:T(2,128)S(1)}, f32[4,2,512]{2,1,0:T(2,128)S(1)}, u32[]{:S(2)}, u32[]{:S(2)}) %collective-permute-start.4) | collective-permute-done | bytes 16416 | tf_op jit(solution)/shard_map/ppermute | solution.py:369
  60.9 2.9 %shard_map.73 = bf16[2048,128]{1,0:T(8,128)(2,1)S(1)} custom-call(bf16[4,2048,512]{2,1,0:T(8,128)(2,1)S(1)} %get-tuple-element.26.po_ref.p_ref, f32[4,1,512]{2,1,0:T(1,128)S(1)} %get-tuple-element.28.lo_ref.level_ref, f32[4,2,512]{2,1,0:T(2,128)S(1)} %get-tuple-element.29.t0, f32[4,2,512]{2,1,0:T(2,128)S(1)} %collective-permute-done.4.t1, ...), custom_call_target="tpu_custom_call" | custom-call | tf_op jit(solution)/shard_map/pallas_call | solution.py:420
  63.8 0.1 collective-permute-start.13
  63.9 1.9 %collective-permute-done.13.refs_0_ = bf16[2048,128]{1,0:T(8,128)(2,1)S(1)} collective-permute-done((bf16[2048,128]{1,0:T(8,128)(2,1)S(1)}, bf16[2048,128]{1,0:T(8,128)(2,1)S(1)}, u32[]{:S(2)}, u32[]{:S(2)}) %collective-permute-start.13) | collective-permute-done | bytes 524320 | tf_op jit(solution)/shard_map/ppermute | solution.py:382
  65.8 2.9 %shard_map.74 = (f32[4,128,128]{2,1,0:T(8,128)S(1)}, bf16[4,128,128]{2,1,0:T(8,128)(2,1)S(1)}, bf16[4,128,128]{2,1,0:T(8,128)(2,1)S(1)}, bf16[4,128,128]{2,1,0:T(8,128)(2,1)S(1)}) custom-call(bf16[4,2048,512]{2,1,0:T(8,128)(2,1)S(1)} %get-tuple-element.24.pm_ref.p_ref, f32[4,1,512]{2,1,0:T(1,128)S(1)} %get-tuple-element.27.lm_ref.level_ref, ...), custom_call_target="tpu_custom_call" | custom-call | tf_op jit(solution)/shard_map/pallas_call | solution.py:420
  68.7 0.6 collective-permute-start.14
  69.3 2.3 %collective-permute-start.15 = (bf16[4,128,128]{2,1,0:T(8,128)(2,1)S(1)}, bf16[4,128,128]{2,1,0:T(8,128)(2,1)S(1)}, u32[]{:S(2)}, u32[]{:S(2)}) collective-permute-start(bf16[4,128,128]{2,1,0:T(8,128)(2,1)S(1)} %get-tuple-element.40), channel_id=1, source_target_pairs={{0,8},{4,12},{8,0},{12,4},{1,9},{5,13},{9,1},{13,5},{2,10},{6,14},... | collective-permute-start | bytes 393224 | tf_op jit(solution)/shard_map/ppermute | solution.py:373
  71.6 1.6 %collective-permute-start.16 = (bf16[4,128,128]{2,1,0:T(8,128)(2,1)S(1)}, bf16[4,128,128]{2,1,0:T(8,128)(2,1)S(1)}, u32[]{:S(2)}, u32[]{:S(2)}) collective-permute-start(bf16[4,128,128]{2,1,0:T(8,128)(2,1)S(1)} %get-tuple-element.41), channel_id=1, source_target_pairs={{0,12},{4,0},{8,4},{12,8},{1,13},{5,1},{9,5},{13,9},{2,14},{6,2},{... | collective-permute-start | bytes 393224 | tf_op jit(solution)/shard_map/ppermute | solution.py:373
  73.2 1.7 %shard_map.72 = (bf16[128,512]{1,0:T(8,128)(2,1)S(1)}, bf16[128,512]{1,0:T(8,128)(2,1)S(1)}) custom-call(bf16[4,2048,512]{2,1,0:T(8,128)(2,1)S(1)} %get-tuple-element.24.pm_ref.p_ref, bf16[4,2048,512]{2,1,0:T(8,128)(2,1)S(1)} %get-tuple-element.26.po_ref.p_ref, f32[4,1,512]{2,1,0:T(1,128)S(1)} %get-tuple-element.27.lm_ref.level_ref, ...), custom_call_target="tpu_custom_call" | custom-call | tf_op jit(solution)/shard_map/pallas_call | solution.py:420
  74.9 1.3 %collective-permute-start.11 = (bf16[128,512]{1,0:T(8,128)(2,1)S(1)}, bf16[128,512]{1,0:T(8,128)(2,1)S(1)}, u32[]{:S(2)}, u32[]{:S(2)}) collective-permute-start(bf16[128,512]{1,0:T(8,128)(2,1)S(1)} %get-tuple-element.34), channel_id=1, source_target_pairs={{0,64},{32,96},{1,65},{33,97},{2,66},{34,98},{3,67},{35,99},{4,68}... | collective-permute-start | bytes 393224 | tf_op jit(solution)/shard_map/ppermute | solution.py:365
  76.2 1.3 %collective-permute-start.12 = (bf16[128,512]{1,0:T(8,128)(2,1)S(1)}, bf16[128,512]{1,0:T(8,128)(2,1)S(1)}, u32[]{:S(2)}, u32[]{:S(2)}) collective-permute-start(bf16[128,512]{1,0:T(8,128)(2,1)S(1)} %get-tuple-element.35), channel_id=1, source_target_pairs={{0,96},{1,97},{2,98},{3,99},{4,100},{5,101},{6,102},{7,103},{8,104... | collective-permute-start | bytes 393224 | tf_op jit(solution)/shard_map/ppermute | solution.py:365
  77.5 1.5 %shard_map.71 = (f32[128,512]{1,0:T(8,128)S(1)}, bf16[128,512]{1,0:T(8,128)(2,1)S(1)}) custom-call(bf16[4,2048,512]{2,1,0:T(8,128)(2,1)S(1)} %get-tuple-element.24.pm_ref.p_ref, bf16[4,2048,512]{2,1,0:T(8,128)(2,1)S(1)} %get-tuple-element.26.po_ref.p_ref, f32[4,1,512]{2,1,0:T(1,128)S(1)} %get-tuple-element.27.lm_ref.level_ref, ...), custom_call_target="tpu_custom_call" | custom-call | tf_op jit(solution)/shard_map/pallas_call | solution.py:420
  79.0 0.0 collective-permute-done.14.r1
  79.0 1.3 %collective-permute-start.10 = (bf16[128,512]{1,0:T(8,128)(2,1)S(1)}, bf16[128,512]{1,0:T(8,128)(2,1)S(1)}, u32[]{:S(2)}, u32[]{:S(2)}) collective-permute-start(bf16[128,512]{1,0:T(8,128)(2,1)S(1)} %get-tuple-element.33), channel_id=1, source_target_pairs={{0,32},{32,64},{64,96},{1,33},{33,65},{65,97},{2,34},{34,66},{66,9... | collective-permute-start | bytes 393224 | tf_op jit(solution)/shard_map/ppermute | solution.py:365
  80.3 0.0 collective-permute-done.15.r2
  80.3 0.0 collective-permute-done.16.r3
  80.3 0.1 shard_map.75
  80.4 2.8 %collective-permute-start.17 = (bf16[128,128]{1,0:T(8,128)(2,1)S(1)}, bf16[128,128]{1,0:T(8,128)(2,1)S(1)}, u32[]{:S(2)}, u32[]{:S(2)}) collective-permute-start(bf16[128,128]{1,0:T(8,128)(2,1)S(1)} %get-tuple-element.43), channel_id=1, source_target_pairs={{0,16},{16,2},{2,18},{18,0},{1,17},{17,3},{3,19},{19,1},{4,20},{20... | collective-permute-start | bytes 98312 | tf_op jit(solution)/shard_map/ppermute | solution.py:378
  83.3 5.0 %collective-permute-start.18 = (bf16[128,128]{1,0:T(8,128)(2,1)S(1)}, bf16[128,128]{1,0:T(8,128)(2,1)S(1)}, u32[]{:S(2)}, u32[]{:S(2)}) collective-permute-start(bf16[128,128]{1,0:T(8,128)(2,1)S(1)} %get-tuple-element.44), channel_id=1, source_target_pairs={{0,2},{16,18},{2,0},{18,16},{1,3},{17,19},{3,1},{19,17},{4,6},{20,... | collective-permute-start | bytes 98312 | tf_op jit(solution)/shard_map/ppermute | solution.py:378
  88.3 0.0 collective-permute-done.11
  88.3 0.0 collective-permute-start.19
  88.3 0.0 collective-permute-done.12
  88.3 0.0 collective-permute-done.10
  88.3 0.7 add_convert_fusion
  89.0 0.0 collective-permute-done.17
  89.0 1.5 %collective-permute-done.18 = bf16[128,128]{1,0:T(8,128)(2,1)S(1)} collective-permute-done((bf16[128,128]{1,0:T(8,128)(2,1)S(1)}, bf16[128,128]{1,0:T(8,128)(2,1)S(1)}, u32[]{:S(2)}, u32[]{:S(2)}) %collective-permute-start.18) | collective-permute-done | bytes 32800 | tf_op jit(solution)/shard_map/ppermute | solution.py:378
  90.5 1.7 %collective-permute-done.19 = bf16[128,128]{1,0:T(8,128)(2,1)S(1)} collective-permute-done((bf16[128,128]{1,0:T(8,128)(2,1)S(1)}, bf16[128,128]{1,0:T(8,128)(2,1)S(1)}, u32[]{:S(2)}, u32[]{:S(2)}) %collective-permute-start.19) | collective-permute-done | bytes 32800 | tf_op jit(solution)/shard_map/ppermute | solution.py:378
  92.2 0.6 add_convert_fusion.1
Async XLA Ops:
  0.6 44.2 %copy-start = (bf16[128,512]{1,0:T(8,128)(2,1)S(1)}, bf16[128,512]{1,0:T(8,128)(2,1)}, u32[]{:S(2)}) copy-start(bf16[128,512]{1,0:T(8,128)(2,1)} %refs_1_.3) | copy-start | bytes 393220
  30.2 18.7 %collective-permute-start.3 = (bf16[16,256,128]{2,1,0:T(8,128)(2,1)S(1)}, bf16[16,256,128]{2,1,0:T(8,128)(2,1)S(1)}, u32[]{:S(2)}, u32[]{:S(2)}) collective-permute-start(bf16[16,256,128]{2,1,0:T(8,128)(2,1)S(1)} %all_to_all.5.refs_0_.bm_ref), channel_id=1, source_target_pairs={{0,1},{1,0},{2,3},{3,2},{4,5},{5,4},{6,7},{7,6},{8,9},{9,8},{10,11... | collective-permute-start | bytes 3145736 | tf_op jit(solution)/shard_map/ppermute | solution.py:382
  30.2 12.0 %collective-permute-start.2 = (bf16[128,512]{1,0:T(8,128)(2,1)}, bf16[128,512]{1,0:T(8,128)(2,1)S(1)}, u32[]{:S(2)}, u32[]{:S(2)}) collective-permute-start(bf16[128,512]{1,0:T(8,128)(2,1)} %refs_1_.3), channel_id=1, source_target_pairs={{96,0},{97,1},{98,2},{99,3},{100,4},{101,5},{102,6},{103,7},{104,8... | collective-permute-start | bytes 393224 | tf_op jit(solution)/shard_map/ppermute | solution.py:361
  31.5 12.0 %collective-permute-start.1 = (bf16[128,512]{1,0:T(8,128)(2,1)}, bf16[128,512]{1,0:T(8,128)(2,1)S(1)}, u32[]{:S(2)}, u32[]{:S(2)}) collective-permute-start(bf16[128,512]{1,0:T(8,128)(2,1)} %refs_1_.3), channel_id=1, source_target_pairs={{64,0},{96,32},{65,1},{97,33},{66,2},{98,34},{67,3},{99,35},{68,4}... | collective-permute-start | bytes 393224 | tf_op jit(solution)/shard_map/ppermute | solution.py:361
  32.8 12.0 %collective-permute-start = (bf16[128,512]{1,0:T(8,128)(2,1)}, bf16[128,512]{1,0:T(8,128)(2,1)S(1)}, u32[]{:S(2)}, u32[]{:S(2)}) collective-permute-start(bf16[128,512]{1,0:T(8,128)(2,1)} %refs_1_.3), channel_id=1, source_target_pairs={{32,0},{64,32},{96,64},{33,1},{65,33},{97,65},{34,2},{66,34},{98,6... | collective-permute-start | bytes 393224 | tf_op jit(solution)/shard_map/ppermute | solution.py:361
  39.4 16.6 %collective-permute-start.9 = (bf16[128,512]{1,0:T(8,128)(2,1)}, bf16[128,512]{1,0:T(8,128)(2,1)S(1)}, u32[]{:S(2)}, u32[]{:S(2)}) collective-permute-start(bf16[128,512]{1,0:T(8,128)(2,1)} %project_c.1.c0), channel_id=1, source_target_pairs={{96,0},{97,1},{98,2},{99,3},{100,4},{101,5},{102,6},{103,7},{104,8... | collective-permute-start | bytes 393224 | tf_op jit(solution)/shard_map/ppermute | solution.py:361
  42.3 13.7 %collective-permute-start.8 = (bf16[128,512]{1,0:T(8,128)(2,1)}, bf16[128,512]{1,0:T(8,128)(2,1)S(1)}, u32[]{:S(2)}, u32[]{:S(2)}) collective-permute-start(bf16[128,512]{1,0:T(8,128)(2,1)} %project_c.1.c0), channel_id=1, source_target_pairs={{64,0},{96,32},{65,1},{97,33},{66,2},{98,34},{67,3},{99,35},{68,4}... | collective-permute-start | bytes 393224 | tf_op jit(solution)/shard_map/ppermute | solution.py:361
  43.6 12.4 %collective-permute-start.7 = (bf16[128,512]{1,0:T(8,128)(2,1)}, bf16[128,512]{1,0:T(8,128)(2,1)S(1)}, u32[]{:S(2)}, u32[]{:S(2)}) collective-permute-start(bf16[128,512]{1,0:T(8,128)(2,1)} %project_c.1.c0), channel_id=1, source_target_pairs={{32,0},{64,32},{96,64},{33,1},{65,33},{97,65},{34,2},{66,34},{98,6... | collective-permute-start | bytes 393224 | tf_op jit(solution)/shard_map/ppermute | solution.py:361
  53.1 6.7 %collective-permute-start.6 = (f32[4,2,512]{2,1,0:T(2,128)S(1)}, f32[4,2,512]{2,1,0:T(2,128)S(1)}, u32[]{:S(2)}, u32[]{:S(2)}) collective-permute-start(f32[4,2,512]{2,1,0:T(2,128)S(1)} %get-tuple-element.29.t0), channel_id=1, source_target_pairs={{0,96},{32,0},{64,32},{96,64},{1,97},{33,1},{65,33},{97,65},{2,98}... | collective-permute-start | bytes 49160 | tf_op jit(solution)/shard_map/ppermute | solution.py:369
  53.2 6.7 %collective-permute-start.5 = (f32[4,2,512]{2,1,0:T(2,128)S(1)}, f32[4,2,512]{2,1,0:T(2,128)S(1)}, u32[]{:S(2)}, u32[]{:S(2)}) collective-permute-start(f32[4,2,512]{2,1,0:T(2,128)S(1)} %get-tuple-element.29.t0), channel_id=1, source_target_pairs={{0,64},{32,96},{64,0},{96,32},{1,65},{33,97},{65,1},{97,33},{2,66}... | collective-permute-start | bytes 49160 | tf_op jit(solution)/shard_map/ppermute | solution.py:369
  56.0 5.0 %collective-permute-start.4 = (f32[4,2,512]{2,1,0:T(2,128)S(1)}, f32[4,2,512]{2,1,0:T(2,128)S(1)}, u32[]{:S(2)}, u32[]{:S(2)}) collective-permute-start(f32[4,2,512]{2,1,0:T(2,128)S(1)} %get-tuple-element.29.t0), channel_id=1, source_target_pairs={{0,32},{32,64},{64,96},{96,0},{1,33},{33,65},{65,97},{97,1},{2,34}... | collective-permute-start | bytes 49160 | tf_op jit(solution)/shard_map/ppermute | solution.py:369
  56.0 0.9 copy-start.1
  63.8 2.0 %collective-permute-start.13 = (bf16[2048,128]{1,0:T(8,128)(2,1)S(1)}, bf16[2048,128]{1,0:T(8,128)(2,1)S(1)}, u32[]{:S(2)}, u32[]{:S(2)}) collective-permute-start(bf16[2048,128]{1,0:T(8,128)(2,1)S(1)} %shard_map.73), channel_id=1, source_target_pairs={{0,1},{1,0},{2,3},{3,2},{4,5},{5,4},{6,7},{7,6},{8,9},{9,8},{10,11... | collective-permute-start | bytes 1572872 | tf_op jit(solution)/shard_map/ppermute | solution.py:382
  68.7 10.3 %collective-permute-start.14 = (bf16[4,128,128]{2,1,0:T(8,128)(2,1)S(1)}, bf16[4,128,128]{2,1,0:T(8,128)(2,1)S(1)}, u32[]{:S(2)}, u32[]{:S(2)}) collective-permute-start(bf16[4,128,128]{2,1,0:T(8,128)(2,1)S(1)} %get-tuple-element.39), channel_id=1, source_target_pairs={{0,4},{4,8},{8,12},{12,0},{1,5},{5,9},{9,13},{13,1},{2,6},{6,10},{... | collective-permute-start | bytes 393224 | tf_op jit(solution)/shard_map/ppermute | solution.py:373
  69.3 11.0 %collective-permute-start.15 = (bf16[4,128,128]{2,1,0:T(8,128)(2,1)S(1)}, bf16[4,128,128]{2,1,0:T(8,128)(2,1)S(1)}, u32[]{:S(2)}, u32[]{:S(2)}) collective-permute-start(bf16[4,128,128]{2,1,0:T(8,128)(2,1)S(1)} %get-tuple-element.40), channel_id=1, source_target_pairs={{0,8},{4,12},{8,0},{12,4},{1,9},{5,13},{9,1},{13,5},{2,10},{6,14},... | collective-permute-start | bytes 393224 | tf_op jit(solution)/shard_map/ppermute | solution.py:373
  71.6 8.7 %collective-permute-start.16 = (bf16[4,128,128]{2,1,0:T(8,128)(2,1)S(1)}, bf16[4,128,128]{2,1,0:T(8,128)(2,1)S(1)}, u32[]{:S(2)}, u32[]{:S(2)}) collective-permute-start(bf16[4,128,128]{2,1,0:T(8,128)(2,1)S(1)} %get-tuple-element.41), channel_id=1, source_target_pairs={{0,12},{4,0},{8,4},{12,8},{1,13},{5,1},{9,5},{13,9},{2,14},{6,2},{... | collective-permute-start | bytes 393224 | tf_op jit(solution)/shard_map/ppermute | solution.py:373
  74.9 13.4 %collective-permute-start.11 = (bf16[128,512]{1,0:T(8,128)(2,1)S(1)}, bf16[128,512]{1,0:T(8,128)(2,1)S(1)}, u32[]{:S(2)}, u32[]{:S(2)}) collective-permute-start(bf16[128,512]{1,0:T(8,128)(2,1)S(1)} %get-tuple-element.34), channel_id=1, source_target_pairs={{0,64},{32,96},{1,65},{33,97},{2,66},{34,98},{3,67},{35,99},{4,68}... | collective-permute-start | bytes 393224 | tf_op jit(solution)/shard_map/ppermute | solution.py:365
  76.2 12.1 %collective-permute-start.12 = (bf16[128,512]{1,0:T(8,128)(2,1)S(1)}, bf16[128,512]{1,0:T(8,128)(2,1)S(1)}, u32[]{:S(2)}, u32[]{:S(2)}) collective-permute-start(bf16[128,512]{1,0:T(8,128)(2,1)S(1)} %get-tuple-element.35), channel_id=1, source_target_pairs={{0,96},{1,97},{2,98},{3,99},{4,100},{5,101},{6,102},{7,103},{8,104... | collective-permute-start | bytes 393224 | tf_op jit(solution)/shard_map/ppermute | solution.py:365
  79.0 9.3 %collective-permute-start.10 = (bf16[128,512]{1,0:T(8,128)(2,1)S(1)}, bf16[128,512]{1,0:T(8,128)(2,1)S(1)}, u32[]{:S(2)}, u32[]{:S(2)}) collective-permute-start(bf16[128,512]{1,0:T(8,128)(2,1)S(1)} %get-tuple-element.33), channel_id=1, source_target_pairs={{0,32},{32,64},{64,96},{1,33},{33,65},{65,97},{2,34},{34,66},{66,9... | collective-permute-start | bytes 393224 | tf_op jit(solution)/shard_map/ppermute | solution.py:365
  80.4 8.6 %collective-permute-start.17 = (bf16[128,128]{1,0:T(8,128)(2,1)S(1)}, bf16[128,128]{1,0:T(8,128)(2,1)S(1)}, u32[]{:S(2)}, u32[]{:S(2)}) collective-permute-start(bf16[128,128]{1,0:T(8,128)(2,1)S(1)} %get-tuple-element.43), channel_id=1, source_target_pairs={{0,16},{16,2},{2,18},{18,0},{1,17},{17,3},{3,19},{19,1},{4,20},{20... | collective-permute-start | bytes 98312 | tf_op jit(solution)/shard_map/ppermute | solution.py:378
  83.3 7.3 %collective-permute-start.18 = (bf16[128,128]{1,0:T(8,128)(2,1)S(1)}, bf16[128,128]{1,0:T(8,128)(2,1)S(1)}, u32[]{:S(2)}, u32[]{:S(2)}) collective-permute-start(bf16[128,128]{1,0:T(8,128)(2,1)S(1)} %get-tuple-element.44), channel_id=1, source_target_pairs={{0,2},{16,18},{2,0},{18,16},{1,3},{17,19},{3,1},{19,17},{4,6},{20,... | collective-permute-start | bytes 98312 | tf_op jit(solution)/shard_map/ppermute | solution.py:378
  88.3 3.9 %collective-permute-start.19 = (bf16[128,128]{1,0:T(8,128)(2,1)S(1)}, bf16[128,128]{1,0:T(8,128)(2,1)S(1)}, u32[]{:S(2)}, u32[]{:S(2)}) collective-permute-start(bf16[128,128]{1,0:T(8,128)(2,1)S(1)} %get-tuple-element.45), channel_id=1, source_target_pairs={{0,18},{16,0},{2,16},{18,2},{1,19},{17,1},{3,17},{19,3},{4,22},{20... | collective-permute-start | bytes 98312 | tf_op jit(solution)/shard_map/ppermute | solution.py:378

commit v4 on v3

--- a/solution.py
+++ b/solution.py
@@ -410,7 +410,7 @@
         out_specs=vmem,
         scratch_shapes=[pltpu.VMEM(hidden_states.shape, bf16), pltpu.VMEM(w_c.shape, bf16),
                         pltpu.SemaphoreType.DMA((2 * DEPTH,))],
-        compiler_params=pltpu.CompilerParams(vmem_limit_bytes=58 * 1024 * 1024),
+        compiler_params=pltpu.CompilerParams(vmem_limit_bytes=52 * 1024 * 1024),
         name="project_c",
     )(hidden_states, w_c)
     crows = [c_proj] + [down(c_proj, k) for k in (1, 2, 3)]
@@ -456,7 +456,8 @@
     o3, o2 = call(functools.partial(row_sums_kernel, True), row_ins, (part, part), row_room)
     o0, o1 = call(functools.partial(row_sums_kernel, False), row_ins,
                   (shaped((TOK, ROWS), full), part), row_room)
-    given = [up(o, k) for k, o in enumerate((o1, o2, o3), 1)]
+    given = [up(o, k) for k, o in ((2, o2), (3, o3))]
+    given.append(up(o1, 1))
     sent = shaped((TOK, HEAD), half)
     h0, *h_sent = call(join_x_kernel, (g0, *g_near), (shaped((TOK, HEAD), full), sent, sent, sent),
                        [((RING, TOK, HEAD), full)])

time: 93.2 us -> 93.1 us (level)
  waiting for transfers between devices: 7.75 us -> 9.31 us
  transfers between devices with their start and end apart: 20 -> 20, of which waited for: 5 -> 5; matrix products, arithmetic and copies ran while one was open for 1% -> 1% of each run, Pallas kernels for 21% -> 20%
where the time goes in v4:
time: 93.1 us; the launch traced here: 92.8 us
  Pallas kernels  29.2 us (31%)
  starting transfers between devices  26.9 us (29%)
  blocking collectives  25.1 us (27%)
  waiting for transfers between devices  9.31 us (10%)
  other arithmetic  1.35 us (1%)
    all_to_all x1, blocking collectives, exchange(): return lax.all_to_all(value, PLANE, 0, 0, tiled=True)  25.1 us
    pallas_call x8, Pallas kernels, call(): pl.pallas_call(kernel, out_shape=outs, in_specs=[vmem] * len(ins), out_sp...  20.1 us
    ppermute x3, starting transfers between devices, along_z(): lax.ppermute(value, ('zl', 'zh'), [(index[z], index[(z + k) % RING]) for...  7.8 us
    ppermute x6, starting transfers between devices, down(): return lax.ppermute(value, 'y', [(s, s - k) for s in range(k, RING)])  7.73 us
    pallas_call x1, Pallas kernels, on_device(): pl.pallas_call(project_c_kernel, out_shape=shaped((TOK, ROWS), bf16), in_...  4.62 us
    ppermute x3, starting transfers between devices, along_x(): return lax.ppermute(value, 'x', [(s, (s + k) % RING) for s in range(RING)])  4.56 us
    pallas_call x1, Pallas kernels, on_device(): pl.pallas_call(project_b_kernel, out_shape=shaped((PLANE_N, 2 * TOK, HEAD...  4.54 us
    ppermute x3, starting transfers between devices, up(): return lax.ppermute(value, 'y', [(s, s + k) for s in range(RING - k)])  3.89 us
  transfers between devices with their start and end apart: 20, of which 5 were waited for; matrix products, arithmetic and copies ran while one was open for 1% of the time, Pallas kernels for 20%

profile of v4, /device:TPU:0, one launch (start us, length us, event | category | flops | bytes accessed | tf_op | source)
XLA Modules:
  0.0 92.8 jit_solution(17321033877689589650)
XLA Ops:
  0.6 0.0 copy-start
  0.6 4.5 %project_b.1 = bf16[16,256,128]{2,1,0:T(8,128)(2,1)} custom-call(bf16[128,8192]{1,0:T(8,128)(2,1)} %h_ref.3, bf16[8192,128]{1,0:T(8,128)(2,1)} %w_ref.2, bf16[128,128]{1,0:T(8,128)(2,1)} %k_ref.1), custom_call_target="tpu_custom_call" | custom-call | tf_op jit(solution)/shard_map/project_b/pallas_call | solution.py:394
  5.2 25.1 %all_to_all.5.refs_0_.bm_ref = bf16[16,256,128]{2,1,0:T(8,128)(2,1)S(1)} all-to-all(bf16[16,256,128]{2,1,0:T(8,128)(2,1)} %project_b.1), channel_id=1, replica_groups=mesh['y'=4,'zl'=2,'x'=4,'zh'=2,'c'=2] {'zl','x','zh'}, dimensions={0} | all-to-all | bytes 2097152 | tf_op jit(solution)/shard_map/all_to_all | solution.py:386
  30.2 0.0 collective-permute-start.3
  30.2 1.3 %collective-permute-start.2 = (bf16[128,512]{1,0:T(8,128)(2,1)}, bf16[128,512]{1,0:T(8,128)(2,1)S(1)}, u32[]{:S(2)}, u32[]{:S(2)}) collective-permute-start(bf16[128,512]{1,0:T(8,128)(2,1)} %refs_1_.3), channel_id=1, source_target_pairs={{96,0},{97,1},{98,2},{99,3},{100,4},{101,5},{102,6},{103,7},{104,8... | collective-permute-start | bytes 393224 | tf_op jit(solution)/shard_map/ppermute | solution.py:361
  31.5 1.3 %collective-permute-start.1 = (bf16[128,512]{1,0:T(8,128)(2,1)}, bf16[128,512]{1,0:T(8,128)(2,1)S(1)}, u32[]{:S(2)}, u32[]{:S(2)}) collective-permute-start(bf16[128,512]{1,0:T(8,128)(2,1)} %refs_1_.3), channel_id=1, source_target_pairs={{64,0},{96,32},{65,1},{97,33},{66,2},{98,34},{67,3},{99,35},{68,4}... | collective-permute-start | bytes 393224 | tf_op jit(solution)/shard_map/ppermute | solution.py:361
  32.8 1.3 %collective-permute-start = (bf16[128,512]{1,0:T(8,128)(2,1)}, bf16[128,512]{1,0:T(8,128)(2,1)S(1)}, u32[]{:S(2)}, u32[]{:S(2)}) collective-permute-start(bf16[128,512]{1,0:T(8,128)(2,1)} %refs_1_.3), channel_id=1, source_target_pairs={{32,0},{64,32},{96,64},{33,1},{65,33},{97,65},{34,2},{66,34},{98,6... | collective-permute-start | bytes 393224 | tf_op jit(solution)/shard_map/ppermute | solution.py:361
  34.1 4.6 %project_c.1.c0 = bf16[128,512]{1,0:T(8,128)(2,1)S(1)} custom-call(bf16[128,8192]{1,0:T(8,128)(2,1)} %h_ref.3, bf16[8192,512]{1,0:T(8,128)(2,1)} %w_ref.3), custom_call_target="tpu_custom_call" | custom-call | tf_op jit(solution)/shard_map/project_c/pallas_call | solution.py:406
  38.8 1.3 %collective-permute-start.9 = (bf16[128,512]{1,0:T(8,128)(2,1)S(1)}, bf16[128,512]{1,0:T(8,128)(2,1)S(1)}, u32[]{:S(2)}, u32[]{:S(2)}) collective-permute-start(bf16[128,512]{1,0:T(8,128)(2,1)S(1)} %project_c.1.c0), channel_id=1, source_target_pairs={{96,0},{97,1},{98,2},{99,3},{100,4},{101,5},{102,6},{103,7},{104,8... | collective-permute-start | bytes 393224 | tf_op jit(solution)/shard_map/ppermute | solution.py:361
  40.1 2.2 %collective-permute-done.2.refs_4_ = bf16[128,512]{1,0:T(8,128)(2,1)S(1)} collective-permute-done((bf16[128,512]{1,0:T(8,128)(2,1)}, bf16[128,512]{1,0:T(8,128)(2,1)S(1)}, u32[]{:S(2)}, u32[]{:S(2)}) %collective-permute-start.2) | collective-permute-done | bytes 131104 | tf_op jit(solution)/shard_map/ppermute | solution.py:361
  42.3 1.3 %collective-permute-start.8 = (bf16[128,512]{1,0:T(8,128)(2,1)S(1)}, bf16[128,512]{1,0:T(8,128)(2,1)S(1)}, u32[]{:S(2)}, u32[]{:S(2)}) collective-permute-start(bf16[128,512]{1,0:T(8,128)(2,1)S(1)} %project_c.1.c0), channel_id=1, source_target_pairs={{64,0},{96,32},{65,1},{97,33},{66,2},{98,34},{67,3},{99,35},{68,4}... | collective-permute-start | bytes 393224 | tf_op jit(solution)/shard_map/ppermute | solution.py:361
  43.6 0.0 collective-permute-done.1.refs_3_
  43.6 1.3 %collective-permute-start.7 = (bf16[128,512]{1,0:T(8,128)(2,1)S(1)}, bf16[128,512]{1,0:T(8,128)(2,1)S(1)}, u32[]{:S(2)}, u32[]{:S(2)}) collective-permute-start(bf16[128,512]{1,0:T(8,128)(2,1)S(1)} %project_c.1.c0), channel_id=1, source_target_pairs={{32,0},{64,32},{96,64},{33,1},{65,33},{97,65},{34,2},{66,34},{98,6... | collective-permute-start | bytes 393224 | tf_op jit(solution)/shard_map/ppermute | solution.py:361
  44.9 0.0 collective-permute-done.refs_2_
  44.9 0.0 copy-done
  44.9 4.0 %shard_map.68 = (bf16[4,2048,512]{2,1,0:T(8,128)(2,1)S(1)}, f32[4,1,512]{2,1,0:T(1,128)S(1)}, f32[4,2,512]{2,1,0:T(2,128)S(1)}) custom-call(bf16[16,256,128]{2,1,0:T(8,128)(2,1)S(1)} %all_to_all.5.refs_0_.bm_ref, bf16[128,512]{1,0:T(8,128)(2,1)S(1)} %copy-done, bf16[128,512]{1,0:T(8,128)(2,1)S(1)} %collective-permute-done.refs_2_, ...), custom_call_target="tpu_custom_call" | custom-call | tf_op jit(solution)/shard_map/pallas_call | solution.py:420
  48.9 0.0 collective-permute-done.3.refs_0_.bo_ref
  48.9 4.2 %shard_map.69 = (bf16[4,2048,512]{2,1,0:T(8,128)(2,1)S(1)}, f32[4,1,512]{2,1,0:T(1,128)S(1)}, f32[4,2,512]{2,1,0:T(2,128)S(1)}) custom-call(bf16[16,256,128]{2,1,0:T(8,128)(2,1)S(1)} %collective-permute-done.3.refs_0_.bo_ref, bf16[128,512]{1,0:T(8,128)(2,1)S(1)} %copy-done, bf16[128,512]{1,0:T(8,128)(2,1)S(1)} %collective-permute-done.refs_2_, ...), custom_call_target="tpu_custom_call" | custom-call | tf_op jit(solution)/shard_map/pallas_call | solution.py:420
  53.1 0.1 collective-permute-start.6
  53.2 2.8 %collective-permute-start.5 = (f32[4,2,512]{2,1,0:T(2,128)S(1)}, f32[4,2,512]{2,1,0:T(2,128)S(1)}, u32[]{:S(2)}, u32[]{:S(2)}) collective-permute-start(f32[4,2,512]{2,1,0:T(2,128)S(1)} %get-tuple-element.29.t0), channel_id=1, source_target_pairs={{0,64},{32,96},{64,0},{96,32},{1,65},{33,97},{65,1},{97,33},{2,66}... | collective-permute-start | bytes 49160 | tf_op jit(solution)/shard_map/ppermute | solution.py:369
  56.0 0.0 collective-permute-done.9.c3
  56.0 0.0 collective-permute-start.4
  56.0 0.0 collective-permute-done.8.c2
  56.0 0.0 collective-permute-done.7.c1
  56.0 2.9 %shard_map.70 = (bf16[4,128,512]{2,1,0:T(8,128)(2,1)S(1)}, bf16[2,128,2048]{2,1,0:T(8,128)(2,1)S(1)}, f32[4,128,512]{2,1,0:T(8,128)S(1)}, f32[2,2048,128]{2,1,0:T(8,128)S(1)}) custom-call(bf16[16,256,128]{2,1,0:T(8,128)(2,1)S(1)} %all_to_all.5.refs_0_.bm_ref, bf16[16,256,128]{2,1,0:T(8,128)(2,1)S(1)} %collective-permute-done.3.refs_0_.bo_ref, ...), custom_call_target="tpu_custom_call" | custom-call | tf_op jit(solution)/shard_map/pallas_call | solution.py:420
  58.9 0.0 collective-permute-done.6.t3
  58.9 0.0 collective-permute-done.5.t2
  58.9 2.0 %collective-permute-done.4.t1 = f32[4,2,512]{2,1,0:T(2,128)S(1)} collective-permute-done((f32[4,2,512]{2,1,0:T(2,128)S(1)}, f32[4,2,512]{2,1,0:T(2,128)S(1)}, u32[]{:S(2)}, u32[]{:S(2)}) %collective-permute-start.4) | collective-permute-done | bytes 16416 | tf_op jit(solution)/shard_map/ppermute | solution.py:369
  60.9 2.9 %shard_map.73 = bf16[2048,128]{1,0:T(8,128)(2,1)S(1)} custom-call(bf16[4,2048,512]{2,1,0:T(8,128)(2,1)S(1)} %get-tuple-element.26.po_ref.p_ref, f32[4,1,512]{2,1,0:T(1,128)S(1)} %get-tuple-element.28.lo_ref.level_ref, f32[4,2,512]{2,1,0:T(2,128)S(1)} %get-tuple-element.29.t0, f32[4,2,512]{2,1,0:T(2,128)S(1)} %collective-permute-done.4.t1, ...), custom_call_target="tpu_custom_call" | custom-call | tf_op jit(solution)/shard_map/pallas_call | solution.py:420
  63.8 0.1 collective-permute-start.13
  63.9 1.9 %collective-permute-done.13.refs_0_ = bf16[2048,128]{1,0:T(8,128)(2,1)S(1)} collective-permute-done((bf16[2048,128]{1,0:T(8,128)(2,1)S(1)}, bf16[2048,128]{1,0:T(8,128)(2,1)S(1)}, u32[]{:S(2)}, u32[]{:S(2)}) %collective-permute-start.13) | collective-permute-done | bytes 524320 | tf_op jit(solution)/shard_map/ppermute | solution.py:382
  65.8 2.9 %shard_map.74 = (f32[4,128,128]{2,1,0:T(8,128)S(1)}, bf16[4,128,128]{2,1,0:T(8,128)(2,1)S(1)}, bf16[4,128,128]{2,1,0:T(8,128)(2,1)S(1)}, bf16[4,128,128]{2,1,0:T(8,128)(2,1)S(1)}) custom-call(bf16[4,2048,512]{2,1,0:T(8,128)(2,1)S(1)} %get-tuple-element.24.pm_ref.p_ref, f32[4,1,512]{2,1,0:T(1,128)S(1)} %get-tuple-element.27.lm_ref.level_ref, ...), custom_call_target="tpu_custom_call" | custom-call | tf_op jit(solution)/shard_map/pallas_call | solution.py:420
  68.7 0.6 collective-permute-start.14
  69.3 2.3 %collective-permute-start.15 = (bf16[4,128,128]{2,1,0:T(8,128)(2,1)S(1)}, bf16[4,128,128]{2,1,0:T(8,128)(2,1)S(1)}, u32[]{:S(2)}, u32[]{:S(2)}) collective-permute-start(bf16[4,128,128]{2,1,0:T(8,128)(2,1)S(1)} %get-tuple-element.40), channel_id=1, source_target_pairs={{0,8},{4,12},{8,0},{12,4},{1,9},{5,13},{9,1},{13,5},{2,10},{6,14},... | collective-permute-start | bytes 393224 | tf_op jit(solution)/shard_map/ppermute | solution.py:373
  71.6 1.6 %collective-permute-start.16 = (bf16[4,128,128]{2,1,0:T(8,128)(2,1)S(1)}, bf16[4,128,128]{2,1,0:T(8,128)(2,1)S(1)}, u32[]{:S(2)}, u32[]{:S(2)}) collective-permute-start(bf16[4,128,128]{2,1,0:T(8,128)(2,1)S(1)} %get-tuple-element.41), channel_id=1, source_target_pairs={{0,12},{4,0},{8,4},{12,8},{1,13},{5,1},{9,5},{13,9},{2,14},{6,2},{... | collective-permute-start | bytes 393224 | tf_op jit(solution)/shard_map/ppermute | solution.py:373
  73.2 1.7 %shard_map.72 = (bf16[128,512]{1,0:T(8,128)(2,1)S(1)}, bf16[128,512]{1,0:T(8,128)(2,1)S(1)}) custom-call(bf16[4,2048,512]{2,1,0:T(8,128)(2,1)S(1)} %get-tuple-element.24.pm_ref.p_ref, bf16[4,2048,512]{2,1,0:T(8,128)(2,1)S(1)} %get-tuple-element.26.po_ref.p_ref, f32[4,1,512]{2,1,0:T(1,128)S(1)} %get-tuple-element.27.lm_ref.level_ref, ...), custom_call_target="tpu_custom_call" | custom-call | tf_op jit(solution)/shard_map/pallas_call | solution.py:420
  74.9 1.3 %collective-permute-start.10 = (bf16[128,512]{1,0:T(8,128)(2,1)S(1)}, bf16[128,512]{1,0:T(8,128)(2,1)S(1)}, u32[]{:S(2)}, u32[]{:S(2)}) collective-permute-start(bf16[128,512]{1,0:T(8,128)(2,1)S(1)} %get-tuple-element.33), channel_id=1, source_target_pairs={{0,64},{32,96},{1,65},{33,97},{2,66},{34,98},{3,67},{35,99},{4,68}... | collective-permute-start | bytes 393224 | tf_op jit(solution)/shard_map/ppermute | solution.py:365
  76.2 1.3 %collective-permute-start.11 = (bf16[128,512]{1,0:T(8,128)(2,1)S(1)}, bf16[128,512]{1,0:T(8,128)(2,1)S(1)}, u32[]{:S(2)}, u32[]{:S(2)}) collective-permute-start(bf16[128,512]{1,0:T(8,128)(2,1)S(1)} %get-tuple-element.34), channel_id=1, source_target_pairs={{0,96},{1,97},{2,98},{3,99},{4,100},{5,101},{6,102},{7,103},{8,104... | collective-permute-start | bytes 393224 | tf_op jit(solution)/shard_map/ppermute | solution.py:365
  77.5 1.5 %shard_map.71 = (f32[128,512]{1,0:T(8,128)S(1)}, bf16[128,512]{1,0:T(8,128)(2,1)S(1)}) custom-call(bf16[4,2048,512]{2,1,0:T(8,128)(2,1)S(1)} %get-tuple-element.24.pm_ref.p_ref, bf16[4,2048,512]{2,1,0:T(8,128)(2,1)S(1)} %get-tuple-element.26.po_ref.p_ref, f32[4,1,512]{2,1,0:T(1,128)S(1)} %get-tuple-element.27.lm_ref.level_ref, ...), custom_call_target="tpu_custom_call" | custom-call | tf_op jit(solution)/shard_map/pallas_call | solution.py:420
  79.0 0.0 collective-permute-done.14.r1
  79.0 1.3 %collective-permute-start.12 = (bf16[128,512]{1,0:T(8,128)(2,1)S(1)}, bf16[128,512]{1,0:T(8,128)(2,1)S(1)}, u32[]{:S(2)}, u32[]{:S(2)}) collective-permute-start(bf16[128,512]{1,0:T(8,128)(2,1)S(1)} %get-tuple-element.35), channel_id=1, source_target_pairs={{0,32},{32,64},{64,96},{1,33},{33,65},{65,97},{2,34},{34,66},{66,9... | collective-permute-start | bytes 393224 | tf_op jit(solution)/shard_map/ppermute | solution.py:365
  80.3 0.0 collective-permute-done.15.r2
  80.3 0.0 collective-permute-done.16.r3
  80.3 0.1 shard_map.75
  80.4 2.9 %collective-permute-start.17 = (bf16[128,128]{1,0:T(8,128)(2,1)S(1)}, bf16[128,128]{1,0:T(8,128)(2,1)S(1)}, u32[]{:S(2)}, u32[]{:S(2)}) collective-permute-start(bf16[128,128]{1,0:T(8,128)(2,1)S(1)} %get-tuple-element.43), channel_id=1, source_target_pairs={{0,16},{16,2},{2,18},{18,0},{1,17},{17,3},{3,19},{19,1},{4,20},{20... | collective-permute-start | bytes 98312 | tf_op jit(solution)/shard_map/ppermute | solution.py:378
  83.3 4.9 %collective-permute-start.18 = (bf16[128,128]{1,0:T(8,128)(2,1)S(1)}, bf16[128,128]{1,0:T(8,128)(2,1)S(1)}, u32[]{:S(2)}, u32[]{:S(2)}) collective-permute-start(bf16[128,128]{1,0:T(8,128)(2,1)S(1)} %get-tuple-element.44), channel_id=1, source_target_pairs={{0,2},{16,18},{2,0},{18,16},{1,3},{17,19},{3,1},{19,17},{4,6},{20,... | collective-permute-start | bytes 98312 | tf_op jit(solution)/shard_map/ppermute | solution.py:378
  88.2 0.0 collective-permute-done.10
  88.2 0.0 collective-permute-start.19
  88.2 0.0 collective-permute-done.11
  88.2 0.0 collective-permute-done.12
  88.2 0.7 add_convert_fusion
  88.9 0.0 collective-permute-done.17
  89.0 1.5 %collective-permute-done.18 = bf16[128,128]{1,0:T(8,128)(2,1)S(1)} collective-permute-done((bf16[128,128]{1,0:T(8,128)(2,1)S(1)}, bf16[128,128]{1,0:T(8,128)(2,1)S(1)}, u32[]{:S(2)}, u32[]{:S(2)}) %collective-permute-start.18) | collective-permute-done | bytes 32800 | tf_op jit(solution)/shard_map/ppermute | solution.py:378
  90.4 1.7 %collective-permute-done.19 = bf16[128,128]{1,0:T(8,128)(2,1)S(1)} collective-permute-done((bf16[128,128]{1,0:T(8,128)(2,1)S(1)}, bf16[128,128]{1,0:T(8,128)(2,1)S(1)}, u32[]{:S(2)}, u32[]{:S(2)}) %collective-permute-start.19) | collective-permute-done | bytes 32800 | tf_op jit(solution)/shard_map/ppermute | solution.py:378
  92.1 0.6 add_convert_fusion.1
Async XLA Ops:
  0.6 44.2 %copy-start = (bf16[128,512]{1,0:T(8,128)(2,1)S(1)}, bf16[128,512]{1,0:T(8,128)(2,1)}, u32[]{:S(2)}) copy-start(bf16[128,512]{1,0:T(8,128)(2,1)} %refs_1_.3) | copy-start | bytes 393220
  30.2 18.7 %collective-permute-start.3 = (bf16[16,256,128]{2,1,0:T(8,128)(2,1)S(1)}, bf16[16,256,128]{2,1,0:T(8,128)(2,1)S(1)}, u32[]{:S(2)}, u32[]{:S(2)}) collective-permute-start(bf16[16,256,128]{2,1,0:T(8,128)(2,1)S(1)} %all_to_all.5.refs_0_.bm_ref), channel_id=1, source_target_pairs={{0,1},{1,0},{2,3},{3,2},{4,5},{5,4},{6,7},{7,6},{8,9},{9,8},{10,11... | collective-permute-start | bytes 3145736 | tf_op jit(solution)/shard_map/ppermute | solution.py:382
  30.2 12.0 %collective-permute-start.2 = (bf16[128,512]{1,0:T(8,128)(2,1)}, bf16[128,512]{1,0:T(8,128)(2,1)S(1)}, u32[]{:S(2)}, u32[]{:S(2)}) collective-permute-start(bf16[128,512]{1,0:T(8,128)(2,1)} %refs_1_.3), channel_id=1, source_target_pairs={{96,0},{97,1},{98,2},{99,3},{100,4},{101,5},{102,6},{103,7},{104,8... | collective-permute-start | bytes 393224 | tf_op jit(solution)/shard_map/ppermute | solution.py:361
  31.5 12.0 %collective-permute-start.1 = (bf16[128,512]{1,0:T(8,128)(2,1)}, bf16[128,512]{1,0:T(8,128)(2,1)S(1)}, u32[]{:S(2)}, u32[]{:S(2)}) collective-permute-start(bf16[128,512]{1,0:T(8,128)(2,1)} %refs_1_.3), channel_id=1, source_target_pairs={{64,0},{96,32},{65,1},{97,33},{66,2},{98,34},{67,3},{99,35},{68,4}... | collective-permute-start | bytes 393224 | tf_op jit(solution)/shard_map/ppermute | solution.py:361
  32.8 12.0 %collective-permute-start = (bf16[128,512]{1,0:T(8,128)(2,1)}, bf16[128,512]{1,0:T(8,128)(2,1)S(1)}, u32[]{:S(2)}, u32[]{:S(2)}) collective-permute-start(bf16[128,512]{1,0:T(8,128)(2,1)} %refs_1_.3), channel_id=1, source_target_pairs={{32,0},{64,32},{96,64},{33,1},{65,33},{97,65},{34,2},{66,34},{98,6... | collective-permute-start | bytes 393224 | tf_op jit(solution)/shard_map/ppermute | solution.py:361
  38.8 17.2 %collective-permute-start.9 = (bf16[128,512]{1,0:T(8,128)(2,1)S(1)}, bf16[128,512]{1,0:T(8,128)(2,1)S(1)}, u32[]{:S(2)}, u32[]{:S(2)}) collective-permute-start(bf16[128,512]{1,0:T(8,128)(2,1)S(1)} %project_c.1.c0), channel_id=1, source_target_pairs={{96,0},{97,1},{98,2},{99,3},{100,4},{101,5},{102,6},{103,7},{104,8... | collective-permute-start | bytes 393224 | tf_op jit(solution)/shard_map/ppermute | solution.py:361
  42.3 13.7 %collective-permute-start.8 = (bf16[128,512]{1,0:T(8,128)(2,1)S(1)}, bf16[128,512]{1,0:T(8,128)(2,1)S(1)}, u32[]{:S(2)}, u32[]{:S(2)}) collective-permute-start(bf16[128,512]{1,0:T(8,128)(2,1)S(1)} %project_c.1.c0), channel_id=1, source_target_pairs={{64,0},{96,32},{65,1},{97,33},{66,2},{98,34},{67,3},{99,35},{68,4}... | collective-permute-start | bytes 393224 | tf_op jit(solution)/shard_map/ppermute | solution.py:361
  43.6 12.4 %collective-permute-start.7 = (bf16[128,512]{1,0:T(8,128)(2,1)S(1)}, bf16[128,512]{1,0:T(8,128)(2,1)S(1)}, u32[]{:S(2)}, u32[]{:S(2)}) collective-permute-start(bf16[128,512]{1,0:T(8,128)(2,1)S(1)} %project_c.1.c0), channel_id=1, source_target_pairs={{32,0},{64,32},{96,64},{33,1},{65,33},{97,65},{34,2},{66,34},{98,6... | collective-permute-start | bytes 393224 | tf_op jit(solution)/shard_map/ppermute | solution.py:361
  53.1 5.8 %collective-permute-start.6 = (f32[4,2,512]{2,1,0:T(2,128)S(1)}, f32[4,2,512]{2,1,0:T(2,128)S(1)}, u32[]{:S(2)}, u32[]{:S(2)}) collective-permute-start(f32[4,2,512]{2,1,0:T(2,128)S(1)} %get-tuple-element.29.t0), channel_id=1, source_target_pairs={{0,96},{32,0},{64,32},{96,64},{1,97},{33,1},{65,33},{97,65},{2,98}... | collective-permute-start | bytes 49160 | tf_op jit(solution)/shard_map/ppermute | solution.py:369
  53.2 5.7 %collective-permute-start.5 = (f32[4,2,512]{2,1,0:T(2,128)S(1)}, f32[4,2,512]{2,1,0:T(2,128)S(1)}, u32[]{:S(2)}, u32[]{:S(2)}) collective-permute-start(f32[4,2,512]{2,1,0:T(2,128)S(1)} %get-tuple-element.29.t0), channel_id=1, source_target_pairs={{0,64},{32,96},{64,0},{96,32},{1,65},{33,97},{65,1},{97,33},{2,66}... | collective-permute-start | bytes 49160 | tf_op jit(solution)/shard_map/ppermute | solution.py:369
  56.0 5.0 %collective-permute-start.4 = (f32[4,2,512]{2,1,0:T(2,128)S(1)}, f32[4,2,512]{2,1,0:T(2,128)S(1)}, u32[]{:S(2)}, u32[]{:S(2)}) collective-permute-start(f32[4,2,512]{2,1,0:T(2,128)S(1)} %get-tuple-element.29.t0), channel_id=1, source_target_pairs={{0,32},{32,64},{64,96},{96,0},{1,33},{33,65},{65,97},{97,1},{2,34}... | collective-permute-start | bytes 49160 | tf_op jit(solution)/shard_map/ppermute | solution.py:369
  63.8 2.0 %collective-permute-start.13 = (bf16[2048,128]{1,0:T(8,128)(2,1)S(1)}, bf16[2048,128]{1,0:T(8,128)(2,1)S(1)}, u32[]{:S(2)}, u32[]{:S(2)}) collective-permute-start(bf16[2048,128]{1,0:T(8,128)(2,1)S(1)} %shard_map.73), channel_id=1, source_target_pairs={{0,1},{1,0},{2,3},{3,2},{4,5},{5,4},{6,7},{7,6},{8,9},{9,8},{10,11... | collective-permute-start | bytes 1572872 | tf_op jit(solution)/shard_map/ppermute | solution.py:382
  68.7 10.3 %collective-permute-start.14 = (bf16[4,128,128]{2,1,0:T(8,128)(2,1)S(1)}, bf16[4,128,128]{2,1,0:T(8,128)(2,1)S(1)}, u32[]{:S(2)}, u32[]{:S(2)}) collective-permute-start(bf16[4,128,128]{2,1,0:T(8,128)(2,1)S(1)} %get-tuple-element.39), channel_id=1, source_target_pairs={{0,4},{4,8},{8,12},{12,0},{1,5},{5,9},{9,13},{13,1},{2,6},{6,10},{... | collective-permute-start | bytes 393224 | tf_op jit(solution)/shard_map/ppermute | solution.py:373
  69.3 11.0 %collective-permute-start.15 = (bf16[4,128,128]{2,1,0:T(8,128)(2,1)S(1)}, bf16[4,128,128]{2,1,0:T(8,128)(2,1)S(1)}, u32[]{:S(2)}, u32[]{:S(2)}) collective-permute-start(bf16[4,128,128]{2,1,0:T(8,128)(2,1)S(1)} %get-tuple-element.40), channel_id=1, source_target_pairs={{0,8},{4,12},{8,0},{12,4},{1,9},{5,13},{9,1},{13,5},{2,10},{6,14},... | collective-permute-start | bytes 393224 | tf_op jit(solution)/shard_map/ppermute | solution.py:373
  71.6 8.7 %collective-permute-start.16 = (bf16[4,128,128]{2,1,0:T(8,128)(2,1)S(1)}, bf16[4,128,128]{2,1,0:T(8,128)(2,1)S(1)}, u32[]{:S(2)}, u32[]{:S(2)}) collective-permute-start(bf16[4,128,128]{2,1,0:T(8,128)(2,1)S(1)} %get-tuple-element.41), channel_id=1, source_target_pairs={{0,12},{4,0},{8,4},{12,8},{1,13},{5,1},{9,5},{13,9},{2,14},{6,2},{... | collective-permute-start | bytes 393224 | tf_op jit(solution)/shard_map/ppermute | solution.py:373
  74.9 13.3 %collective-permute-start.10 = (bf16[128,512]{1,0:T(8,128)(2,1)S(1)}, bf16[128,512]{1,0:T(8,128)(2,1)S(1)}, u32[]{:S(2)}, u32[]{:S(2)}) collective-permute-start(bf16[128,512]{1,0:T(8,128)(2,1)S(1)} %get-tuple-element.33), channel_id=1, source_target_pairs={{0,64},{32,96},{1,65},{33,97},{2,66},{34,98},{3,67},{35,99},{4,68}... | collective-permute-start | bytes 393224 | tf_op jit(solution)/shard_map/ppermute | solution.py:365
  76.2 12.0 %collective-permute-start.11 = (bf16[128,512]{1,0:T(8,128)(2,1)S(1)}, bf16[128,512]{1,0:T(8,128)(2,1)S(1)}, u32[]{:S(2)}, u32[]{:S(2)}) collective-permute-start(bf16[128,512]{1,0:T(8,128)(2,1)S(1)} %get-tuple-element.34), channel_id=1, source_target_pairs={{0,96},{1,97},{2,98},{3,99},{4,100},{5,101},{6,102},{7,103},{8,104... | collective-permute-start | bytes 393224 | tf_op jit(solution)/shard_map/ppermute | solution.py:365
  79.0 9.2 %collective-permute-start.12 = (bf16[128,512]{1,0:T(8,128)(2,1)S(1)}, bf16[128,512]{1,0:T(8,128)(2,1)S(1)}, u32[]{:S(2)}, u32[]{:S(2)}) collective-permute-start(bf16[128,512]{1,0:T(8,128)(2,1)S(1)} %get-tuple-element.35), channel_id=1, source_target_pairs={{0,32},{32,64},{64,96},{1,33},{33,65},{65,97},{2,34},{34,66},{66,9... | collective-permute-start | bytes 393224 | tf_op jit(solution)/shard_map/ppermute | solution.py:365
  80.4 8.5 %collective-permute-start.17 = (bf16[128,128]{1,0:T(8,128)(2,1)S(1)}, bf16[128,128]{1,0:T(8,128)(2,1)S(1)}, u32[]{:S(2)}, u32[]{:S(2)}) collective-permute-start(bf16[128,128]{1,0:T(8,128)(2,1)S(1)} %get-tuple-element.43), channel_id=1, source_target_pairs={{0,16},{16,2},{2,18},{18,0},{1,17},{17,3},{3,19},{19,1},{4,20},{20... | collective-permute-start | bytes 98312 | tf_op jit(solution)/shard_map/ppermute | solution.py:378
  83.3 7.2 %collective-permute-start.18 = (bf16[128,128]{1,0:T(8,128)(2,1)S(1)}, bf16[128,128]{1,0:T(8,128)(2,1)S(1)}, u32[]{:S(2)}, u32[]{:S(2)}) collective-permute-start(bf16[128,128]{1,0:T(8,128)(2,1)S(1)} %get-tuple-element.44), channel_id=1, source_target_pairs={{0,2},{16,18},{2,0},{18,16},{1,3},{17,19},{3,1},{19,17},{4,6},{20,... | collective-permute-start | bytes 98312 | tf_op jit(solution)/shard_map/ppermute | solution.py:378
  88.2 3.9 %collective-permute-start.19 = (bf16[128,128]{1,0:T(8,128)(2,1)S(1)}, bf16[128,128]{1,0:T(8,128)(2,1)S(1)}, u32[]{:S(2)}, u32[]{:S(2)}) collective-permute-start(bf16[128,128]{1,0:T(8,128)(2,1)S(1)} %get-tuple-element.45), channel_id=1, source_target_pairs={{0,18},{16,0},{2,16},{18,2},{1,19},{17,1},{3,17},{19,3},{4,22},{20... | collective-permute-start | bytes 98312 | tf_op jit(solution)/shard_map/ppermute | solution.py:378
